TPU v7x, 256 devices: a whole 4x4x8 slice. The times are simulated.
256 devices in a mesh: dp: 32 (over x, z), expert: 8 (over y, core).
Axes of the slice: x: 4, y: 4, z: 8, core: 2. Of those that a mesh axis runs over, the one named last changes fastest.
Arguments:
- tokens: bfloat16 [1024, 2048], P('expert'), may hold values from -6 to 6
- cotangent: bfloat16 [1024, 2048], P('expert'), may hold values from -0.75 to 0.75
- router_logits: float32 [1024, 2], P('expert'), may hold values from -6 to 6
- routes: int32 [1024, 2], P('expert'), may hold values from 0 to 7, all different within a row; in each aligned block of 128 rows (0 to 127, 128 to 255, ...) at most 48 rows name the same one
- gate_weight: bfloat16 [8, 7168, 2048], P('expert', 'dp'), may hold values from -0.125 to 0.125
- up_weight: bfloat16 [8, 7168, 2048], P('expert', 'dp'), may hold values from -0.125 to 0.125
- down_weight: bfloat16 [8, 7168, 2048], P('expert', 'dp'), may hold values from -0.0625 to 0.0625
- dir_gate: bfloat16 [8, 7168, 2048], P('expert', 'dp'), may hold values from -0.125 to 0.125
- dir_up: bfloat16 [8, 7168, 2048], P('expert', 'dp'), may hold values from -0.125 to 0.125
- dir_down: bfloat16 [8, 7168, 2048], P('expert', 'dp'), may hold values from -0.0625 to 0.0625
Outputs:
- mixed: bfloat16 [1024, 2048], P('expert')
- hvp_gate: float32 [8, 7168, 2048], P('expert', 'dp')
- hvp_up: float32 [8, 7168, 2048], P('expert', 'dp')
- hvp_down: float32 [8, 7168, 2048], P('expert', 'dp')
Inputs may be any that keep to these rules, and one draw needn't show every extreme that they name: `routes`: each row names 2 different experts; among the 128 rows of one index of the expert axis no expert is named more than 48 times, and in every draw some block names some expert exactly 48 times.
All inputs are finite; a program needn't handle non-finite values.
Results may differ from a plain program's by a relative error of at most 0.0074.
Values may be sent and summed in bfloat16 or wider, within the bound.
No kernel may reach another device: no remote copies, remote signals or barrier semaphores. Data moves between devices by JAX's collectives and lax.ppermute only.
A program may use at most 64 MiB of HBM per device.

v0:
```python
import jax
import jax.numpy as jnp
from jax import lax
from jax.sharding import PartitionSpec as P


def cut_along(value, dim, peers):
    before, after = (value.shape[:dim], value.shape[dim + 1 :])
    return jnp.moveaxis(value.reshape(*before, peers, -1, *after), dim, 0)


def summed_on_arrival(value, axis, dim):
    peers = lax.axis_size(axis)
    pieces = lax.all_to_all(cut_along(value, dim, peers), axis, 0, 0, tiled=True)
    return jnp.sum(pieces.astype(jnp.float32), axis=0)


def joined_along(pieces, dim):
    lengths = list(pieces.shape[1:])
    lengths[dim] *= pieces.shape[0]
    return jnp.moveaxis(pieces, 0, dim).reshape(lengths)


def sent_to_all(value, axis):
    copies = jnp.broadcast_to(value, (lax.axis_size(axis), *value.shape))
    return lax.all_to_all(copies, axis, split_axis=0, concat_axis=0, tiled=True)


def gathered_copies(value, axis, dim):
    return joined_along(sent_to_all(value, axis), dim)


def derivatives(preact):
    sigmoid_value = jax.nn.sigmoid(preact)
    slope_one = sigmoid_value * (1.0 + preact * (1.0 - sigmoid_value))
    slope_two = sigmoid_value * (1.0 - sigmoid_value) * (2.0 + preact * (1.0 - 2.0 * sigmoid_value))
    return (preact * sigmoid_value, slope_one, slope_two)


def project(left_rows, matrix):
    return jnp.einsum("rd,hd->rh", left_rows, matrix, preferred_element_type=jnp.float32)


def outer_sum(left_rows, right_rows):
    return jnp.einsum("rh,rd->hd", left_rows, right_rows, preferred_element_type=jnp.float32)


def block_terms(weights, token_rows, cot_rows):
    gate_mat, up_mat, down_mat, gate_dir, up_dir, down_dir = weights
    preact = project(token_rows, gate_mat)
    up_value = project(token_rows, up_mat)
    back_grad = project(cot_rows, down_mat)
    tang_gate = project(token_rows, gate_dir)
    tang_up = project(token_rows, up_dir)
    back_tang = project(cot_rows, down_dir)
    silu_value, slope_one, slope_two = derivatives(preact)
    hidden = (silu_value * up_value).astype(jnp.bfloat16)
    silu_tang = slope_one * tang_gate
    hidden_tang = (silu_tang * up_value + silu_value * tang_up).astype(jnp.bfloat16)
    resid_gate = (
        (back_tang * up_value + back_grad * tang_up) * slope_one
        + back_grad * up_value * slope_two * tang_gate
    ).astype(jnp.bfloat16)
    resid_up = (back_tang * silu_value + back_grad * silu_tang).astype(jnp.bfloat16)
    return (
        hidden,
        outer_sum(resid_gate, token_rows),
        outer_sum(resid_up, token_rows),
        outer_sum(hidden_tang, cot_rows),
    )


def shards(
    tokens,
    cotangent,
    router_logits,
    routes,
    gate_weight,
    up_weight,
    down_weight,
    dir_gate,
    dir_up,
    dir_down,
):
    tok_dev = tokens.shape[0]
    model_width = tokens.shape[1]
    top_count = routes.shape[1]
    experts = lax.axis_size("expert") * gate_weight.shape[0]
    capacity = top_count * tok_dev * 3 // (2 * experts)
    local_rows = experts * capacity
    weights = (gate_weight[0], up_weight[0], down_weight[0], dir_gate[0], dir_up[0], dir_down[0])
    gate_first = jax.nn.sigmoid(router_logits[:, 0] - router_logits[:, 1])
    gate_prob = jnp.stack([gate_first, 1.0 - gate_first], axis=1)
    flat_routes = routes.reshape(-1)
    onehot = (flat_routes[:, None] == jnp.arange(experts, dtype=jnp.int32)[None, :]).astype(
        jnp.int32
    )
    earlier = jnp.cumsum(onehot, axis=0) - onehot
    slot_pos = jnp.sum(earlier * onehot, axis=1)
    slot_index = flat_routes * capacity + slot_pos
    dispatch = (jnp.arange(local_rows, dtype=jnp.int32)[:, None] == slot_index[None, :]).astype(
        jnp.bfloat16
    )
    repeated = jnp.repeat(tokens, top_count, axis=0)
    scaled = (
        gate_prob.reshape(-1)[:, None]
        * jnp.repeat(cotangent, top_count, axis=0).astype(jnp.float32)
    ).astype(jnp.bfloat16)
    send_rows = (
        jnp.dot(dispatch, repeated, preferred_element_type=jnp.float32)
        .astype(jnp.bfloat16)
        .reshape(experts, capacity, model_width)
    )
    send_cot = (
        jnp.dot(dispatch, scaled, preferred_element_type=jnp.float32)
        .astype(jnp.bfloat16)
        .reshape(experts, capacity, model_width)
    )
    arrived_rows, arrived_cot = (
        lax.all_to_all(send_rows, "expert", split_axis=0, concat_axis=0, tiled=True),
        lax.all_to_all(send_cot, "expert", split_axis=0, concat_axis=0, tiled=True),
    )
    hidden, hvp_gate, hvp_up, hvp_down = block_terms(
        weights,
        arrived_rows.reshape(local_rows, model_width),
        arrived_cot.reshape(local_rows, model_width),
    )
    partial_out = jnp.dot(hidden, weights[2], preferred_element_type=jnp.float32)
    shares = summed_on_arrival(partial_out.astype(jnp.bfloat16), "dp", 1)
    share_width = shares.shape[1]
    expert_out = shares.astype(jnp.bfloat16).reshape(experts, capacity, share_width)
    returned = lax.all_to_all(expert_out, "expert", split_axis=0, concat_axis=0, tiled=True)
    picked = jnp.dot(
        dispatch.T, returned.reshape(local_rows, share_width), preferred_element_type=jnp.float32
    ).reshape(tok_dev, top_count, share_width)
    mixed_share = jnp.sum(gate_prob[:, :, None] * picked, axis=1).astype(jnp.bfloat16)
    mixed = gathered_copies(mixed_share, "dp", 1)
    return (mixed, hvp_gate[None], hvp_up[None], hvp_down[None])


def solution(mesh):
    in_specs = (
        P("expert", None),
        P("expert", None),
        P("expert", None),
        P("expert", None),
        P("expert", "dp", None),
        P("expert", "dp", None),
        P("expert", "dp", None),
        P("expert", "dp", None),
        P("expert", "dp", None),
        P("expert", "dp", None),
    )
    out_specs = (
        P("expert", None),
        P("expert", "dp", None),
        P("expert", "dp", None),
        P("expert", "dp", None),
    )
    return jax.shard_map(shards, mesh=mesh, in_specs=in_specs, out_specs=out_specs, check_vma=False)
```

profile of v0, /device:TPU:32, one launch (start us, length us, event | category | flops | bytes accessed | tf_op | source)
XLA Modules:
  0.0 152.5 jit_solution(13120432840209204215)
XLA Ops:
  0.6 0.0 copy-start
  0.6 0.9 copy.20
  1.5 0.1 reshape.93
  1.7 0.1 eq.55
  1.8 0.6 reduce-window.6
  2.4 0.2 slice_reduce_fusion
  2.6 0.1 fusion.32
  2.8 1.7 %broadcast_in_dim.22 = bf16[128,2,2048]{2,1,0:T(2,128)(2,1)S(1)} broadcast(bf16[128,2048]{1,0:T(8,128)(2,1)} %param.10), dimensions={0,2} | broadcast | bytes 1572864 | tf_op jit(solution)/shard_map/broadcast_in_dim | solution.py:104
  4.4 0.4 reshape.95
  4.9 0.6 convolution_convert_fusion.2
  5.5 0.0 copy-start.3
  5.5 26.0 %all_to_all.25 = bf16[8,48,2048]{2,1,0:T(8,128)(2,1)S(1)} all-to-all(bf16[8,48,2048]{2,1,0:T(8,128)(2,1)S(1)} %bitcast.68), channel_id=1, replica_groups=mesh['dp'=32,'expert'=8] {'expert'}, dimensions={0} | all-to-all | bytes 3145728 | tf_op jit(solution)/shard_map/all_to_all | solution.py:120
  31.5 0.0 copy-start.4
  31.5 0.0 copy-done.3
  31.5 0.7 fusion.13
  32.2 0.5 copy-done.4
  32.7 0.7 fusion.11
  33.4 0.0 copy-done
  33.4 1.8 %convolution_convert_fusion.1 = bf16[384,2048]{1,0:T(8,128)(2,1)} fusion(bf16[1,224,2048]{2,1,0:T(8,128)(2,1)S(1)} %copy-done, f32[384,224]{0,1:T(8,128)S(1)} %fusion.11, f32[384,224]{0,1:T(8,128)S(1)} %fusion.13), kind=kOutput, calls=%fused_computation.1 | convolution fusion | flops 353624064 | bytes 3178496 | tf_op jit(solution)/shard_map/dot_general | solution.py:128
  35.1 2.6 %copy.22 = bf16[384,2048]{0,1:T(8,128)(2,1)} copy(bf16[384,2048]{1,0:T(8,128)(2,1)} %convolution_convert_fusion.1) | data formatting | bytes 3145728 | tf_op jit(solution)/shard_map/convert_element_type | solution.py:129
  37.7 0.0 copy-start.7
  37.7 11.4 %all-to-all-start.1 = ((bf16[32,384,64]{1,2,0:T(8,128)(2,1)}), bf16[32,384,64]{1,2,0:T(8,128)(2,1)}, u32[]{:S(2)}, u32[]{:S(2)}) async-start(bf16[32,384,64]{1,2,0:T(8,128)(2,1)} %bitcast.67), calls=%async_computation.1 | async-start | bytes 3145728 | tf_op jit(solution)/shard_map/all_to_all | solution.py:14
  49.1 0.0 copy-done.7
  49.1 0.1 copy.26
  49.3 0.1 mul.95
  49.4 3.5 %broadcast_in_dim.24 = f32[128,2,2048]{2,1,0:T(2,128)} broadcast(bf16[128,2048]{1,0:T(8,128)(2,1)} %param.11), dimensions={0,2} | broadcast | bytes 2621440 | tf_op jit(solution)/shard_map/broadcast_in_dim | solution.py:107
  52.8 3.7 %convert_element_type.51 = f32[256,2048]{1,0:T(8,128)} reshape(f32[128,2,2048]{2,1,0:T(2,128)} %broadcast_in_dim.24) | data formatting | bytes 4194304 | tf_op jit(solution)/shard_map/convert_element_type | solution.py:107
  56.5 3.4 %convolution_convert_fusion = bf16[384,2048]{1,0:T(8,128)(2,1)} fusion(f32[256,2048]{1,0:T(8,128)} %convert_element_type.51, f32[256]{0:T(256)S(1)} %mul.95, s32[256]{0:T(256)S(1)} %multiply_add_fusion), kind=kOutput, calls=%fused_computation | convolution fusion | flops 404586496 | bytes 3672064 | tf_op jit(solution)/shard_map/dot_general | solution.py:115
  59.9 28.3 %all-to-all-done.1 = bf16[32,384,64]{1,2,0:T(8,128)(2,1)} async-done(((bf16[32,384,64]{1,2,0:T(8,128)(2,1)}), bf16[32,384,64]{1,2,0:T(8,128)(2,1)}, u32[]{:S(2)}, u32[]{:S(2)}) %all-to-all-start.1) | async-done | bytes 1572896 | tf_op jit(solution)/shard_map/all_to_all | solution.py:14
  88.2 4.3 %all-to-all-start.4 = ((bf16[8,48,2048]{2,1,0:T(8,128)(2,1)}), bf16[8,48,2048]{2,1,0:T(8,128)(2,1)}, u32[]{:S(2)}, u32[]{:S(2)}) async-start(bf16[8,48,2048]{2,1,0:T(8,128)(2,1)} %bitcast.66), calls=%async_computation.4 | async-start | bytes 3145728 | tf_op jit(solution)/shard_map/all_to_all | solution.py:121
  92.5 0.1 iota_compare_fusion.3
  92.7 0.8 eq.61
  93.4 0.0 copy-start.5
  93.5 2.0 %fusion.2 = f32[384,224]{0,1:T(8,128)S(1)} fusion(bf16[384,2048]{1,0:T(8,128)(2,1)S(1)} %bitcast.62, bf16[1,224,2048]{2,1,0:T(8,128)(2,1)} %param.17), kind=kOutput, calls=%fused_computation.10 | convolution fusion | flops 352321536 | bytes 2834432 | tf_op jit(solution)/shard_map/rd,hd->rh/dot_general | solution.py:41
  95.4 0.0 copy-done.5
  95.4 1.4 fusion.4
  96.9 2.3 %reduce_sum.31 = bf16[384,64]{0,1:T(8,128)(2,1)} reduce(bf16[32,384,64]{1,2,0:T(8,128)(2,1)} %all-to-all-done.1, bf16[]{:T(256)} %constant.14.clone.1), dimensions={0}, to_apply=%region_3.4 | reduce | flops 761856 | bytes 1622018 | tf_op jit(solution)/shard_map/reduce_sum | solution.py:15
  99.1 1.5 %copy.28 = bf16[384,64]{1,0:T(8,128)(2,1)} copy(bf16[384,64]{0,1:T(8,128)(2,1)} %reduce_sum.31) | data formatting | bytes 98304 | tf_op jit(solution)/shard_map/reshape | solution.py:131
  100.7 1.6 %reshape.106 = bf16[8,2,1536]{2,1,0:T(2,128)(2,1)} reshape(bf16[8,48,64]{2,1,0:T(8,128)(2,1)} %bitcast.69) | data formatting | bytes 98304
  102.3 11.8 %all-to-all-done.4 = bf16[8,48,2048]{2,1,0:T(8,128)(2,1)} async-done(((bf16[8,48,2048]{2,1,0:T(8,128)(2,1)}), bf16[8,48,2048]{2,1,0:T(8,128)(2,1)}, u32[]{:S(2)}, u32[]{:S(2)}) %all-to-all-start.4) | async-done | bytes 1572896 | tf_op jit(solution)/shard_map/all_to_all | solution.py:121
  114.1 4.0 %all-to-all-start.2 = ((bf16[8,2,1536]{2,1,0:T(2,128)(2,1)}), bf16[8,2,1536]{2,1,0:T(2,128)(2,1)}, u32[]{:S(2)}, u32[]{:S(2)}) async-start(bf16[8,2,1536]{2,1,0:T(2,128)(2,1)} %reshape.106), calls=%async_computation.2 | async-start | bytes 98304 | tf_op jit(solution)/shard_map/all_to_all | solution.py:132
  118.1 2.8 %fusion.8 = f32[384,224]{0,1:T(8,128)} fusion(bf16[384,2048]{1,0:T(8,128)(2,1)} %bitcast.15, bf16[1,224,2048]{2,1,0:T(8,128)(2,1)S(1)} %copy-done), kind=kOutput, calls=%fused_computation.16 | convolution fusion | flops 352321536 | bytes 2834432 | tf_op jit(solution)/shard_map/rd,hd->rh/dot_general | solution.py:41
  120.9 2.7 %all-to-all-done.2 = bf16[8,2,1536]{2,1,0:T(2,128)(2,1)} async-done(((bf16[8,2,1536]{2,1,0:T(2,128)(2,1)}), bf16[8,2,1536]{2,1,0:T(2,128)(2,1)}, u32[]{:S(2)}, u32[]{:S(2)}) %all-to-all-start.2) | async-done | bytes 49184 | tf_op jit(solution)/shard_map/all_to_all | solution.py:132
  123.6 1.6 %reshape.107 = bf16[8,48,64]{2,1,0:T(8,128)(2,1)} reshape(bf16[8,2,1536]{2,1,0:T(2,128)(2,1)} %all-to-all-done.2) | data formatting | bytes 98304
  125.2 1.2 fusion
  126.4 0.9 broadcast_in_dim.23
  127.3 5.6 %all-to-all-start.3 = ((bf16[32,128,64]{1,2,0:T(8,128)(2,1)}), bf16[32,128,64]{1,2,0:T(8,128)(2,1)}, u32[]{:S(2)}, u32[]{:S(2)}) async-start(bf16[32,128,64]{1,2,0:T(8,128)(2,1)} %broadcast_in_dim.23), calls=%async_computation.3 | async-start | bytes 1048576 | tf_op jit(solution)/shard_map/all_to_all | solution.py:26
  132.9 0.0 copy-start.6
  132.9 3.6 %convolution_bitcast_fusion = f32[1,224,2048]{2,1,0:T(8,128)} fusion(bf16[384,2048]{1,0:T(8,128)(2,1)} %bitcast.15, f32[384,224]{0,1:T(8,128)} %fusion.4, f32[384,224]{0,1:T(8,128)S(1)} %fusion.11, f32[384,224]{0,1:T(8,128)S(1)} %fusion.2, f32[384,224]{0,1:T(8,128)S(1)} %fusion.13), kind=kOutput, calls=%fused_computation.3 | convolution fusion | flops 353439744 | bytes 4784128 | tf_op jit(solution)/shard_map/rh,rd->hd/dot_general | solution.py:45
  136.4 0.0 copy-done.6
  136.4 0.0 copy-start.2
  136.4 2.2 %fusion.6 = f32[384,224]{0,1:T(8,128)S(1)} fusion(bf16[384,2048]{1,0:T(8,128)(2,1)} %bitcast.15, bf16[1,224,2048]{2,1,0:T(8,128)(2,1)S(1)} %copy-done.6), kind=kOutput, calls=%fused_computation.14 | convolution fusion | flops 352321536 | bytes 2834432 | tf_op jit(solution)/shard_map/rd,hd->rh/dot_general | solution.py:41
  138.6 0.0 copy-done.2
  138.6 0.0 copy-start.1
  138.6 1.9 %convolution_bitcast_fusion.1 = f32[1,224,2048]{2,1,0:T(8,128)} fusion(bf16[384,2048]{1,0:T(8,128)(2,1)S(1)} %bitcast.64, f32[384,224]{0,1:T(8,128)S(1)} %copy-done.2, f32[384,224]{0,1:T(8,128)S(1)} %fusion.6, f32[384,224]{0,1:T(8,128)S(1)} %fusion.2, f32[384,224]{0,1:T(8,128)S(1)} %fusion.13), kind=kOutput, calls=%fused_computation.4 | convolution fusion | flops 353439744 | bytes 4784128 | tf_op jit(solution)/shard_map/rh,rd->hd/dot_general | solution.py:45
  140.6 0.0 copy-done.1
  140.6 2.0 %convolution_bitcast_fusion.2 = f32[1,224,2048]{2,1,0:T(8,128)} fusion(bf16[384,2048]{1,0:T(8,128)(2,1)S(1)} %bitcast.65, f32[384,224]{0,1:T(8,128)S(1)} %fusion.2, f32[384,224]{0,1:T(8,128)S(1)} %fusion.13, f32[384,224]{0,1:T(8,128)S(1)} %copy-done.2, f32[384,224]{0,1:T(8,128)S(1)} %fusion.11, f32[384,224]{0,1:T(8,128)S(1)} %copy-done.1, ...), kind=kOutput, calls=%fused_computation.5 | convolution fusion | flops 354213888 | bytes 5472256 | tf_op jit(solution)/shard_map/rh,rd->hd/dot_general | solution.py:45
  142.6 7.9 %all-to-all-done.3 = bf16[32,128,64]{1,2,0:T(8,128)(2,1)} async-done(((bf16[32,128,64]{1,2,0:T(8,128)(2,1)}), bf16[32,128,64]{1,2,0:T(8,128)(2,1)}, u32[]{:S(2)}, u32[]{:S(2)}) %all-to-all-start.3) | async-done | bytes 524320 | tf_op jit(solution)/shard_map/all_to_all | solution.py:26
  150.4 2.0 %copy.27 = bf16[128,2048]{1,0:T(8,128)(2,1)} copy(bf16[128,2048]{0,1:T(8,128)(2,1)} %bitcast.13) | data formatting | bytes 1048576
  (6 shorter events, 0.1 us)
Async XLA Ops:
  0.6 32.7 %copy-start = (bf16[1,224,2048]{2,1,0:T(8,128)(2,1)S(1)}, bf16[1,224,2048]{2,1,0:T(8,128)(2,1)}, u32[]{:S(2)}) copy-start(bf16[1,224,2048]{2,1,0:T(8,128)(2,1)} %param.16) | copy-start | bytes 2752516
  5.5 26.0 %copy-start.3 = (bf16[1,224,2048]{2,1,0:T(8,128)(2,1)S(1)}, bf16[1,224,2048]{2,1,0:T(8,128)(2,1)}, u32[]{:S(2)}) copy-start(bf16[1,224,2048]{2,1,0:T(8,128)(2,1)} %param.14) | copy-start | bytes 2752516
  31.5 1.2 copy-start.4
  37.7 11.4 %copy-start.7 = (f32[128,2]{0,1:T(2,128)S(1)}, f32[128,2]{0,1:T(2,128)}, u32[]{:S(2)}) copy-start(f32[128,2]{0,1:T(2,128)} %param.12) | copy-start | bytes 3076
  37.7 50.5 %all-to-all-start.1 = ((bf16[32,384,64]{1,2,0:T(8,128)(2,1)}), bf16[32,384,64]{1,2,0:T(8,128)(2,1)}, u32[]{:S(2)}, u32[]{:S(2)}) async-start(bf16[32,384,64]{1,2,0:T(8,128)(2,1)} %bitcast.67), calls=%async_computation.1 | async-start | bytes 3145728 | tf_op jit(solution)/shard_map/all_to_all | solution.py:14
  88.2 25.9 %all-to-all-start.4 = ((bf16[8,48,2048]{2,1,0:T(8,128)(2,1)}), bf16[8,48,2048]{2,1,0:T(8,128)(2,1)}, u32[]{:S(2)}, u32[]{:S(2)}) async-start(bf16[8,48,2048]{2,1,0:T(8,128)(2,1)} %bitcast.66), calls=%async_computation.4 | async-start | bytes 3145728 | tf_op jit(solution)/shard_map/all_to_all | solution.py:121
  93.4 2.0 %copy-start.5 = (bf16[1,224,2048]{2,1,0:T(8,128)(2,1)S(1)}, bf16[1,224,2048]{2,1,0:T(8,128)(2,1)}, u32[]{:S(2)}) copy-start(bf16[1,224,2048]{2,1,0:T(8,128)(2,1)} %param.18) | copy-start | bytes 2752516
  114.1 9.5 %all-to-all-start.2 = ((bf16[8,2,1536]{2,1,0:T(2,128)(2,1)}), bf16[8,2,1536]{2,1,0:T(2,128)(2,1)}, u32[]{:S(2)}, u32[]{:S(2)}) async-start(bf16[8,2,1536]{2,1,0:T(2,128)(2,1)} %reshape.106), calls=%async_computation.2 | async-start | bytes 98304 | tf_op jit(solution)/shard_map/all_to_all | solution.py:132
  127.3 23.1 %all-to-all-start.3 = ((bf16[32,128,64]{1,2,0:T(8,128)(2,1)}), bf16[32,128,64]{1,2,0:T(8,128)(2,1)}, u32[]{:S(2)}, u32[]{:S(2)}) async-start(bf16[32,128,64]{1,2,0:T(8,128)(2,1)} %broadcast_in_dim.23), calls=%async_computation.3 | async-start | bytes 1048576 | tf_op jit(solution)/shard_map/all_to_all | solution.py:26
  132.9 3.6 %copy-start.6 = (bf16[1,224,2048]{2,1,0:T(8,128)(2,1)S(1)}, bf16[1,224,2048]{2,1,0:T(8,128)(2,1)}, u32[]{:S(2)}) copy-start(bf16[1,224,2048]{2,1,0:T(8,128)(2,1)} %param.19) | copy-start | bytes 2752516
  136.4 2.2 %copy-start.2 = (f32[384,224]{0,1:T(8,128)S(1)}, f32[384,224]{0,1:T(8,128)}, u32[]{:S(2)}) copy-start(f32[384,224]{0,1:T(8,128)} %fusion.8) | copy-start | bytes 1032196
  138.6 2.0 %copy-start.1 = (f32[384,224]{0,1:T(8,128)S(1)}, f32[384,224]{0,1:T(8,128)}, u32[]{:S(2)}) copy-start(f32[384,224]{0,1:T(8,128)} %fusion.4) | copy-start | bytes 1032196
where the time goes:
time: 154 us; the launch traced here: 152 us
  waiting for transfers between devices  50.7 us (33%)
  blocking collectives  26 us (17%)
  starting transfers between devices  25.2 us (16%)
  matrix products  24.2 us (16%)
  local copies, waits for them, and re-layouts  22.4 us (15%)
  other arithmetic  3.12 us (2%)
    all_to_all x1, waiting for transfers between devices, summed_on_arrival(): lax.all_to_all(cut_along(value, dim, peers), axis, 0, 0, tiled=True)  28.3 us
    all_to_all x1, blocking collectives, shards(): lax.all_to_all(send_rows, 'expert', split_axis=0, concat_axis=0, tiled=True)  26 us
    all_to_all x1, waiting for transfers between devices, shards(): lax.all_to_all(send_cot, 'expert', split_axis=0, concat_axis=0, tiled=True)  11.8 us
    all_to_all x1, starting transfers between devices, summed_on_arrival(): lax.all_to_all(cut_along(value, dim, peers), axis, 0, 0, tiled=True)  11.4 us
    dot_general x6, matrix products, project(): jnp.einsum('rd,hd->rh', left_rows, matrix, preferred_element_type=jnp.flo...  9.79 us
    all_to_all x1, waiting for transfers between devices, sent_to_all(): return lax.all_to_all(copies, axis, split_axis=0, concat_axis=0, tiled=True)  7.85 us
    dot_general x3, matrix products, outer_sum(): jnp.einsum('rh,rd->hd', left_rows, right_rows, preferred_element_type=jnp...  7.52 us
    unnamed x20, local copies, waits for them, and re-layouts  6.61 us
  transfers between devices with their start and end apart: 4, of which 4 were waited for; matrix products, arithmetic and copies ran while one was open for 22% of the time, Pallas kernels for 0%

commit v1 on v0

v1 whole, which is shorter than its diff:
```python
import jax
import jax.numpy as jnp
from jax import lax
from jax.experimental import pallas as pl
from jax.experimental.pallas import tpu as pltpu
from jax.sharding import Mesh, PartitionSpec as P

F32, BF16, I32 = jnp.float32, jnp.bfloat16, jnp.int32
CAP = 48
EXPERTS = 8
SPLIT = 8
FAR = 4
VMEM_LIMIT = 40 * 1024 * 1024

NEAR_AXES = ("x", "zl")
BACK_AXES = ("zh", "y", "c")
DP_AXES = ("x", "zh", "zl")
EXPERT_AXES = ("y", "c")


def call(body, outs, name):
    return pl.pallas_call(
        body,
        out_shape=outs,
        name=name,
        compiler_params=pltpu.CompilerParams(vmem_limit_bytes=VMEM_LIMIT),
    )


def iota(shape, dim):
    return lax.broadcasted_iota(I32, shape, dim)


def slots_of(routes):
    first, second = routes[0:1, :], routes[1:2, :]
    tok = routes.shape[1]
    experts = iota((EXPERTS, tok), 0)
    is_first, is_second = experts == first, experts == second
    member = jnp.where(is_first | is_second, 1.0, 0.0).astype(BF16)
    before = jnp.where(iota((tok, tok), 0) < iota((tok, tok), 1), 1.0, 0.0).astype(BF16)
    count = jnp.dot(member, before, preferred_element_type=F32)
    pos_first = jnp.sum(jnp.where(is_first, count, 0.0), axis=0, keepdims=True).astype(I32)
    pos_second = jnp.sum(jnp.where(is_second, count, 0.0), axis=0, keepdims=True).astype(I32)
    return first, second, pos_first, pos_second


def gate_probs(logits):
    first = jax.nn.sigmoid(logits[0:1, :] - logits[1:2, :])
    return first, 1.0 - first


def send_tokens_body(routes_ref, tok_ref, out_ref):
    first, second, pos_first, pos_second = slots_of(routes_ref[...])
    tok = tok_ref.shape[0]
    rows = iota((EXPERTS * CAP, tok), 0)
    hit = (rows == first * CAP + pos_first) | (rows == second * CAP + pos_second)
    dispatch = jnp.where(hit, 1.0, 0.0).astype(BF16)
    out = jnp.dot(dispatch, tok_ref[...], preferred_element_type=F32)
    out_ref[...] = out.astype(BF16).reshape(out_ref.shape)


def send_cot_body(me_ref, routes_ref, logits_ref, cot_ref, *out_refs):
    me = me_ref[0]
    first, second, pos_first, pos_second = slots_of(routes_ref[...])
    prob_first, prob_second = gate_probs(logits_ref[...])
    tok = cot_ref.shape[0]
    rows = iota((EXPERTS * CAP, tok), 0)
    hit_first = rows == (first ^ me) * CAP + pos_first
    hit_second = rows == (second ^ me) * CAP + pos_second
    dispatch = jnp.where(hit_first | hit_second, 1.0, 0.0).astype(BF16)
    weight = jnp.where(hit_first, prob_first, 0.0) + jnp.where(hit_second, prob_second, 0.0)
    weight = jnp.sum(weight, axis=1, keepdims=True)
    picked = jnp.dot(dispatch, cot_ref[...], preferred_element_type=F32)
    scaled = (picked * weight).astype(BF16)
    for i, out_ref in enumerate(out_refs):
        out_ref[...] = scaled[i * CAP : (i + 1) * CAP]


def place_body(me_ref, *refs):
    out_ref = refs[-1]
    me = me_ref[0]
    for i, ref in enumerate(refs[:-1]):
        out_ref[me ^ i] = ref[...]


def nt_dot(rows, matrix):
    return lax.dot_general(rows, matrix, (((1,), (1,)), ((), ())), preferred_element_type=F32)


def forward_body(x_ref, gate_ref, up_ref, down_ref, pre_ref, up_out_ref, part_ref):
    rows = x_ref[...]
    pre = nt_dot(rows, gate_ref[...])
    up_value = nt_dot(rows, up_ref[...])
    pre_ref[...] = pre
    up_out_ref[...] = up_value
    hidden = (pre * jax.nn.sigmoid(pre) * up_value).astype(BF16)
    width = part_ref.shape[2]
    for j in range(SPLIT):
        part = jnp.dot(
            hidden, down_ref[:, j * width : (j + 1) * width], preferred_element_type=F32
        )
        part_ref[j] = part.astype(BF16)


def near_sum_body(part_ref, out_ref):
    half = CAP // 2
    total = part_ref[0].astype(F32)
    for j in range(1, SPLIT):
        total = total + part_ref[j].astype(F32)
    left = iota((half, 128), 1) < 64
    for s in range(EXPERTS):
        for m in range(2):
            cols = slice(128 * m, 128 * m + 128)
            upper = total[s * CAP : s * CAP + half, cols]
            lower = total[s * CAP + half : (s + 1) * CAP, cols]
            even = jnp.where(left, upper, pltpu.roll(lower, 64, 1))
            odd = jnp.where(left, pltpu.roll(upper, 64, 1), lower)
            out_ref[2 * m * EXPERTS + s] = even.astype(BF16)
            out_ref[(2 * m + 1) * EXPERTS + s] = odd.astype(BF16)


def combine_body(routes_ref, logits_ref, back_ref, out_ref):
    half = CAP // 2
    first, second, pos_first, pos_second = slots_of(routes_ref[...])
    prob_first, prob_second = gate_probs(logits_ref[...])
    tok = routes_ref.shape[1]
    total = back_ref[0:EXPERTS].astype(F32)
    for z in range(1, FAR):
        total = total + back_ref[z * EXPERTS : (z + 1) * EXPERTS].astype(F32)
    held = total.astype(BF16).reshape(EXPERTS * half, 128)
    rows = iota((EXPERTS * half, tok), 0)

    def pick(expert, pos):
        base = expert * half + pos
        in_upper = jnp.where((rows == base) & (pos < half), 1.0, 0.0).astype(BF16)
        in_lower = jnp.where((rows == base - half) & (pos >= half), 1.0, 0.0).astype(BF16)
        dims = (((0,), (0,)), ((), ()))
        from_upper = lax.dot_general(held, in_upper, dims, preferred_element_type=F32)
        from_lower = lax.dot_general(held, in_lower, dims, preferred_element_type=F32)
        return from_upper[0:64] + from_lower[64:128]

    mixed = prob_first * pick(first, pos_first) + prob_second * pick(second, pos_second)
    mixed = mixed.astype(BF16)
    for j in range(out_ref.shape[0]):
        out_ref[j] = mixed


def turn_body(in_ref, out_ref):
    for m in range(out_ref.shape[1] // 128):
        block = in_ref[2 * m : 2 * m + 2].reshape(128, 128)
        out_ref[:, 128 * m : 128 * m + 128] = block.T


def derivatives(preact):
    sigmoid_value = jax.nn.sigmoid(preact)
    slope_one = sigmoid_value * (1.0 + preact * (1.0 - sigmoid_value))
    slope_two = sigmoid_value * (1.0 - sigmoid_value) * (2.0 + preact * (1.0 - 2.0 * sigmoid_value))
    return (preact * sigmoid_value, slope_one, slope_two)


def outer_sum(left_rows, right_rows):
    return jnp.einsum("rh,rd->hd", left_rows, right_rows, preferred_element_type=F32)


def shards(
    tokens,
    cotangent,
    router_logits,
    routes,
    gate_weight,
    up_weight,
    down_weight,
    dir_gate,
    dir_up,
    dir_down,
):
    tok, width = tokens.shape
    rows = EXPERTS * CAP
    units = gate_weight.shape[1]
    sds = jax.ShapeDtypeStruct
    routes_t = routes.T
    logits_t = router_logits.T
    me = (lax.axis_index("y") * 2 + lax.axis_index("c")).astype(I32).reshape(1)
    gate_mat, up_mat, down_mat = gate_weight[0], up_weight[0], down_weight[0]
    gate_dir, up_dir, down_dir = dir_gate[0], dir_up[0], dir_down[0]

    send_x = call(send_tokens_body, sds((EXPERTS, CAP, width), BF16), "send_tokens")(
        routes_t, tokens
    )
    slot_x = lax.all_to_all(send_x, EXPERT_AXES, 0, 0, tiled=True).reshape(rows, width)

    smem = pl.BlockSpec(memory_space=pltpu.SMEM)
    vmem = pl.BlockSpec(memory_space=pltpu.VMEM)
    params = pltpu.CompilerParams(vmem_limit_bytes=VMEM_LIMIT)
    send_c = pl.pallas_call(
        send_cot_body,
        out_shape=[sds((CAP, width), BF16)] * EXPERTS,
        in_specs=[smem, vmem, vmem, vmem],
        compiler_params=params,
        name="send_cot",
    )(me, routes_t, logits_t, cotangent)

    preact, up_value, partial_out = call(
        forward_body,
        [
            sds((rows, units), F32),
            sds((rows, units), F32),
            sds((SPLIT, rows, width // SPLIT), BF16),
        ],
        "forward",
    )(slot_x, gate_mat, up_mat, down_mat)

    near = lax.all_to_all(partial_out, NEAR_AXES, 0, 0, tiled=True)

    send_c, _ = lax.optimization_barrier((send_c, partial_out))
    pieces = [send_c[0]]
    for i in range(1, EXPERTS):
        pairs = [(d, d ^ i) for d in range(EXPERTS)]
        pieces.append(lax.ppermute(send_c[i], EXPERT_AXES, pairs))

    tang_gate = jnp.einsum("rd,hd->rh", slot_x, gate_dir, preferred_element_type=F32)
    tang_up = jnp.einsum("rd,hd->rh", slot_x, up_dir, preferred_element_type=F32)

    near_total = call(near_sum_body, sds((FAR * EXPERTS, CAP // 2, 128), BF16), "near_sum")(near)
    back = lax.all_to_all(near_total, BACK_AXES, 0, 0, tiled=True)

    slot_c = pl.pallas_call(
        place_body,
        out_shape=sds((EXPERTS, CAP, width), BF16),
        in_specs=[smem] + [vmem] * EXPERTS,
        compiler_params=params,
        name="place",
    )(me, *pieces).reshape(rows, width)

    back_grad = jnp.einsum("rd,hd->rh", slot_c, down_mat, preferred_element_type=F32)
    back_tang = jnp.einsum("rd,hd->rh", slot_c, down_dir, preferred_element_type=F32)
    silu_value, slope_one, slope_two = derivatives(preact)
    silu_tang = slope_one * tang_gate
    hidden_tang = (silu_tang * up_value + silu_value * tang_up).astype(BF16)
    resid_gate = (
        (back_tang * up_value + back_grad * tang_up) * slope_one
        + back_grad * up_value * slope_two * tang_gate
    ).astype(BF16)
    resid_up = (back_tang * silu_value + back_grad * silu_tang).astype(BF16)
    hvp_gate = outer_sum(resid_gate, slot_x)
    hvp_up = outer_sum(resid_up, slot_x)
    hvp_down = outer_sum(hidden_tang, slot_c)

    share = call(combine_body, sds((32, 64, tok), BF16), "combine")(routes_t, logits_t, back)
    full = lax.all_to_all(share, ("x", "zl", "zh"), 0, 0, tiled=True)
    mixed = call(turn_body, sds((tok, width), BF16), "turn")(full)
    return (mixed, hvp_gate[None], hvp_up[None], hvp_down[None])


def solution(mesh):
    grid = Mesh(mesh.devices.reshape(4, 4, 2, 4, 2), ("x", "zh", "zl", "y", "c"))
    by_expert = P(EXPERT_AXES, None)
    by_both = P(EXPERT_AXES, DP_AXES, None)
    return jax.shard_map(
        shards,
        mesh=grid,
        in_specs=(by_expert,) * 4 + (by_both,) * 6,
        out_specs=(by_expert,) + (by_both,) * 3,
        check_vma=False,
    )
```

time: 154 us -> 117 us (0.76)
  waiting for transfers between devices: 50.7 us -> 26.2 us
  local copies, waits for them, and re-layouts: 22.4 us -> 7.67 us
  matrix products: 24.2 us -> 13.8 us
  Pallas kernels: 0 us -> 8.83 us
  starting transfers between devices: 25.2 us -> 31.7 us
  other arithmetic: 3.12 us -> 0 us
    all_to_all x4 -> x3, waiting for transfers between devices: 50.7 us -> 17.4 us  [the longest x1 9.91 us: shards(): near = lax.all_to_all(partial_out, NEAR_AXES, 0, 0, tiled=True)]
    dot_general x13 -> x7, matrix products: 24.2 us -> 13.8 us  [the longest x3 6.2 us: outer_sum(): jnp.einsum('rh,rd->hd', left_rows, right_rows, preferred_element_type=F32)]
    pallas_call x0 -> x7, Pallas kernels: none -> 8.83 us  [the longest x1 2.36 us: shards(): call(near_sum_body, sds((FAR * EXPERTS, CAP // 2, 128), BF16), 'near_sum')]
    ppermute x0 -> x7, waiting for transfers between devices: none -> 8.8 us  [shards(): pieces.append(lax.ppermute(send_c[i], EXPERT_AXES, pairs))]
    ppermute x0 -> x7, starting transfers between devices: none -> 8.09 us  [shards(): pieces.append(lax.ppermute(send_c[i], EXPERT_AXES, pairs))]
    convert_element_type x2 -> x0, local copies, waits for them, and re-layouts: 6.23 us -> none  [the longest x1 3.66 us: shards(): jnp.repeat(cotangent, top_count, axis=0).astype(jnp.float32)]
    broadcast_in_dim x3 -> x0, local copies, waits for them, and re-layouts: 6.04 us -> none  [the longest x1 3.45 us: shards(): jnp.repeat(cotangent, top_count, axis=0).astype(jnp.float32)]
    reduce_sum x2 -> x0, other arithmetic: 2.35 us -> none  [the longest x1 2.26 us: summed_on_arrival(): return jnp.sum(pieces.astype(jnp.float32), axis=0)]
  transfers between devices with their start and end apart: 4 -> 10, of which waited for: 4 -> 4; matrix products, arithmetic and copies ran while one was open for 22% -> 12% of each run, Pallas kernels for 0% -> 5%
where the time goes in v1:
time: 117 us; the launch traced here: 115 us
  starting transfers between devices  31.7 us (27%)
  waiting for transfers between devices  26.2 us (22%)
  blocking collectives  26.1 us (22%)
  matrix products  13.8 us (12%)
  Pallas kernels  8.83 us (8%)
  local copies, waits for them, and re-layouts  7.67 us (7%)
    all_to_all x1, blocking collectives, shards(): lax.all_to_all(send_x, EXPERT_AXES, 0, 0, tiled=True).reshape(rows, width)  26.1 us
    all_to_all x1, waiting for transfers between devices, shards(): near = lax.all_to_all(partial_out, NEAR_AXES, 0, 0, tiled=True)  9.91 us
    all_to_all x1, starting transfers between devices, shards(): full = lax.all_to_all(share, ('x', 'zl', 'zh'), 0, 0, tiled=True)  9.03 us
    ppermute x7, waiting for transfers between devices, shards(): pieces.append(lax.ppermute(send_c[i], EXPERT_AXES, pairs))  8.8 us
    all_to_all x1, starting transfers between devices, shards(): back = lax.all_to_all(near_total, BACK_AXES, 0, 0, tiled=True)  8.69 us
    ppermute x7, starting transfers between devices, shards(): pieces.append(lax.ppermute(send_c[i], EXPERT_AXES, pairs))  8.09 us
    unnamed x46, local copies, waits for them, and re-layouts  7.67 us
    all_to_all x1, waiting for transfers between devices, shards(): full = lax.all_to_all(share, ('x', 'zl', 'zh'), 0, 0, tiled=True)  7.5 us
  transfers between devices with their start and end apart: 10, of which 4 were waited for; matrix products, arithmetic and copies ran while one was open for 12% of the time, Pallas kernels for 5%

profile of v1, /device:TPU:32, one launch (start us, length us, event | category | flops | bytes accessed | tf_op | source)
XLA Modules:
  0.0 115.2 jit_solution(5471491272474079111)
XLA Ops:
  0.6 0.0 copy-start
  0.6 0.0 copy-start.12
  0.7 1.1 copy-done.12
  1.8 0.7 copy-done.15
  2.4 0.7 send_tokens.1
  3.1 0.0 copy-start.7
  3.2 0.0 copy-start.8
  3.2 0.0 copy-start.9
  3.2 26.1 %all_to_all.20 = bf16[8,48,2048]{2,1,0:T(8,128)(2,1)S(1)} all-to-all(bf16[8,48,2048]{2,1,0:T(8,128)(2,1)S(1)} %send_tokens.1), channel_id=1, replica_groups=mesh['x'=4,'zh'=4,'zl'=2,'y'=4,'c'=2] {'y','c'}, dimensions={0} | all-to-all | bytes 3145728 | tf_op jit(solution)/shard_map/all_to_all | solution.py:190
  29.3 0.0 copy-done.7
  29.3 0.0 copy-done.8
  29.3 0.0 copy-done.9
  29.3 1.5 %forward.1 = (f32[384,224]{1,0:T(8,128)S(1)}, f32[384,224]{1,0:T(8,128)S(1)}, bf16[8,384,256]{2,1,0:T(8,128)(2,1)S(1)}) custom-call(bf16[384,2048]{1,0:T(8,128)(2,1)S(1)} %bitcast.32, bf16[224,2048]{1,0:T(8,128)(2,1)S(1)} %bitcast.40, bf16[224,2048]{1,0:T(8,128)(2,1)S(1)} %bitcast.41, bf16[224,2048]{1,0:T(8,128)(2,1)S(1)} %bitcast.42), custom_call_target="tpu_custom_call" | custom-call | tf_op jit(solution)/shard_map/forward/pallas_call | solution.py:203
  30.8 0.0 copy-start.4
  30.8 0.7 copy-done.4
  31.5 1.1 copy-done.6
  32.7 5.9 %all-to-all-start.1 = ((bf16[8,384,256]{2,1,0:T(8,128)(2,1)}), bf16[8,384,256]{2,1,0:T(8,128)(2,1)}, u32[]{:S(2)}, u32[]{:S(2)}) async-start(bf16[8,384,256]{2,1,0:T(8,128)(2,1)} %copy-done.6), calls=%async_computation.1 | async-start | bytes 3145728 | tf_op jit(solution)/shard_map/all_to_all | solution.py:213
  38.6 0.0 copy-done.11
  38.6 0.0 copy-done.16
  38.6 0.0 copy-done.17
  38.6 1.6 %send_cot.1 = (bf16[48,2048]{1,0:T(8,128)(2,1)S(1)}, bf16[48,2048]{1,0:T(8,128)(2,1)}, bf16[48,2048]{1,0:T(8,128)(2,1)}, bf16[48,2048]{1,0:T(8,128)(2,1)}, bf16[...) custom-call(s32[1]{0:T(128)} %bitcast.6.me_ref, ...), custom_call_target="tpu_custom_call" | custom-call | tf_op jit(solution)/shard_map/send_cot/pallas_call | solution.py:195
  40.2 0.7 copy-done.13
  40.9 0.7 copy-done.18
  41.5 0.7 copy-done.19
  42.2 0.0 collective-permute-start
  42.2 0.7 collective-permute-start.1
  42.9 1.1 collective-permute-start.2
  44.1 0.9 collective-permute-start.3
  44.9 2.3 %collective-permute-start.4 = (bf16[48,2048]{1,0:T(8,128)(2,1)}, bf16[48,2048]{1,0:T(8,128)(2,1)}, u32[]{:S(2)}, u32[]{:S(2)}) collective-permute-start(bf16[48,2048]{1,0:T(8,128)(2,1)} %get-tuple-element.37), channel_id=1, source_target_pairs={{0,5},{1,4},{2,7},{3,6},{4,1},{5,0},{6,3},{7,2},{8,13},{9,12},{10,... | collective-permute-start | bytes 589832 | tf_op jit(solution)/shard_map/ppermute | solution.py:219
  47.2 0.0 copy-done
  47.2 1.3 %fusion = f32[384,224]{1,0:T(8,128)} fusion(bf16[384,2048]{1,0:T(8,128)(2,1)S(1)} %bitcast.33, bf16[1,224,2048]{2,1,0:T(8,128)(2,1)S(1)} %copy-done), kind=kOutput, calls=%fused_computation.3 | convolution fusion | flops 352321536 | bytes 2834432 | tf_op jit(solution)/shard_map/rd,hd->rh/dot_general | solution.py:221
  48.6 9.9 %all-to-all-done.1.part_ref = bf16[8,384,256]{2,1,0:T(8,128)(2,1)} async-done(((bf16[8,384,256]{2,1,0:T(8,128)(2,1)}), bf16[8,384,256]{2,1,0:T(8,128)(2,1)}, u32[]{:S(2)}, u32[]{:S(2)}) %all-to-all-start.1) | async-done | bytes 1572896 | tf_op jit(solution)/shard_map/all_to_all | solution.py:213
  58.5 2.4 %near_sum.1 = bf16[32,24,128]{2,1,0:T(8,128)(2,1)} custom-call(bf16[8,384,256]{2,1,0:T(8,128)(2,1)} %all-to-all-done.1.part_ref), custom_call_target="tpu_custom_call" | custom-call | tf_op jit(solution)/shard_map/near_sum/pallas_call | solution.py:224
  60.8 8.7 %all-to-all-start.2 = ((bf16[32,24,128]{2,1,0:T(8,128)(2,1)}), bf16[32,24,128]{2,1,0:T(8,128)(2,1)S(1)}, u32[]{:S(2)}, u32[]{:S(2)}) async-start(bf16[32,24,128]{2,1,0:T(8,128)(2,1)} %near_sum.1), calls=%async_computation.2 | async-start | bytes 393216 | tf_op jit(solution)/shard_map/all_to_all | solution.py:225
  69.5 0.0 collective-permute-done.refs_1_
  69.5 3.1 %collective-permute-start.5 = (bf16[48,2048]{1,0:T(8,128)(2,1)}, bf16[48,2048]{1,0:T(8,128)(2,1)S(1)}, u32[]{:S(2)}, u32[]{:S(2)}) collective-permute-start(bf16[48,2048]{1,0:T(8,128)(2,1)} %copy-done.19), channel_id=1, source_target_pairs={{0,6},{1,7},{2,4},{3,5},{4,2},{5,3},{6,0},{7,1},{8,14},{9,15},{10,... | collective-permute-start | bytes 589832 | tf_op jit(solution)/shard_map/ppermute | solution.py:219
  72.6 0.0 collective-permute-done.1.refs_2_
  72.6 0.0 collective-permute-start.6
  72.6 2.5 %fusion.2 = f32[384,224]{1,0:T(8,128)} fusion(bf16[384,2048]{1,0:T(8,128)(2,1)S(1)} %bitcast.34, bf16[1,224,2048]{2,1,0:T(8,128)(2,1)} %param.18), kind=kOutput, calls=%fused_computation.5 | convolution fusion | flops 352321536 | bytes 2834432 | tf_op jit(solution)/shard_map/rd,hd->rh/dot_general | solution.py:222
  75.2 0.0 collective-permute-done.2.refs_3_
  75.2 0.0 collective-permute-done.3.refs_4_
  75.2 0.0 collective-permute-done.4.refs_5_
  75.2 5.1 %collective-permute-done.5.refs_6_ = bf16[48,2048]{1,0:T(8,128)(2,1)S(1)} collective-permute-done((bf16[48,2048]{1,0:T(8,128)(2,1)}, bf16[48,2048]{1,0:T(8,128)(2,1)S(1)}, u32[]{:S(2)}, u32[]{:S(2)}) %collective-permute-start.5) | collective-permute-done | bytes 196640 | tf_op jit(solution)/shard_map/ppermute | solution.py:219
  80.2 3.7 %collective-permute-done.6.refs_7_ = bf16[48,2048]{1,0:T(8,128)(2,1)S(1)} collective-permute-done((bf16[48,2048]{1,0:T(8,128)(2,1)}, bf16[48,2048]{1,0:T(8,128)(2,1)S(1)}, u32[]{:S(2)}, u32[]{:S(2)}) %collective-permute-start.6) | collective-permute-done | bytes 196640 | tf_op jit(solution)/shard_map/ppermute | solution.py:219
  84.0 0.0 copy-done.14
  84.0 1.3 %place.1 = bf16[8,48,2048]{2,1,0:T(8,128)(2,1)S(1)} custom-call(s32[1]{0:T(128)} %bitcast.6.me_ref, bf16[48,2048]{1,0:T(8,128)(2,1)S(1)} %copy-done.14, bf16[48,2048]{1,0:T(8,128)(2,1)S(1)} %collective-permute-done.refs_1_, bf16[48,2048]{1,0:T(8,128)(2,1)} %collective-permute-done.1.refs_2_, bf16[48,2048]{1,0:T(8,128)(2,1)} %collective-permute-done.2.refs_3_, ...), custom_call_target="tpu_custom_call" | custom-call | tf_op jit(solution)/shard_map/place/pallas_call | solution.py:227
  85.3 0.0 copy-start.1
  85.3 1.1 copy-done.1
  86.4 0.0 copy-done.10
  86.4 1.3 %fusion.21 = f32[384,224]{1,0:T(8,128)} fusion(bf16[384,2048]{1,0:T(8,128)(2,1)S(1)} %bitcast.37, bf16[1,224,2048]{2,1,0:T(8,128)(2,1)S(1)} %copy-done.10), kind=kOutput, calls=%fused_computation.25 | convolution fusion | flops 352321536 | bytes 2834432 | tf_op jit(solution)/shard_map/rd,hd->rh/dot_general | solution.py:235
  87.8 0.0 all-to-all-done.2.back_ref
  87.8 0.4 combine.1
  88.2 0.0 copy-start.3
  88.2 0.8 copy-done.3
  89.0 9.0 %all-to-all-start.3 = ((bf16[32,64,128]{2,1,0:T(8,128)(2,1)}), bf16[32,64,128]{2,1,0:T(8,128)(2,1)S(1)}, u32[]{:S(2)}, u32[]{:S(2)}) async-start(bf16[32,64,128]{2,1,0:T(8,128)(2,1)} %copy-done.3), calls=%async_computation.3 | async-start | bytes 1048576 | tf_op jit(solution)/shard_map/all_to_all | solution.py:250
  98.0 0.0 copy-start.2
  98.1 0.0 copy-start.20
  98.1 2.4 %fusion.4 = f32[384,224]{1,0:T(8,128)S(1)} fusion(bf16[384,2048]{1,0:T(8,128)(2,1)} %bitcast.38, bf16[1,224,2048]{2,1,0:T(8,128)(2,1)} %param.19), kind=kOutput, calls=%fused_computation.7 | convolution fusion | flops 352321536 | bytes 2834432 | tf_op jit(solution)/shard_map/rd,hd->rh/dot_general | solution.py:236
  100.5 0.0 copy-start.22
  100.5 2.0 %convolution_bitcast_fusion = f32[1,224,2048]{2,1,0:T(8,128)} fusion(bf16[384,2048]{1,0:T(8,128)(2,1)S(1)} %bitcast.39, f32[384,224]{1,0:T(8,128)S(1)} %copy-done.21, f32[384,224]{1,0:T(8,128)S(1)} %copy-done.5, f32[384,224]{1,0:T(8,128)S(1)} %get-tuple-element.41, f32[384,224]{1,0:T(8,128)S(1)} %copy-done.20), kind=kOutput, calls=%fused_computation | convolution fusion | flops 353439744 | bytes 4784128 | tf_op jit(solution)/shard_map/rh,rd->hd/dot_general | solution.py:162
  102.6 2.0 %convolution_bitcast_fusion.1 = f32[1,224,2048]{2,1,0:T(8,128)} fusion(bf16[384,2048]{1,0:T(8,128)(2,1)S(1)} %bitcast.35, f32[384,224]{1,0:T(8,128)S(1)} %copy-done.22, f32[384,224]{1,0:T(8,128)S(1)} %fusion.4, f32[384,224]{1,0:T(8,128)S(1)} %get-tuple-element.41, f32[384,224]{1,0:T(8,128)S(1)} %copy-done.20), kind=kOutput, calls=%fused_computation.1 | convolution fusion | flops 353439744 | bytes 4784128 | tf_op jit(solution)/shard_map/rh,rd->hd/dot_general | solution.py:162
  104.6 2.1 %convolution_bitcast_fusion.2 = f32[1,224,2048]{2,1,0:T(8,128)} fusion(bf16[384,2048]{1,0:T(8,128)(2,1)S(1)} %bitcast.36, f32[384,224]{1,0:T(8,128)S(1)} %copy-done.20, f32[384,224]{1,0:T(8,128)S(1)} %get-tuple-element.41, f32[384,224]{1,0:T(8,128)S(1)} %copy-done.22, f32[384,224]{1,0:T(8,128)S(1)} %copy-done.5, f32[384,224]{1,0:T(8,128)S(1)} %copy-done.21, ...), kind=kOutput, calls=%fused_computation.2 | convolution fusion | flops 354213888 | bytes 5472256 | tf_op jit(solution)/shard_map/rh,rd->hd/dot_general | solution.py:162
  106.7 7.5 %all-to-all-done.3.in_ref = bf16[32,64,128]{2,1,0:T(8,128)(2,1)S(1)} async-done(((bf16[32,64,128]{2,1,0:T(8,128)(2,1)}), bf16[32,64,128]{2,1,0:T(8,128)(2,1)S(1)}, u32[]{:S(2)}, u32[]{:S(2)}) %all-to-all-start.3) | async-done | bytes 524320 | tf_op jit(solution)/shard_map/all_to_all | solution.py:250
  114.2 1.0 turn.1
  (17 shorter events, 0.0 us)
Async XLA Ops:
  0.6 46.6 %copy-start = (bf16[1,224,2048]{2,1,0:T(8,128)(2,1)S(1)}, bf16[1,224,2048]{2,1,0:T(8,128)(2,1)}, u32[]{:S(2)}) copy-start(bf16[1,224,2048]{2,1,0:T(8,128)(2,1)} %param.17) | copy-start | bytes 2752516
  0.6 1.1 copy-start.12
  1.8 0.7 copy-start.15
  3.1 26.2 %copy-start.7 = (bf16[1,224,2048]{2,1,0:T(8,128)(2,1)S(1)}, bf16[1,224,2048]{2,1,0:T(8,128)(2,1)}, u32[]{:S(2)}) copy-start(bf16[1,224,2048]{2,1,0:T(8,128)(2,1)} %param.14) | copy-start | bytes 2752516
  3.2 26.2 %copy-start.8 = (bf16[1,224,2048]{2,1,0:T(8,128)(2,1)S(1)}, bf16[1,224,2048]{2,1,0:T(8,128)(2,1)}, u32[]{:S(2)}) copy-start(bf16[1,224,2048]{2,1,0:T(8,128)(2,1)} %param.15) | copy-start | bytes 2752516
  3.2 26.1 %copy-start.9 = (bf16[1,224,2048]{2,1,0:T(8,128)(2,1)S(1)}, bf16[1,224,2048]{2,1,0:T(8,128)(2,1)}, u32[]{:S(2)}) copy-start(bf16[1,224,2048]{2,1,0:T(8,128)(2,1)} %param.16) | copy-start | bytes 2752516
  30.8 0.7 copy-start.4
  31.5 1.1 copy-start.6
  32.7 5.9 %copy-start.11 = (bf16[128,2048]{1,0:T(8,128)(2,1)S(1)}, bf16[128,2048]{1,0:T(8,128)(2,1)}, u32[]{:S(2)}) copy-start(bf16[128,2048]{1,0:T(8,128)(2,1)} %cot_ref.1) | copy-start | bytes 1572868
  32.7 5.9 %copy-start.16 = (s32[128,2]{0,1:T(2,128)S(1)}, s32[128,2]{0,1:T(2,128)}, u32[]{:S(2)}) copy-start(s32[128,2]{0,1:T(2,128)} %param.13) | copy-start | bytes 3076
  32.7 5.9 %copy-start.17 = (f32[128,2]{0,1:T(2,128)S(1)}, f32[128,2]{0,1:T(2,128)}, u32[]{:S(2)}) copy-start(f32[128,2]{0,1:T(2,128)} %param.12) | copy-start | bytes 3076
  32.7 25.8 %all-to-all-start.1 = ((bf16[8,384,256]{2,1,0:T(8,128)(2,1)}), bf16[8,384,256]{2,1,0:T(8,128)(2,1)}, u32[]{:S(2)}, u32[]{:S(2)}) async-start(bf16[8,384,256]{2,1,0:T(8,128)(2,1)} %copy-done.6), calls=%async_computation.1 | async-start | bytes 3145728 | tf_op jit(solution)/shard_map/all_to_all | solution.py:213
  40.2 0.7 copy-start.13
  40.9 0.7 copy-start.18
  41.5 0.7 copy-start.19
  42.2 27.3 %collective-permute-start = (bf16[48,2048]{1,0:T(8,128)(2,1)}, bf16[48,2048]{1,0:T(8,128)(2,1)S(1)}, u32[]{:S(2)}, u32[]{:S(2)}) collective-permute-start(bf16[48,2048]{1,0:T(8,128)(2,1)} %get-tuple-element.33), channel_id=1, source_target_pairs={{0,1},{1,0},{2,3},{3,2},{4,5},{5,4},{6,7},{7,6},{8,9},{9,8},{10,11... | collective-permute-start | bytes 589832 | tf_op jit(solution)/shard_map/ppermute | solution.py:219
  42.2 30.4 %collective-permute-start.1 = (bf16[48,2048]{1,0:T(8,128)(2,1)}, bf16[48,2048]{1,0:T(8,128)(2,1)}, u32[]{:S(2)}, u32[]{:S(2)}) collective-permute-start(bf16[48,2048]{1,0:T(8,128)(2,1)} %get-tuple-element.34), channel_id=1, source_target_pairs={{0,2},{1,3},{2,0},{3,1},{4,6},{5,7},{6,4},{7,5},{8,10},{9,11},{10,... | collective-permute-start | bytes 589832 | tf_op jit(solution)/shard_map/ppermute | solution.py:219
  42.9 32.2 %collective-permute-start.2 = (bf16[48,2048]{1,0:T(8,128)(2,1)}, bf16[48,2048]{1,0:T(8,128)(2,1)}, u32[]{:S(2)}, u32[]{:S(2)}) collective-permute-start(bf16[48,2048]{1,0:T(8,128)(2,1)} %get-tuple-element.35), channel_id=1, source_target_pairs={{0,3},{1,2},{2,1},{3,0},{4,7},{5,6},{6,5},{7,4},{8,11},{9,10},{10,... | collective-permute-start | bytes 589832 | tf_op jit(solution)/shard_map/ppermute | solution.py:219
  44.1 31.1 %collective-permute-start.3 = (bf16[48,2048]{1,0:T(8,128)(2,1)}, bf16[48,2048]{1,0:T(8,128)(2,1)}, u32[]{:S(2)}, u32[]{:S(2)}) collective-permute-start(bf16[48,2048]{1,0:T(8,128)(2,1)} %get-tuple-element.36), channel_id=1, source_target_pairs={{0,4},{1,5},{2,6},{3,7},{4,0},{5,1},{6,2},{7,3},{8,12},{9,13},{10,... | collective-permute-start | bytes 589832 | tf_op jit(solution)/shard_map/ppermute | solution.py:219
  44.9 30.2 %collective-permute-start.4 = (bf16[48,2048]{1,0:T(8,128)(2,1)}, bf16[48,2048]{1,0:T(8,128)(2,1)}, u32[]{:S(2)}, u32[]{:S(2)}) collective-permute-start(bf16[48,2048]{1,0:T(8,128)(2,1)} %get-tuple-element.37), channel_id=1, source_target_pairs={{0,5},{1,4},{2,7},{3,6},{4,1},{5,0},{6,3},{7,2},{8,13},{9,12},{10,... | collective-permute-start | bytes 589832 | tf_op jit(solution)/shard_map/ppermute | solution.py:219
  60.8 23.1 %copy-start.14 = (bf16[48,2048]{1,0:T(8,128)(2,1)S(1)}, bf16[48,2048]{1,0:T(8,128)(2,1)}, u32[]{:S(2)}) copy-start(bf16[48,2048]{1,0:T(8,128)(2,1)} %copy-done.13) | copy-start | bytes 589828
  60.8 27.0 %all-to-all-start.2 = ((bf16[32,24,128]{2,1,0:T(8,128)(2,1)}), bf16[32,24,128]{2,1,0:T(8,128)(2,1)S(1)}, u32[]{:S(2)}, u32[]{:S(2)}) async-start(bf16[32,24,128]{2,1,0:T(8,128)(2,1)} %near_sum.1), calls=%async_computation.2 | async-start | bytes 393216 | tf_op jit(solution)/shard_map/all_to_all | solution.py:225
  69.5 10.7 %collective-permute-start.5 = (bf16[48,2048]{1,0:T(8,128)(2,1)}, bf16[48,2048]{1,0:T(8,128)(2,1)S(1)}, u32[]{:S(2)}, u32[]{:S(2)}) collective-permute-start(bf16[48,2048]{1,0:T(8,128)(2,1)} %copy-done.19), channel_id=1, source_target_pairs={{0,6},{1,7},{2,4},{3,5},{4,2},{5,3},{6,0},{7,1},{8,14},{9,15},{10,... | collective-permute-start | bytes 589832 | tf_op jit(solution)/shard_map/ppermute | solution.py:219
  72.6 11.3 %collective-permute-start.6 = (bf16[48,2048]{1,0:T(8,128)(2,1)}, bf16[48,2048]{1,0:T(8,128)(2,1)S(1)}, u32[]{:S(2)}, u32[]{:S(2)}) collective-permute-start(bf16[48,2048]{1,0:T(8,128)(2,1)} %copy-done.18), channel_id=1, source_target_pairs={{0,7},{1,6},{2,5},{3,4},{4,3},{5,2},{6,1},{7,0},{8,15},{9,14},{10,... | collective-permute-start | bytes 589832 | tf_op jit(solution)/shard_map/ppermute | solution.py:219
  75.2 11.3 %copy-start.10 = (bf16[1,224,2048]{2,1,0:T(8,128)(2,1)S(1)}, bf16[1,224,2048]{2,1,0:T(8,128)(2,1)}, u32[]{:S(2)}) copy-start(bf16[1,224,2048]{2,1,0:T(8,128)(2,1)} %param.16) | copy-start | bytes 2752516
  85.3 1.1 copy-start.1
  88.2 0.8 copy-start.3
  89.0 25.2 %all-to-all-start.3 = ((bf16[32,64,128]{2,1,0:T(8,128)(2,1)}), bf16[32,64,128]{2,1,0:T(8,128)(2,1)S(1)}, u32[]{:S(2)}, u32[]{:S(2)}) async-start(bf16[32,64,128]{2,1,0:T(8,128)(2,1)} %copy-done.3), calls=%async_computation.3 | async-start | bytes 1048576 | tf_op jit(solution)/shard_map/all_to_all | solution.py:250
  98.0 2.5 %copy-start.2 = (bf16[8,48,2048]{2,1,0:T(8,128)(2,1)S(1)}, bf16[8,48,2048]{2,1,0:T(8,128)(2,1)}, u32[]{:S(2)}) copy-start(bf16[8,48,2048]{2,1,0:T(8,128)(2,1)} %copy-done.1) | copy-start | bytes 4718596
  98.1 2.5 %copy-start.5 = (f32[384,224]{1,0:T(8,128)S(1)}, f32[384,224]{1,0:T(8,128)}, u32[]{:S(2)}) copy-start(f32[384,224]{1,0:T(8,128)} %copy-done.4) | copy-start | bytes 1032196
  98.1 2.5 %copy-start.20 = (f32[384,224]{1,0:T(8,128)S(1)}, f32[384,224]{1,0:T(8,128)}, u32[]{:S(2)}) copy-start(f32[384,224]{1,0:T(8,128)} %fusion) | copy-start | bytes 1032196
  98.1 2.4 %copy-start.21 = (f32[384,224]{1,0:T(8,128)S(1)}, f32[384,224]{1,0:T(8,128)}, u32[]{:S(2)}) copy-start(f32[384,224]{1,0:T(8,128)} %fusion.2) | copy-start | bytes 1032196
  100.5 2.0 %copy-start.22 = (f32[384,224]{1,0:T(8,128)S(1)}, f32[384,224]{1,0:T(8,128)}, u32[]{:S(2)}) copy-start(f32[384,224]{1,0:T(8,128)} %fusion.21) | copy-start | bytes 1032196

commit v2 on v1

v2 whole, which is shorter than its diff:
```python
import jax
import jax.numpy as jnp
from jax import lax
from jax.experimental import pallas as pl
from jax.experimental.pallas import tpu as pltpu
from jax.sharding import Mesh, PartitionSpec as P

F32, BF16, I32 = jnp.float32, jnp.bfloat16, jnp.int32
CAP = 48
HALF = CAP // 2
EXPERTS = 8
X, Z, Y = 4, 8, 4
VMEM_LIMIT = 16 * 1024 * 1024

DP_AXES = ("x", "z")
EXPERT_AXES = ("y", "c")
BACK_AXES = ("z", "y", "c")

sds = jax.ShapeDtypeStruct
SMEM = pl.BlockSpec(memory_space=pltpu.SMEM)
VMEM = pl.BlockSpec(memory_space=pltpu.VMEM)
HBM = pl.BlockSpec(memory_space=pltpu.HBM)
ANY = pl.BlockSpec(memory_space=pl.ANY)


def call(body, ins, outs, scratch=(), mflops=0, **kwargs):
    specs, shapes = [pair[0] for pair in outs], [pair[1] for pair in outs]
    single = len(outs) == 1
    return pl.pallas_call(
        body,
        out_shape=shapes[0] if single else shapes,
        in_specs=ins,
        out_specs=specs[0] if single else specs,
        scratch_shapes=list(scratch),
        cost_estimate=pl.CostEstimate(
            flops=mflops * 1000000, bytes_accessed=4000000, transcendentals=0
        ),
        compiler_params=pltpu.CompilerParams(vmem_limit_bytes=VMEM_LIMIT),
        **kwargs,
    )


def in_hbm(value):
    return pltpu.with_memory_space_constraint(value, pltpu.HBM)


def dma(source, target, sem):
    copy = pltpu.make_async_copy(source, target, sem)
    copy.start()
    return copy


def iota(shape, dim):
    return lax.broadcasted_iota(I32, shape, dim)


def slots_of(routes):
    first, second = routes[0:1, :], routes[1:2, :]
    tok = routes.shape[1]
    experts = iota((EXPERTS, tok), 0)
    is_first, is_second = experts == first, experts == second
    member = jnp.where(is_first | is_second, 1.0, 0.0).astype(BF16)
    before = jnp.where(iota((tok, tok), 0) < iota((tok, tok), 1), 1.0, 0.0).astype(BF16)
    count = jnp.dot(member, before, preferred_element_type=F32)
    pos_first = jnp.sum(jnp.where(is_first, count, 0.0), axis=0, keepdims=True).astype(I32)
    pos_second = jnp.sum(jnp.where(is_second, count, 0.0), axis=0, keepdims=True).astype(I32)
    return first, second, pos_first, pos_second


def gate_probs(logits):
    first = jax.nn.sigmoid(logits[0:1, :] - logits[1:2, :])
    return first, 1.0 - first


def nt_dot(rows, matrix):
    return lax.dot_general(rows, matrix, (((1,), (1,)), ((), ())), preferred_element_type=F32)


def tn_dot(rows, matrix):
    return lax.dot_general(rows, matrix, (((0,), (0,)), ((), ())), preferred_element_type=F32)


def send_tokens_body(routes_hbm, tok_hbm, out_hbm, routes_ref, tok_ref, out_ref, sems):
    get_routes = dma(routes_hbm, routes_ref, sems.at[0])
    get_tok = dma(tok_hbm, tok_ref, sems.at[1])
    get_routes.wait()
    first, second, pos_first, pos_second = slots_of(routes_ref[...])
    tok = tok_ref.shape[0]
    rows = iota((EXPERTS * CAP, tok), 0)
    hit = (rows == first * CAP + pos_first) | (rows == second * CAP + pos_second)
    dispatch = jnp.where(hit, 1.0, 0.0).astype(BF16)
    get_tok.wait()
    tokens = tok_ref[...]
    puts = []
    part = EXPERTS // 2
    for j in range(2):
        picked = jnp.dot(
            dispatch[j * part * CAP : (j + 1) * part * CAP], tokens, preferred_element_type=F32
        )
        out_ref[j * part : (j + 1) * part] = picked.astype(BF16).reshape(part, CAP, -1)
        where = pl.ds(j * part, part)
        puts.append(dma(out_ref.at[where], out_hbm.at[where], sems.at[2 + j]))
    for put in puts:
        put.wait()


def send_cot_body(at_ref, *refs):
    routes_refs, logits_refs, cot_refs = refs[0:2], refs[2:4], refs[4:6]
    out_refs = refs[6:]
    y, c = at_ref[0], at_ref[1]
    for j in range(2):
        first, second, pos_first, pos_second = slots_of(routes_refs[j][...])
        prob_first, prob_second = gate_probs(logits_refs[j][...])
        tok = cot_refs[j].shape[0]
        rows = iota((Y * CAP, tok), 0)

        def hit(expert, pos):
            row = ((expert >> 1) ^ y) * CAP + pos
            return rows == jnp.where((expert & 1) == c, row, -1)

        hit_first, hit_second = hit(first, pos_first), hit(second, pos_second)
        dispatch = jnp.where(hit_first | hit_second, 1.0, 0.0).astype(BF16)
        weight = jnp.where(hit_first, prob_first, 0.0) + jnp.where(hit_second, prob_second, 0.0)
        weight = jnp.sum(weight, axis=1, keepdims=True)
        picked = jnp.dot(dispatch, cot_refs[j][...], preferred_element_type=F32)
        scaled = (picked * weight).astype(BF16)
        for i, out_ref in enumerate(out_refs):
            out_ref[j] = scaled[i * CAP : (i + 1) * CAP]


def split_down_body(at_ref, down_ref, *out_refs):
    me = at_ref[2]
    width = out_refs[0].shape[1]
    for i, out_ref in enumerate(out_refs):
        start = pl.multiple_of((me ^ i) * width, 128)
        out_ref[...] = down_ref[:, pl.ds(start, width)]


def forward_body(x_ref, gate_hbm, up_hbm, *refs):
    pre_hbm, value_hbm, hidden_ref, gate_ref, up_ref, pre_ref, value_ref, sems = refs[-8:]
    get_gate = dma(gate_hbm, gate_ref, sems.at[0])
    get_up = dma(up_hbm, up_ref, sems.at[1])
    rows = x_ref[...]
    get_gate.wait()
    pre = nt_dot(gate_ref[...], rows)
    pre_ref[...] = pre
    put_pre = dma(pre_ref, pre_hbm, sems.at[2])
    get_up.wait()
    value = nt_dot(up_ref[...], rows)
    value_ref[...] = value
    put_value = dma(value_ref, value_hbm, sems.at[3])
    hidden_ref[...] = (pre * jax.nn.sigmoid(pre) * value).astype(BF16)
    put_pre.wait()
    put_value.wait()


def down_body(*refs):
    hidden_refs, down_hbms, out_hbm = refs[:X], refs[X : 2 * X], refs[2 * X]
    down_refs, (out_ref, sems) = refs[2 * X + 1 : 3 * X + 1], refs[3 * X + 1 :]
    gets = [dma(a, b, sems.at[i]) for i, (a, b) in enumerate(zip(down_hbms, down_refs))]
    total = None
    for i in range(X):
        gets[i].wait()
        part = tn_dot(hidden_refs[i][...], down_refs[i][...])
        total = part if total is None else total + part
    left = iota((HALF, 128), 1) < 64
    puts = []
    for m in range(Z // 2):
        cols = slice(128 * m, 128 * m + 128)
        for s in range(EXPERTS):
            upper = total[s * CAP : s * CAP + HALF, cols]
            lower = total[s * CAP + HALF : (s + 1) * CAP, cols]
            even = jnp.where(left, upper, pltpu.roll(lower, 64, 1))
            odd = jnp.where(left, pltpu.roll(upper, 64, 1), lower)
            out_ref[2 * m * EXPERTS + s] = even.astype(BF16)
            out_ref[(2 * m + 1) * EXPERTS + s] = odd.astype(BF16)
        where = pl.ds(2 * m * EXPERTS, 2 * EXPERTS)
        puts.append(dma(out_ref.at[where], out_hbm.at[where], sems.at[X + m]))
    for put in puts:
        put.wait()


def combine_body(routes_ref, logits_ref, back_ref, _, out_ref):
    first, second, pos_first, pos_second = slots_of(routes_ref[...])
    prob_first, prob_second = gate_probs(logits_ref[...])
    tok = routes_ref.shape[1]
    total = back_ref[0:EXPERTS].astype(F32)
    for z in range(1, Z):
        total = total + back_ref[z * EXPERTS : (z + 1) * EXPERTS].astype(F32)
    held = total.astype(BF16).reshape(EXPERTS * HALF, 128)
    rows = iota((EXPERTS * HALF, tok), 0)

    def pick(expert, pos):
        base = expert * HALF + pos
        in_upper = jnp.where((rows == base) & (pos < HALF), 1.0, 0.0).astype(BF16)
        in_lower = jnp.where((rows == base - HALF) & (pos >= HALF), 1.0, 0.0).astype(BF16)
        return tn_dot(held, in_upper)[0:64] + tn_dot(held, in_lower)[64:128]

    mixed = prob_first * pick(first, pos_first) + prob_second * pick(second, pos_second)
    mixed = mixed.astype(BF16)
    for z in range(Z):
        out_ref[z] = mixed


def turn_body(at_ref, *refs):
    out_ref = refs[-1]
    me = at_ref[2]
    for i, ref in enumerate(refs[:-1]):
        rows = ref.shape[0] * ref.shape[1]
        block = ref[...].reshape(rows, ref.shape[2])
        for m in range(rows // 128):
            start = pl.multiple_of((me ^ i) * rows + 128 * m, 128)
            out_ref[:, pl.ds(start, 128)] = block[128 * m : 128 * m + 128].T


def tangent_body(
    x_ref, pre_ref, value_ref, gate_dir_ref, up_dir_ref, *out_refs
):
    by_tq_gate_ref, by_q_gate_ref, by_tq_up_ref, by_q_up_ref, hidden_tang_ref = out_refs
    rows = x_ref[...]
    tang_gate = nt_dot(gate_dir_ref[...], rows)
    tang_up = nt_dot(up_dir_ref[...], rows)
    pre, value = pre_ref[...], value_ref[...]
    sig = jax.nn.sigmoid(pre)
    slope_one = sig * (1.0 + pre * (1.0 - sig))
    slope_two = sig * (1.0 - sig) * (2.0 + pre * (1.0 - 2.0 * sig))
    silu = pre * sig
    silu_tang = slope_one * tang_gate
    by_tq_gate_ref[...] = value * slope_one
    by_q_gate_ref[...] = tang_up * slope_one + value * slope_two * tang_gate
    by_tq_up_ref[...] = silu
    by_q_up_ref[...] = silu_tang
    hidden_tang_ref[...] = (silu_tang * value + silu * tang_up).astype(BF16)


def residual_body(at_ref, down_ref, down_dir_ref, *refs):
    pieces, factors = refs[0:Y], refs[Y : Y + 4]
    slot_c_ref, resid_gate_ref, resid_up_ref = refs[Y + 4 :]
    by_tq_gate_ref, by_q_gate_ref, by_tq_up_ref, by_q_up_ref = factors
    y, c = at_ref[0], at_ref[1]
    for i, piece in enumerate(pieces):
        for j in range(2):
            start = pl.multiple_of((2 * (y ^ i) + (c ^ j)) * CAP, CAP)
            slot_c_ref[pl.ds(start, CAP), :] = piece[j]
    rows = slot_c_ref[...]
    back_grad = nt_dot(down_ref[...], rows)
    back_tang = nt_dot(down_dir_ref[...], rows)
    resid_gate = back_tang * by_tq_gate_ref[...] + back_grad * by_q_gate_ref[...]
    resid_up = back_tang * by_tq_up_ref[...] + back_grad * by_q_up_ref[...]
    resid_gate_ref[...] = resid_gate.astype(BF16)
    resid_up_ref[...] = resid_up.astype(BF16)


def outer_body(gate_units_ref, up_units_ref, down_units_ref, x_ref, c_ref, *refs):
    outs, holds, sems = refs[0:3], refs[3:6], refs[6]
    width = x_ref.shape[1]
    step = width // 4
    puts = []
    for g in range(4):
        cols = pl.ds(g * step, step)
        for k, (units_ref, rows_ref) in enumerate(
            ((gate_units_ref, x_ref), (up_units_ref, x_ref), (down_units_ref, c_ref))
        ):
            holds[k][0, :, cols] = jnp.dot(
                units_ref[...], rows_ref[:, cols], preferred_element_type=F32
            )
            puts.append(
                dma(holds[k].at[:, :, cols], outs[k].at[:, :, cols], sems.at[3 * g + k])
            )
    for put in puts:
        put.wait()


def spread(pieces, axes):
    arrived = [pieces[0]]
    for i in range(1, len(pieces)):
        pairs = [(d, d ^ i) for d in range(len(pieces))]
        arrived.append(lax.ppermute(pieces[i], axes, pairs))
    return arrived


def exchange(value, axes):
    return lax.all_to_all(value, axes, 0, 0, tiled=True)


def shards(
    tokens,
    cotangent,
    router_logits,
    routes,
    gate_weight,
    up_weight,
    down_weight,
    dir_gate,
    dir_up,
    dir_down,
):
    tok, width = tokens.shape
    rows = EXPERTS * CAP
    units = gate_weight.shape[1]
    quarter = width // X
    routes_t, logits_t = routes.T, router_logits.T
    at = jnp.stack([lax.axis_index("y"), lax.axis_index("c"), lax.axis_index("x")]).astype(I32)
    down_mat = down_weight[0]
    gate_dir, up_dir, down_dir = dir_gate[0], dir_up[0], dir_down[0]
    dma_sems = pltpu.SemaphoreType.DMA

    send_x = call(
        send_tokens_body,
        [HBM, HBM],
        [(HBM, pltpu.HBM((EXPERTS, CAP, width), BF16))],
        [
            pltpu.VMEM((2, tok), I32),
            pltpu.VMEM((tok, width), BF16),
            pltpu.VMEM((EXPERTS, CAP, width), BF16),
            dma_sems((4,)),
        ],
        mflops=200,
    )(in_hbm(routes_t), in_hbm(tokens))
    slot_x = exchange(send_x, EXPERT_AXES).reshape(rows, width)

    send_down = call(
        split_down_body, [SMEM, VMEM], [(VMEM, pltpu.HBM((units, quarter), BF16))] * X, mflops=200
    )(at, in_hbm(down_mat))
    down_parts = spread(send_down, "x")
    routes_two, logits_two, cot_two = (
        spread([value] * 2, "c") for value in (routes_t, logits_t, cotangent)
    )
    send_c = call(
        send_cot_body,
        [SMEM] + [VMEM] * 6,
        [(VMEM, pltpu.HBM((2, CAP, width), BF16))] * Y,
        mflops=400,
    )(at, *routes_two, *logits_two, *cot_two)

    factor = (VMEM, pltpu.HBM((units, rows), F32))
    half_factor = (VMEM, pltpu.HBM((units, rows), BF16))
    preact, up_value, hidden = call(
        forward_body,
        [VMEM, HBM, HBM] + [ANY] * Y,
        [(HBM, pltpu.HBM((units, rows), F32))] * 2 + [(VMEM, sds((units, rows), BF16))],
        [pltpu.VMEM((units, width), BF16)] * 2
        + [pltpu.VMEM((units, rows), F32)] * 2
        + [dma_sems((4,))],
        mflops=704,
    )(slot_x, in_hbm(gate_weight[0]), in_hbm(up_weight[0]), *[in_hbm(v) for v in send_c])

    hidden_parts = spread([hidden] * X, "x")
    partial_out = call(
        down_body,
        [VMEM] * X + [HBM] * X,
        [(HBM, pltpu.HBM((Z * EXPERTS, HALF, 128), BF16))],
        [pltpu.VMEM((units, quarter), BF16)] * X
        + [pltpu.VMEM((Z * EXPERTS, HALF, 128), BF16), dma_sems((X + Z // 2,))],
        mflops=352,
    )(*hidden_parts, *[in_hbm(part) for part in down_parts])

    pieces = spread(send_c, "y")

    back = exchange(partial_out, BACK_AXES)
    *factors, hidden_tang = call(
        tangent_body, [VMEM] * 5, [factor] * 4 + [half_factor], mflops=704
    )(slot_x, in_hbm(preact), in_hbm(up_value), in_hbm(gate_dir), in_hbm(up_dir))
    share = call(
        combine_body, [VMEM] * 3 + [ANY], [(VMEM, pltpu.HBM((Z, 64, tok), BF16))], mflops=100
    )(routes_t, logits_t, back, in_hbm(hidden_tang))
    over_z = exchange(share, "z")
    blocks = spread([over_z] * X, "x")
    mixed = call(
        turn_body, [SMEM] + [VMEM] * X, [(VMEM, sds((tok, width), BF16))], mflops=100
    )(at, *blocks)

    slot_c, resid_gate, resid_up = call(
        residual_body,
        [SMEM] + [VMEM] * (2 + Y + 4),
        [(VMEM, pltpu.HBM((rows, width), BF16)), half_factor, half_factor],
        mflops=904,
    )(at, *[in_hbm(v) for v in (down_mat, down_dir, *pieces, *factors)])
    hold = pltpu.VMEM((1, units, width), F32)
    out = (HBM, pltpu.HBM((1, units, width), F32))
    hvp = call(outer_body, [VMEM] * 5, [out] * 3, [hold] * 3 + [dma_sems((12,))], mflops=1056)(
        in_hbm(resid_gate),
        in_hbm(resid_up),
        in_hbm(hidden_tang),
        slot_x,
        in_hbm(slot_c),
    )
    return (mixed, *hvp)


def solution(mesh):
    grid = Mesh(mesh.devices.reshape(X, Z, Y, 2), ("x", "z", "y", "c"))
    by_expert = P(EXPERT_AXES, None)
    by_both = P(EXPERT_AXES, DP_AXES, None)

    def step(*args):
        return shards(*args)

    step = jax.shard_map(
        step,
        mesh=grid,
        in_specs=(by_expert,) * 4 + (by_both,) * 6,
        out_specs=(by_expert,) + (by_both,) * 3,
        check_vma=False,
    )
    return step
```

time: 117 us -> 103 us (0.88)
  Pallas kernels: 8.83 us -> 28.6 us
  matrix products: 13.8 us -> 0 us
  blocking collectives: 26.1 us -> 13 us
  local copies, waits for them, and re-layouts: 7.67 us -> 0.04 us
  starting transfers between devices: 31.7 us -> 33.1 us
    pallas_call x7 -> x10, Pallas kernels: 8.83 us -> 28.6 us  [the longest x1 4.48 us: shards(): call(outer_body, [VMEM] * 5, [out] * 3, [hold] * 3 + [dma_sems((12,))], m...]
    dot_general x7 -> x0, matrix products: 13.8 us -> none  [the longest x3 6.2 us: outer_sum(): jnp.einsum('rh,rd->hd', left_rows, right_rows, preferred_element_type=F32)]
    all_to_all x1, blocking collectives: 26.1 us -> 13 us  [exchange(): return lax.all_to_all(value, axes, 0, 0, tiled=True)]
    ppermute x7 -> x15, starting transfers between devices: 8.09 us -> 18.8 us  [spread(): arrived.append(lax.ppermute(pieces[i], axes, pairs))]
    all_to_all x3 -> x2, starting transfers between devices: 23.6 us -> 14.4 us  [exchange(): return lax.all_to_all(value, axes, 0, 0, tiled=True)]
    unnamed x46 -> x16, local copies, waits for them, and re-layouts: 7.67 us -> 0.04 us
    all_to_all x3 -> x2, waiting for transfers between devices: 17.4 us -> 16.6 us  [exchange(): return lax.all_to_all(value, axes, 0, 0, tiled=True)]
    ppermute x7 -> x15, waiting for transfers between devices: 8.8 us -> 9.48 us  [spread(): arrived.append(lax.ppermute(pieces[i], axes, pairs))]
  transfers between devices with their start and end apart: 10 -> 17, of which waited for: 4 -> 5; matrix products, arithmetic and copies ran while one was open for 12% -> 0% of each run, Pallas kernels for 5% -> 21%
where the time goes in v2:
time: 103 us; the launch traced here: 102 us
  starting transfers between devices  33.1 us (32%)
  Pallas kernels  28.6 us (28%)
  waiting for transfers between devices  26.1 us (25%)
  blocking collectives  13 us (13%)
    ppermute x15, starting transfers between devices, spread(): arrived.append(lax.ppermute(pieces[i], axes, pairs))  18.8 us
    all_to_all x2, waiting for transfers between devices, exchange(): return lax.all_to_all(value, axes, 0, 0, tiled=True)  16.6 us
    all_to_all x2, starting transfers between devices, exchange(): return lax.all_to_all(value, axes, 0, 0, tiled=True)  14.4 us
    all_to_all x1, blocking collectives, exchange(): return lax.all_to_all(value, axes, 0, 0, tiled=True)  13 us
    ppermute x15, waiting for transfers between devices, spread(): arrived.append(lax.ppermute(pieces[i], axes, pairs))  9.48 us
    pallas_call x1, Pallas kernels, shards(): call(outer_body, [VMEM] * 5, [out] * 3, [hold] * 3 + [dma_sems((12,))], m...  4.48 us
    pallas_call x1, Pallas kernels, shards(): call(residual_body, [SMEM] + [VMEM] * (2 + Y + 4), [(VMEM, pltpu.HBM((row...  4.38 us
    pallas_call x1, Pallas kernels, shards(): call(tangent_body, [VMEM] * 5, [factor] * 4 + [half_factor], mflops=704)  3.79 us
  transfers between devices with their start and end apart: 17, of which 5 were waited for; matrix products, arithmetic and copies ran while one was open for 0% of the time, Pallas kernels for 21%

profile of v2, /device:TPU:32, one launch (start us, length us, event | category | flops | bytes accessed | tf_op | source)
XLA Modules:
  0.0 101.7 jit_solution(13311731678257718405)
XLA Ops:
  0.6 2.6 %shard_map.129 = bf16[8,48,2048]{2,1,0:T(8,128)(2,1)} custom-call(s32[2,128]{1,0:T(2,128)} %bitcast.15, bf16[128,2048]{1,0:T(8,128)(2,1)} %tok_hbm.1), custom_call_target="tpu_custom_call" | custom-call | flops 200000000 | bytes 4000000 | tf_op jit(solution)/shard_map/pallas_call | solution.py:308
  3.2 0.0 copy-start.2
  3.2 0.0 copy-start
  3.2 0.0 copy-start.1
  3.3 4.6 %all-to-all-start = ((bf16[8,48,2048]{2,1,0:T(8,128)(2,1)}), bf16[8,48,2048]{2,1,0:T(8,128)(2,1)S(1)}, u32[]{:S(2)}, u32[]{:S(2)}) async-start(bf16[8,48,2048]{2,1,0:T(8,128)(2,1)} %shard_map.129), calls=%async_computation | async-start | bytes 3145728 | tf_op jit(solution)/shard_map/all_to_all | solution.py:283
  7.9 0.0 copy-done.2
  7.9 0.5 collective-permute-start.2
  8.4 0.1 pad_add_fusion.at_ref
  8.5 2.2 %shard_map.132 = (bf16[224,512]{1,0:T(8,128)(2,1)}, bf16[224,512]{1,0:T(8,128)(2,1)}, bf16[224,512]{1,0:T(8,128)(2,1)}, bf16[224,512]{1,0:T(8,128)(2,1)}) custom-call(s32[3]{0:T(128)S(1)} %pad_add_fusion.at_ref, bf16[224,2048]{1,0:T(8,128)(2,1)} %bitcast.22), custom_call_target="tpu_custom_call" | custom-call | flops 200000000 | bytes 4000000 | tf_op jit(solution)/shard_map/pallas_call | solution.py:322
  10.7 1.5 %collective-permute-start.6 = (bf16[224,512]{1,0:T(8,128)(2,1)}, bf16[224,512]{1,0:T(8,128)(2,1)S(1)}, u32[]{:S(2)}, u32[]{:S(2)}) collective-permute-start(bf16[224,512]{1,0:T(8,128)(2,1)} %get-tuple-element.32), channel_id=1, source_target_pairs={{0,64},{64,0},{128,192},{192,128},{1,65},{65,1},{129,193},{193,129... | collective-permute-start | bytes 688136 | tf_op jit(solution)/shard_map/ppermute | solution.py:278
  12.2 0.0 copy-done
  12.2 0.0 collective-permute-start
  12.2 0.0 copy-done.1
  12.2 0.5 collective-permute-start.1
  12.7 2.7 %collective-permute-start.7 = (bf16[224,512]{1,0:T(8,128)(2,1)}, bf16[224,512]{1,0:T(8,128)(2,1)}, u32[]{:S(2)}, u32[]{:S(2)}) collective-permute-start(bf16[224,512]{1,0:T(8,128)(2,1)} %get-tuple-element.33), channel_id=1, source_target_pairs={{0,128},{64,192},{128,0},{192,64},{1,129},{65,193},{129,1},{193,65... | collective-permute-start | bytes 688136 | tf_op jit(solution)/shard_map/ppermute | solution.py:278
  15.4 0.0 collective-permute-done.refs_1_
  15.4 0.5 collective-permute-start.8
  15.9 0.0 collective-permute-done.1.refs_3_
  15.9 0.0 collective-permute-done.2.refs_5_
  15.9 2.5 %shard_map.130 = (bf16[2,48,2048]{2,1,0:T(8,128)(2,1)}, bf16[2,48,2048]{2,1,0:T(8,128)(2,1)}, bf16[2,48,2048]{2,1,0:T(8,128)(2,1)}, bf16[2,48,2048]{2,1,0:T(8,128)(2,1)}) custom-call(s32[3]{0:T(128)S(1)} %pad_add_fusion.at_ref, s32[2,128]{1,0:T(2,128)S(1)} %bitcast.17, s32[2,128]{1,0:T(2,128)S(1)} %collective-permute-done.refs_1_, f32[2,128]{1,0:T(2,128)S(1)} %bitcast.20, ...), custom_call_target="tpu_custom_call" | custom-call | flops 400000000 | bytes 4000000 | tf_op jit(solution)/shard_map/pallas_call | solution.py:329
  18.4 11.0 %all-to-all-done = bf16[8,48,2048]{2,1,0:T(8,128)(2,1)S(1)} async-done(((bf16[8,48,2048]{2,1,0:T(8,128)(2,1)}), bf16[8,48,2048]{2,1,0:T(8,128)(2,1)S(1)}, u32[]{:S(2)}, u32[]{:S(2)}) %all-to-all-start) | async-done | bytes 1572896 | tf_op jit(solution)/shard_map/all_to_all | solution.py:283
  29.4 3.4 %shard_map.131 = (f32[224,384]{1,0:T(8,128)}, f32[224,384]{1,0:T(8,128)}, bf16[224,384]{1,0:T(8,128)(2,1)S(1)}) custom-call(bf16[384,2048]{1,0:T(8,128)(2,1)S(1)} %bitcast.12, bf16[224,2048]{1,0:T(8,128)(2,1)} %bitcast.24, bf16[224,2048]{1,0:T(8,128)(2,1)} %bitcast.25, bf16[2,48,2048]{2,1,0:T(8,128)(2,1)} %get-tuple-element.26.refs_0_, ...), custom_call_target="tpu_custom_call" | custom-call | flops 704000000 | bytes 4000000 | tf_op jit(solution)/shard_map/pallas_call | solution.py:338
  32.8 0.0 copy-start.5
  32.9 0.0 copy-start.4
  32.9 0.0 copy-start.3
  32.9 1.6 %collective-permute-start.3 = (bf16[224,384]{1,0:T(8,128)(2,1)S(1)}, bf16[224,384]{1,0:T(8,128)(2,1)S(1)}, u32[]{:S(2)}, u32[]{:S(2)}) collective-permute-start(bf16[224,384]{1,0:T(8,128)(2,1)S(1)} %get-tuple-element.30.refs_0_), channel_id=1, source_target_pairs={{0,64},{64,0},{128,192},{192,128},{1,65},{65,1},{129,193},{193,129... | collective-permute-start | bytes 516104 | tf_op jit(solution)/shard_map/ppermute | solution.py:278
  34.4 2.7 %collective-permute-start.4 = (bf16[224,384]{1,0:T(8,128)(2,1)S(1)}, bf16[224,384]{1,0:T(8,128)(2,1)S(1)}, u32[]{:S(2)}, u32[]{:S(2)}) collective-permute-start(bf16[224,384]{1,0:T(8,128)(2,1)S(1)} %get-tuple-element.30.refs_0_), channel_id=1, source_target_pairs={{0,128},{64,192},{128,0},{192,64},{1,129},{65,193},{129,1},{193,65... | collective-permute-start | bytes 516104 | tf_op jit(solution)/shard_map/ppermute | solution.py:278
  37.2 0.0 collective-permute-done.6.refs_5_
  37.2 0.0 copy-start.7
  37.2 0.5 collective-permute-start.5
  37.7 0.0 collective-permute-done.7.refs_6_
  37.7 0.0 collective-permute-done.8.refs_7_
  37.7 2.5 %collective-permute-done.3.refs_1_ = bf16[224,384]{1,0:T(8,128)(2,1)S(1)} collective-permute-done((bf16[224,384]{1,0:T(8,128)(2,1)S(1)}, bf16[224,384]{1,0:T(8,128)(2,1)S(1)}, u32[]{:S(2)}, u32[]{:S(2)}) %collective-permute-start.3) | collective-permute-done | bytes 172064 | tf_op jit(solution)/shard_map/ppermute | solution.py:278
  40.2 4.5 %collective-permute-done.4.refs_2_ = bf16[224,384]{1,0:T(8,128)(2,1)S(1)} collective-permute-done((bf16[224,384]{1,0:T(8,128)(2,1)S(1)}, bf16[224,384]{1,0:T(8,128)(2,1)S(1)}, u32[]{:S(2)}, u32[]{:S(2)}) %collective-permute-start.4) | collective-permute-done | bytes 172064 | tf_op jit(solution)/shard_map/ppermute | solution.py:278
  44.8 2.4 %collective-permute-done.5.refs_3_ = bf16[224,384]{1,0:T(8,128)(2,1)S(1)} collective-permute-done((bf16[224,384]{1,0:T(8,128)(2,1)S(1)}, bf16[224,384]{1,0:T(8,128)(2,1)S(1)}, u32[]{:S(2)}, u32[]{:S(2)}) %collective-permute-start.5) | collective-permute-done | bytes 172064 | tf_op jit(solution)/shard_map/ppermute | solution.py:278
  47.1 0.0 copy-done.7
  47.1 2.7 %shard_map.133 = bf16[64,24,128]{2,1,0:T(8,128)(2,1)} custom-call(bf16[224,384]{1,0:T(8,128)(2,1)S(1)} %get-tuple-element.30.refs_0_, bf16[224,384]{1,0:T(8,128)(2,1)S(1)} %collective-permute-done.3.refs_1_, bf16[224,384]{1,0:T(8,128)(2,1)S(1)} %collective-permute-done.4.refs_2_, bf16[224,384]{1,0:T(8,128)(2,1)S(1)} %collective-permute-done.5.refs_3_, ...), custom_call_target="tpu_custom_call" | custom-call | flops 352000000 | bytes 4000000 | tf_op jit(solution)/shard_map/pallas_call | solution.py:349
  49.8 9.7 %all-to-all-start.1 = ((bf16[64,24,128]{2,1,0:T(8,128)(2,1)}), bf16[64,24,128]{2,1,0:T(8,128)(2,1)S(1)}, u32[]{:S(2)}, u32[]{:S(2)}) async-start(bf16[64,24,128]{2,1,0:T(8,128)(2,1)} %shard_map.133), calls=%async_computation.1 | async-start | bytes 786432 | tf_op jit(solution)/shard_map/all_to_all | solution.py:283
  59.6 0.0 copy-done.5
  59.6 1.6 %collective-permute-start.12 = (bf16[2,48,2048]{2,1,0:T(8,128)(2,1)S(1)}, bf16[2,48,2048]{2,1,0:T(8,128)(2,1)S(1)}, u32[]{:S(2)}, u32[]{:S(2)}) collective-permute-start(bf16[2,48,2048]{2,1,0:T(8,128)(2,1)S(1)} %copy-done.5), channel_id=1, source_target_pairs={{0,2},{2,0},{4,6},{6,4},{1,3},{3,1},{5,7},{7,5},{8,10},{10,8},{12,... | collective-permute-start | bytes 1179656 | tf_op jit(solution)/shard_map/ppermute | solution.py:278
  61.1 0.0 copy-done.4
  61.1 2.7 %collective-permute-start.13 = (bf16[2,48,2048]{2,1,0:T(8,128)(2,1)S(1)}, bf16[2,48,2048]{2,1,0:T(8,128)(2,1)}, u32[]{:S(2)}, u32[]{:S(2)}) collective-permute-start(bf16[2,48,2048]{2,1,0:T(8,128)(2,1)S(1)} %copy-done.4), channel_id=1, source_target_pairs={{0,4},{2,6},{4,0},{6,2},{1,5},{3,7},{5,1},{7,3},{8,12},{10,14},{12... | collective-permute-start | bytes 1179656 | tf_op jit(solution)/shard_map/ppermute | solution.py:278
  63.8 0.0 copy-done.3
  63.8 0.6 collective-permute-start.14
  64.4 3.8 %shard_map.134 = (f32[224,384]{1,0:T(8,128)}, f32[224,384]{1,0:T(8,128)}, f32[224,384]{1,0:T(8,128)}, f32[224,384]{1,0:T(8,128)}, bf16[224,384]{1,0:T(8,128)(2,1)}) custom-call(bf16[384,2048]{1,0:T(8,128)(2,1)S(1)} %bitcast.13, f32[224,384]{1,0:T(8,128)} %get-tuple-element.35.pre_ref, f32[224,384]{1,0:T(8,128)} %get-tuple-element.36.value_ref, ...), custom_call_target="tpu_custom_call" | custom-call | flops 704000000 | bytes 4000000 | tf_op jit(solution)/shard_map/pallas_call | solution.py:361
  68.2 5.6 %all-to-all-done.1.back_ref = bf16[64,24,128]{2,1,0:T(8,128)(2,1)S(1)} async-done(((bf16[64,24,128]{2,1,0:T(8,128)(2,1)}), bf16[64,24,128]{2,1,0:T(8,128)(2,1)S(1)}, u32[]{:S(2)}, u32[]{:S(2)}) %all-to-all-start.1) | async-done | bytes 393248 | tf_op jit(solution)/shard_map/all_to_all | solution.py:283
  73.7 1.0 %shard_map.135 = bf16[8,64,128]{2,1,0:T(8,128)(2,1)} custom-call(s32[2,128]{1,0:T(2,128)S(1)} %bitcast.18, f32[2,128]{1,0:T(2,128)S(1)} %bitcast.21, bf16[64,24,128]{2,1,0:T(8,128)(2,1)S(1)} %all-to-all-done.1.back_ref, bf16[224,384]{1,0:T(8,128)(2,1)} %get-tuple-element.37._.down_units_ref), custom_call_target="tpu_custom_call" | custom-call | flops 100000000 | bytes 4000000 | tf_op jit(solution)/shard_map/pallas_call | solution.py:364
  74.8 13.0 %all_to_all.15.refs_0_ = bf16[8,64,128]{2,1,0:T(8,128)(2,1)S(1)} all-to-all(bf16[8,64,128]{2,1,0:T(8,128)(2,1)} %shard_map.135), channel_id=1, replica_groups=mesh['x'=4,'z'=8,'y'=4,'c'=2] {'z'}, dimensions={0} | all-to-all | bytes 262144 | tf_op jit(solution)/shard_map/all_to_all | solution.py:283
  87.8 0.0 collective-permute-start.10
  87.8 1.9 %collective-permute-start.11 = (bf16[8,64,128]{2,1,0:T(8,128)(2,1)S(1)}, bf16[8,64,128]{2,1,0:T(8,128)(2,1)S(1)}, u32[]{:S(2)}, u32[]{:S(2)}) collective-permute-start(bf16[8,64,128]{2,1,0:T(8,128)(2,1)S(1)} %all_to_all.15.refs_0_), channel_id=1, source_target_pairs={{0,192},{64,128},{128,64},{192,0},{1,193},{65,129},{129,65},{193,1... | collective-permute-start | bytes 393224 | tf_op jit(solution)/shard_map/ppermute | solution.py:278
  89.7 0.0 collective-permute-done.12.refs_1_
  89.7 0.0 copy-start.6
  89.7 1.6 %collective-permute-start.9 = (bf16[8,64,128]{2,1,0:T(8,128)(2,1)S(1)}, bf16[8,64,128]{2,1,0:T(8,128)(2,1)S(1)}, u32[]{:S(2)}, u32[]{:S(2)}) collective-permute-start(bf16[8,64,128]{2,1,0:T(8,128)(2,1)S(1)} %all_to_all.15.refs_0_), channel_id=1, source_target_pairs={{0,64},{64,0},{128,192},{192,128},{1,65},{65,1},{129,193},{193,129... | collective-permute-start | bytes 393224 | tf_op jit(solution)/shard_map/ppermute | solution.py:278
  91.3 0.0 collective-permute-done.13.refs_2_
  91.3 0.0 collective-permute-done.14.refs_3_
  91.3 0.0 copy-done.6
  91.3 4.4 %shard_map.137 = (bf16[384,2048]{1,0:T(8,128)(2,1)}, bf16[224,384]{1,0:T(8,128)(2,1)}, bf16[224,384]{1,0:T(8,128)(2,1)}) custom-call(s32[3]{0:T(128)S(1)} %pad_add_fusion.at_ref, bf16[224,2048]{1,0:T(8,128)(2,1)} %bitcast.23, bf16[224,2048]{1,0:T(8,128)(2,1)} %bitcast.26, bf16[2,48,2048]{2,1,0:T(8,128)(2,1)} %get-tuple-element.26.refs_0_, ...), custom_call_target="tpu_custom_call" | custom-call | flops 904000000 | bytes 4000000 | tf_op jit(solution)/shard_map/pallas_call | solution.py:373
  95.7 4.5 %shard_map.138 = (f32[1,224,2048]{2,1,0:T(8,128)}, f32[1,224,2048]{2,1,0:T(8,128)}, f32[1,224,2048]{2,1,0:T(8,128)}) custom-call(bf16[224,384]{1,0:T(8,128)(2,1)} %get-tuple-element.42.gate_units_ref, bf16[224,384]{1,0:T(8,128)(2,1)} %get-tuple-element.43.up_units_ref, bf16[224,384]{1,0:T(8,128)(2,1)} %get-tuple-element.37._.down_units_ref, ...), custom_call_target="tpu_custom_call" | custom-call | flops 1056000000 | bytes 4000000 | tf_op jit(solution)/shard_map/pallas_call | solution.py:381
  100.2 0.0 collective-permute-done.10.refs_2_
  100.2 0.0 collective-permute-done.11.refs_3_
  100.2 0.0 collective-permute-done.9.refs_1_
  100.2 1.5 %shard_map.136 = bf16[128,2048]{1,0:T(8,128)(2,1)} custom-call(s32[3]{0:T(128)S(1)} %pad_add_fusion.at_ref, bf16[8,64,128]{2,1,0:T(8,128)(2,1)S(1)} %all_to_all.15.refs_0_, bf16[8,64,128]{2,1,0:T(8,128)(2,1)S(1)} %collective-permute-done.9.refs_1_, bf16[8,64,128]{2,1,0:T(8,128)(2,1)S(1)} %collective-permute-done.10.refs_2_, ...), custom_call_target="tpu_custom_call" | custom-call | flops 100000000 | bytes 4000000 | tf_op jit(solution)/shard_map/pallas_call | solution.py:369
Async XLA Ops:
  3.2 4.7 %copy-start.2 = (bf16[128,2048]{1,0:T(8,128)(2,1)S(1)}, bf16[128,2048]{1,0:T(8,128)(2,1)}, u32[]{:S(2)}) copy-start(bf16[128,2048]{1,0:T(8,128)(2,1)} %refs_4_.1) | copy-start | bytes 1572868
  3.2 8.9 %copy-start = (s32[128,2]{0,1:T(2,128)S(1)}, s32[128,2]{0,1:T(2,128)}, u32[]{:S(2)}) copy-start(s32[128,2]{0,1:T(2,128)} %param.13) | copy-start | bytes 3076
  3.2 8.9 %copy-start.1 = (f32[128,2]{0,1:T(2,128)S(1)}, f32[128,2]{0,1:T(2,128)}, u32[]{:S(2)}) copy-start(f32[128,2]{0,1:T(2,128)} %param.12) | copy-start | bytes 3076
  3.3 26.2 %all-to-all-start = ((bf16[8,48,2048]{2,1,0:T(8,128)(2,1)}), bf16[8,48,2048]{2,1,0:T(8,128)(2,1)S(1)}, u32[]{:S(2)}, u32[]{:S(2)}) async-start(bf16[8,48,2048]{2,1,0:T(8,128)(2,1)} %shard_map.129), calls=%async_computation | async-start | bytes 3145728 | tf_op jit(solution)/shard_map/all_to_all | solution.py:283
  7.9 8.0 %collective-permute-start.2 = (bf16[128,2048]{1,0:T(8,128)(2,1)S(1)}, bf16[128,2048]{1,0:T(8,128)(2,1)S(1)}, u32[]{:S(2)}, u32[]{:S(2)}) collective-permute-start(bf16[128,2048]{1,0:T(8,128)(2,1)S(1)} %copy-done.2), channel_id=1, source_target_pairs={{0,1},{1,0},{2,3},{3,2},{4,5},{5,4},{6,7},{7,6},{8,9},{9,8},{10,11... | collective-permute-start | bytes 1572872 | tf_op jit(solution)/shard_map/ppermute | solution.py:278
  10.7 26.5 %collective-permute-start.6 = (bf16[224,512]{1,0:T(8,128)(2,1)}, bf16[224,512]{1,0:T(8,128)(2,1)S(1)}, u32[]{:S(2)}, u32[]{:S(2)}) collective-permute-start(bf16[224,512]{1,0:T(8,128)(2,1)} %get-tuple-element.32), channel_id=1, source_target_pairs={{0,64},{64,0},{128,192},{192,128},{1,65},{65,1},{129,193},{193,129... | collective-permute-start | bytes 688136 | tf_op jit(solution)/shard_map/ppermute | solution.py:278
  12.2 3.2 %collective-permute-start = (s32[2,128]{1,0:T(2,128)S(1)}, s32[2,128]{1,0:T(2,128)S(1)}, u32[]{:S(2)}, u32[]{:S(2)}) collective-permute-start(s32[2,128]{1,0:T(2,128)S(1)} %bitcast.16), channel_id=1, source_target_pairs={{0,1},{1,0},{2,3},{3,2},{4,5},{5,4},{6,7},{7,6},{8,9},{9,8},{10,11... | collective-permute-start | bytes 3080 | tf_op jit(solution)/shard_map/ppermute | solution.py:278
  12.2 3.7 %collective-permute-start.1 = (f32[2,128]{1,0:T(2,128)S(1)}, f32[2,128]{1,0:T(2,128)S(1)}, u32[]{:S(2)}, u32[]{:S(2)}) collective-permute-start(f32[2,128]{1,0:T(2,128)S(1)} %bitcast.19), channel_id=1, source_target_pairs={{0,1},{1,0},{2,3},{3,2},{4,5},{5,4},{6,7},{7,6},{8,9},{9,8},{10,11... | collective-permute-start | bytes 3080 | tf_op jit(solution)/shard_map/ppermute | solution.py:278
  12.7 25.0 %collective-permute-start.7 = (bf16[224,512]{1,0:T(8,128)(2,1)}, bf16[224,512]{1,0:T(8,128)(2,1)}, u32[]{:S(2)}, u32[]{:S(2)}) collective-permute-start(bf16[224,512]{1,0:T(8,128)(2,1)} %get-tuple-element.33), channel_id=1, source_target_pairs={{0,128},{64,192},{128,0},{192,64},{1,129},{65,193},{129,1},{193,65... | collective-permute-start | bytes 688136 | tf_op jit(solution)/shard_map/ppermute | solution.py:278
  15.4 22.3 %collective-permute-start.8 = (bf16[224,512]{1,0:T(8,128)(2,1)}, bf16[224,512]{1,0:T(8,128)(2,1)}, u32[]{:S(2)}, u32[]{:S(2)}) collective-permute-start(bf16[224,512]{1,0:T(8,128)(2,1)} %get-tuple-element.34), channel_id=1, source_target_pairs={{0,192},{64,128},{128,64},{192,0},{1,193},{65,129},{129,65},{193,1... | collective-permute-start | bytes 688136 | tf_op jit(solution)/shard_map/ppermute | solution.py:278
  32.8 26.7 %copy-start.5 = (bf16[2,48,2048]{2,1,0:T(8,128)(2,1)S(1)}, bf16[2,48,2048]{2,1,0:T(8,128)(2,1)}, u32[]{:S(2)}) copy-start(bf16[2,48,2048]{2,1,0:T(8,128)(2,1)} %get-tuple-element.27.refs_1_) | copy-start | bytes 1179652
  32.9 28.3 %copy-start.4 = (bf16[2,48,2048]{2,1,0:T(8,128)(2,1)S(1)}, bf16[2,48,2048]{2,1,0:T(8,128)(2,1)}, u32[]{:S(2)}) copy-start(bf16[2,48,2048]{2,1,0:T(8,128)(2,1)} %get-tuple-element.28.refs_2_) | copy-start | bytes 1179652
  32.9 30.9 %copy-start.3 = (bf16[2,48,2048]{2,1,0:T(8,128)(2,1)S(1)}, bf16[2,48,2048]{2,1,0:T(8,128)(2,1)}, u32[]{:S(2)}) copy-start(bf16[2,48,2048]{2,1,0:T(8,128)(2,1)} %get-tuple-element.29.refs_3_) | copy-start | bytes 1179652
  32.9 7.3 %collective-permute-start.3 = (bf16[224,384]{1,0:T(8,128)(2,1)S(1)}, bf16[224,384]{1,0:T(8,128)(2,1)S(1)}, u32[]{:S(2)}, u32[]{:S(2)}) collective-permute-start(bf16[224,384]{1,0:T(8,128)(2,1)S(1)} %get-tuple-element.30.refs_0_), channel_id=1, source_target_pairs={{0,64},{64,0},{128,192},{192,128},{1,65},{65,1},{129,193},{193,129... | collective-permute-start | bytes 516104 | tf_op jit(solution)/shard_map/ppermute | solution.py:278
  34.4 10.3 %collective-permute-start.4 = (bf16[224,384]{1,0:T(8,128)(2,1)S(1)}, bf16[224,384]{1,0:T(8,128)(2,1)S(1)}, u32[]{:S(2)}, u32[]{:S(2)}) collective-permute-start(bf16[224,384]{1,0:T(8,128)(2,1)S(1)} %get-tuple-element.30.refs_0_), channel_id=1, source_target_pairs={{0,128},{64,192},{128,0},{192,64},{1,129},{65,193},{129,1},{193,65... | collective-permute-start | bytes 516104 | tf_op jit(solution)/shard_map/ppermute | solution.py:278
  37.2 10.0 %copy-start.7 = (bf16[224,512]{1,0:T(8,128)(2,1)}, bf16[224,512]{1,0:T(8,128)(2,1)S(1)}, u32[]{:S(2)}) copy-start(bf16[224,512]{1,0:T(8,128)(2,1)S(1)} %collective-permute-done.6.refs_5_) | copy-start | bytes 688132
  37.2 9.9 %collective-permute-start.5 = (bf16[224,384]{1,0:T(8,128)(2,1)S(1)}, bf16[224,384]{1,0:T(8,128)(2,1)S(1)}, u32[]{:S(2)}, u32[]{:S(2)}) collective-permute-start(bf16[224,384]{1,0:T(8,128)(2,1)S(1)} %get-tuple-element.30.refs_0_), channel_id=1, source_target_pairs={{0,192},{64,128},{128,64},{192,0},{1,193},{65,129},{129,65},{193,1... | collective-permute-start | bytes 516104 | tf_op jit(solution)/shard_map/ppermute | solution.py:278
  49.8 23.9 %all-to-all-start.1 = ((bf16[64,24,128]{2,1,0:T(8,128)(2,1)}), bf16[64,24,128]{2,1,0:T(8,128)(2,1)S(1)}, u32[]{:S(2)}, u32[]{:S(2)}) async-start(bf16[64,24,128]{2,1,0:T(8,128)(2,1)} %shard_map.133), calls=%async_computation.1 | async-start | bytes 786432 | tf_op jit(solution)/shard_map/all_to_all | solution.py:283
  59.6 30.1 %collective-permute-start.12 = (bf16[2,48,2048]{2,1,0:T(8,128)(2,1)S(1)}, bf16[2,48,2048]{2,1,0:T(8,128)(2,1)S(1)}, u32[]{:S(2)}, u32[]{:S(2)}) collective-permute-start(bf16[2,48,2048]{2,1,0:T(8,128)(2,1)S(1)} %copy-done.5), channel_id=1, source_target_pairs={{0,2},{2,0},{4,6},{6,4},{1,3},{3,1},{5,7},{7,5},{8,10},{10,8},{12,... | collective-permute-start | bytes 1179656 | tf_op jit(solution)/shard_map/ppermute | solution.py:278
  61.1 30.1 %collective-permute-start.13 = (bf16[2,48,2048]{2,1,0:T(8,128)(2,1)S(1)}, bf16[2,48,2048]{2,1,0:T(8,128)(2,1)}, u32[]{:S(2)}, u32[]{:S(2)}) collective-permute-start(bf16[2,48,2048]{2,1,0:T(8,128)(2,1)S(1)} %copy-done.4), channel_id=1, source_target_pairs={{0,4},{2,6},{4,0},{6,2},{1,5},{3,7},{5,1},{7,3},{8,12},{10,14},{12... | collective-permute-start | bytes 1179656 | tf_op jit(solution)/shard_map/ppermute | solution.py:278
  63.8 27.5 %collective-permute-start.14 = (bf16[2,48,2048]{2,1,0:T(8,128)(2,1)S(1)}, bf16[2,48,2048]{2,1,0:T(8,128)(2,1)}, u32[]{:S(2)}, u32[]{:S(2)}) collective-permute-start(bf16[2,48,2048]{2,1,0:T(8,128)(2,1)S(1)} %copy-done.3), channel_id=1, source_target_pairs={{0,6},{2,4},{4,2},{6,0},{1,7},{3,5},{5,3},{7,1},{8,14},{10,12},{12... | collective-permute-start | bytes 1179656 | tf_op jit(solution)/shard_map/ppermute | solution.py:278
  87.8 12.4 %collective-permute-start.10 = (bf16[8,64,128]{2,1,0:T(8,128)(2,1)S(1)}, bf16[8,64,128]{2,1,0:T(8,128)(2,1)S(1)}, u32[]{:S(2)}, u32[]{:S(2)}) collective-permute-start(bf16[8,64,128]{2,1,0:T(8,128)(2,1)S(1)} %all_to_all.15.refs_0_), channel_id=1, source_target_pairs={{0,128},{64,192},{128,0},{192,64},{1,129},{65,193},{129,1},{193,65... | collective-permute-start | bytes 393224 | tf_op jit(solution)/shard_map/ppermute | solution.py:278
  87.8 12.4 %collective-permute-start.11 = (bf16[8,64,128]{2,1,0:T(8,128)(2,1)S(1)}, bf16[8,64,128]{2,1,0:T(8,128)(2,1)S(1)}, u32[]{:S(2)}, u32[]{:S(2)}) collective-permute-start(bf16[8,64,128]{2,1,0:T(8,128)(2,1)S(1)} %all_to_all.15.refs_0_), channel_id=1, source_target_pairs={{0,192},{64,128},{128,64},{192,0},{1,193},{65,129},{129,65},{193,1... | collective-permute-start | bytes 393224 | tf_op jit(solution)/shard_map/ppermute | solution.py:278
  89.7 1.6 %copy-start.6 = (bf16[2,48,2048]{2,1,0:T(8,128)(2,1)}, bf16[2,48,2048]{2,1,0:T(8,128)(2,1)S(1)}, u32[]{:S(2)}) copy-start(bf16[2,48,2048]{2,1,0:T(8,128)(2,1)S(1)} %collective-permute-done.12.refs_1_) | copy-start | bytes 1179652
  89.7 10.5 %collective-permute-start.9 = (bf16[8,64,128]{2,1,0:T(8,128)(2,1)S(1)}, bf16[8,64,128]{2,1,0:T(8,128)(2,1)S(1)}, u32[]{:S(2)}, u32[]{:S(2)}) collective-permute-start(bf16[8,64,128]{2,1,0:T(8,128)(2,1)S(1)} %all_to_all.15.refs_0_), channel_id=1, source_target_pairs={{0,64},{64,0},{128,192},{192,128},{1,65},{65,1},{129,193},{193,129... | collective-permute-start | bytes 393224 | tf_op jit(solution)/shard_map/ppermute | solution.py:278

commit v3 on v2

v3 whole, which is shorter than its diff:
```python
import functools

import jax
import jax.numpy as jnp
from jax import lax
from jax.experimental import pallas as pl
from jax.experimental.pallas import tpu as pltpu
from jax.sharding import Mesh, PartitionSpec as P

F32, BF16, I32 = jnp.float32, jnp.bfloat16, jnp.int32
CAP = 48
HALF = CAP // 2
EXPERTS = 8
X, Z, Y = 4, 8, 4
NEAR, FAR = (0, 1, 3), (2,)
VMEM_LIMIT = 16 * 1024 * 1024

DP_AXES = ("x", "z")
EXPERT_AXES = ("y", "c")
BACK_AXES = ("z", "y", "c")

sds = jax.ShapeDtypeStruct
VMEM = pl.BlockSpec(memory_space=pltpu.VMEM)
HBM = pl.BlockSpec(memory_space=pltpu.HBM)
ANY = pl.BlockSpec(memory_space=pl.ANY)


def call(body, ins, outs, scratch=(), mflops=0, **kwargs):
    specs, shapes = [pair[0] for pair in outs], [pair[1] for pair in outs]
    single = len(outs) == 1
    return pl.pallas_call(
        body,
        out_shape=shapes[0] if single else shapes,
        in_specs=ins,
        out_specs=specs[0] if single else specs,
        scratch_shapes=list(scratch),
        cost_estimate=pl.CostEstimate(
            flops=mflops * 1000000, bytes_accessed=4000000, transcendentals=0
        ),
        compiler_params=pltpu.CompilerParams(vmem_limit_bytes=VMEM_LIMIT),
        **kwargs,
    )


def in_hbm(value):
    return pltpu.with_memory_space_constraint(value, pltpu.HBM)


def dma(source, target, sem):
    copy = pltpu.make_async_copy(source, target, sem)
    copy.start()
    return copy


def iota(shape, dim):
    return lax.broadcasted_iota(I32, shape, dim)


def slots_of(routes):
    first, second = routes[0:1, :], routes[1:2, :]
    tok = routes.shape[1]
    experts = iota((EXPERTS, tok), 0)
    is_first, is_second = experts == first, experts == second
    member = jnp.where(is_first | is_second, 1.0, 0.0).astype(BF16)
    before = jnp.where(iota((tok, tok), 0) < iota((tok, tok), 1), 1.0, 0.0).astype(BF16)
    count = jnp.dot(member, before, preferred_element_type=F32)
    pos_first = jnp.sum(jnp.where(is_first, count, 0.0), axis=0, keepdims=True).astype(I32)
    pos_second = jnp.sum(jnp.where(is_second, count, 0.0), axis=0, keepdims=True).astype(I32)
    return first, second, pos_first, pos_second


def gate_probs(logits):
    first = jax.nn.sigmoid(logits[0:1, :] - logits[1:2, :])
    return first, 1.0 - first


def nt_dot(rows, matrix):
    return lax.dot_general(rows, matrix, (((1,), (1,)), ((), ())), preferred_element_type=F32)


def tn_dot(rows, matrix):
    return lax.dot_general(rows, matrix, (((0,), (0,)), ((), ())), preferred_element_type=F32)


def hits(routes, count, row_of):
    first, second, pos_first, pos_second = slots_of(routes)
    rows = iota((count, routes.shape[1]), 0)
    hit = (rows == row_of(first, pos_first)) | (rows == row_of(second, pos_second))
    return jnp.where(hit, 1.0, 0.0).astype(BF16)


def pick_rows(routes, value, count, row_of, weights=None):
    first, second, pos_first, pos_second = slots_of(routes)
    rows = iota((count, value.shape[0]), 0)
    hit_first = rows == row_of(first, pos_first)
    hit_second = rows == row_of(second, pos_second)
    dispatch = jnp.where(hit_first | hit_second, 1.0, 0.0).astype(BF16)
    picked = jnp.dot(dispatch, value, preferred_element_type=F32)
    if weights is not None:
        weight = jnp.where(hit_first, weights[0], 0.0) + jnp.where(hit_second, weights[1], 0.0)
        picked = picked * jnp.sum(weight, axis=1, keepdims=True)
    return picked.astype(BF16)


def send_near_body(routes_hbm, tok_hbm, own_hbm, *refs):
    out_refs, (own_ref, routes_ref, tok_ref, sems) = refs[:-4], refs[-4:]
    get_routes = dma(routes_hbm, routes_ref, sems.at[0])
    get_tok = dma(tok_hbm, tok_ref, sems.at[1])
    y, c = lax.axis_index("y"), lax.axis_index("c")

    def row_of(expert, pos):
        chip = (expert >> 1) ^ y
        block = jnp.where(chip == 3, 2, chip) * 2 + ((expert & 1) ^ c)
        return jnp.where(chip == 2, -1, block * CAP + pos)

    get_routes.wait()
    dispatch = hits(routes_ref[...], len(NEAR) * 2 * CAP, row_of)
    get_tok.wait()
    tokens = tok_ref[...]
    put = None
    for k, ref in enumerate((own_ref, *out_refs)):
        part = dispatch[k * 2 * CAP : (k + 1) * 2 * CAP]
        ref[...] = jnp.dot(part, tokens, preferred_element_type=F32).astype(BF16)
        put = put or dma(own_ref, own_hbm, sems.at[0])
    put.wait()


def send_far_body(*refs):
    routes_refs, tok_refs, out_ref = refs[0:2], refs[2:4], refs[4]
    y, c = lax.axis_index("y"), lax.axis_index("c")

    def row_of(expert, pos):
        wanted = (((expert >> 1) ^ y) == 2) & ((expert & 1) == c)
        return jnp.where(wanted, pos, -1)

    for j in range(2):
        picked = pick_rows(routes_refs[j][...], tok_refs[j][...], CAP, row_of)
        out_ref[j * CAP : (j + 1) * CAP] = picked


def send_cot_body(*refs):
    routes_refs, logits_refs, cot_refs = refs[0:2], refs[2:4], refs[4:6]
    out_refs = refs[6:]
    y, c = lax.axis_index("y"), lax.axis_index("c")

    def row_of(expert, pos):
        return jnp.where((expert & 1) == c, ((expert >> 1) ^ y) * CAP + pos, -1)

    for j in range(2):
        probs = gate_probs(logits_refs[j][...])
        picked = pick_rows(routes_refs[j][...], cot_refs[j][...], Y * CAP, row_of, probs)
        for i, out_ref in enumerate(out_refs):
            out_ref[j * CAP : (j + 1) * CAP] = picked[i * CAP : (i + 1) * CAP]


def split_down_body(down_hbm, own_hbm, *refs):
    out_refs, (own_ref, sems) = refs[:-2], refs[-2:]
    me = lax.axis_index("x")
    width = own_ref.shape[1]
    gets = []
    for i, ref in enumerate((own_ref, *out_refs)):
        start = pl.multiple_of((me ^ i) * width, 128)
        gets.append(dma(down_hbm.at[:, pl.ds(start, width)], ref, sems.at[i]))
    gets[0].wait()
    put = dma(own_ref, own_hbm, sems.at[0])
    for get in gets[1:]:
        get.wait()
    put.wait()


def rows_of(refs):
    return jnp.concatenate([ref[...] for ref in refs], axis=0)


def forward_body(near, *refs):
    count = 2 * len(NEAR) if near else 1
    pieces, (gate_ref, up_ref) = refs[:count], refs[count : count + 2]
    if near:
        parts = [ref[(k % 2) * CAP : (k % 2 + 1) * CAP] for k, ref in enumerate(pieces)]
        pre_hbm, value_hbm, hidden_ref, rows_hbm, pre_ref, value_ref, sems, rows_ref = refs[
            count + 2 :
        ]
        rows = jnp.concatenate(parts, axis=0)
        rows_ref[...] = rows
        puts = [dma(rows_ref, rows_hbm, sems.at[2])]
    else:
        pre_hbm, value_hbm, hidden_ref, pre_ref, value_ref, sems = refs[count + 2 :]
        rows, puts = pieces[0][...], []
    pre = nt_dot(rows, gate_ref[...])
    pre_ref[...] = pre
    puts.append(dma(pre_ref, pre_hbm, sems.at[0]))
    value = nt_dot(rows, up_ref[...])
    value_ref[...] = value
    puts.append(dma(value_ref, value_hbm, sems.at[1]))
    hidden_ref[...] = (pre * jax.nn.sigmoid(pre) * value).astype(BF16)
    for put in puts:
        put.wait()


def down_body(chips, *refs):
    hidden_refs, down_refs = refs[:X], refs[X : 2 * X]
    out_hbm, out_ref, sems = refs[-3:]
    y, c = lax.axis_index("y"), lax.axis_index("c")
    total = None
    for i in range(X):
        part = jnp.dot(hidden_refs[i][...], down_refs[i][...], preferred_element_type=F32)
        total = part if total is None else total + part
    left = iota((HALF, 128), 1) < 64
    puts = []
    for k, chip in enumerate(chips):
        for j in range(2):
            own = 2 * k + j
            for m in range(Z // 2):
                cols = slice(128 * m, 128 * m + 128)
                upper = total[own * CAP : own * CAP + HALF, cols]
                lower = total[own * CAP + HALF : (own + 1) * CAP, cols]
                even = jnp.where(left, upper, pltpu.roll(lower, 64, 1))
                odd = jnp.where(left, pltpu.roll(upper, 64, 1), lower)
                out_ref[own, 2 * m] = even.astype(BF16)
                out_ref[own, 2 * m + 1] = odd.astype(BF16)
            block = 2 * (y ^ chip) + (c ^ j)
            puts.append(dma(out_ref.at[own], out_hbm.at[:, block], sems.at[own]))
    for put in puts:
        put.wait()


def combine_body(routes_ref, logits_ref, back_ref, out_ref):
    first, second, pos_first, pos_second = slots_of(routes_ref[...])
    prob_first, prob_second = gate_probs(logits_ref[...])
    tok = routes_ref.shape[1]
    total = back_ref[0:EXPERTS].astype(F32)
    for z in range(1, Z):
        total = total + back_ref[z * EXPERTS : (z + 1) * EXPERTS].astype(F32)
    held = total.astype(BF16).reshape(EXPERTS * HALF, 128)
    rows = iota((EXPERTS * HALF, tok), 0)

    def pick(expert, pos):
        base = expert * HALF + pos
        in_upper = jnp.where((rows == base) & (pos < HALF), 1.0, 0.0).astype(BF16)
        in_lower = jnp.where((rows == base - HALF) & (pos >= HALF), 1.0, 0.0).astype(BF16)
        return tn_dot(held, in_upper)[0:64] + tn_dot(held, in_lower)[64:128]

    mixed = prob_first * pick(first, pos_first) + prob_second * pick(second, pos_second)
    mixed = mixed.astype(BF16)
    for z in range(Z):
        out_ref[z] = mixed


def turn_body(*refs):
    out_ref = refs[-1]
    me = lax.axis_index("x")
    for i, ref in enumerate(refs[:-1]):
        rows = ref.shape[0] * ref.shape[1]
        block = ref[...].reshape(rows, ref.shape[2])
        for m in range(rows // 128):
            start = pl.multiple_of((me ^ i) * rows + 128 * m, 128)
            out_ref[:, pl.ds(start, 128)] = block[128 * m : 128 * m + 128].T


def tangent_body(*refs):
    piece_refs, pre_refs, value_refs = refs[0:2], refs[2:4], refs[4:6]
    gate_dir_ref, up_dir_ref, *out_refs = refs[6:]
    by_tq_gate_ref, by_q_gate_ref, by_tq_up_ref, by_q_up_ref, hidden_tang_ref = out_refs
    rows = rows_of(piece_refs)
    tang_gate = nt_dot(rows, gate_dir_ref[...])
    tang_up = nt_dot(rows, up_dir_ref[...])
    pre, value = rows_of(pre_refs), rows_of(value_refs)
    sig = jax.nn.sigmoid(pre)
    slope_one = sig * (1.0 + pre * (1.0 - sig))
    slope_two = sig * (1.0 - sig) * (2.0 + pre * (1.0 - 2.0 * sig))
    silu = pre * sig
    silu_tang = slope_one * tang_gate
    by_tq_gate_ref[...] = value * slope_one
    by_q_gate_ref[...] = tang_up * slope_one + value * slope_two * tang_gate
    by_tq_up_ref[...] = silu
    by_q_up_ref[...] = silu_tang
    hidden_tang_ref[...] = (silu_tang * value + silu * tang_up).astype(BF16)


def residual_body(down_ref, down_dir_ref, *refs):
    by_tq_gate_ref, by_q_gate_ref, by_tq_up_ref, by_q_up_ref = refs[Y : Y + 4]
    resid_gate_ref, resid_up_ref = refs[Y + 4 :]
    rows = rows_of(refs[:Y])
    back_grad = nt_dot(rows, down_ref[...])
    back_tang = nt_dot(rows, down_dir_ref[...])
    resid_gate = back_tang * by_tq_gate_ref[...] + back_grad * by_q_gate_ref[...]
    resid_up = back_tang * by_tq_up_ref[...] + back_grad * by_q_up_ref[...]
    resid_gate_ref[...] = resid_gate.astype(BF16)
    resid_up_ref[...] = resid_up.astype(BF16)


def outer_body(gate_units_ref, up_units_ref, down_units_ref, *refs):
    x_refs, c_refs = refs[:2], refs[2 : 2 + Y]
    outs, holds, sems = refs[-7:-4], refs[-4:-1], refs[-1]
    step = x_refs[0].shape[1] // 4
    puts = []
    units = [ref[...].T for ref in (gate_units_ref, up_units_ref, down_units_ref)]
    for g in range(4):
        cols = slice(g * step, (g + 1) * step)
        x_rows = jnp.concatenate([ref[:, cols] for ref in x_refs], axis=0)
        c_rows = jnp.concatenate([ref[:, cols] for ref in c_refs], axis=0)
        for k, rows in enumerate((x_rows, x_rows, c_rows)):
            holds[k][0, :, cols] = jnp.dot(units[k], rows, preferred_element_type=F32)
            where = pl.ds(g * step, step)
            puts.append(
                dma(holds[k].at[:, :, where], outs[k].at[:, :, where], sems.at[3 * g + k])
            )
    for put in puts:
        put.wait()


def spread(pieces, axes):
    arrived = [pieces[0]]
    for i in range(1, len(pieces)):
        pairs = [(d, d ^ i) for d in range(len(pieces))]
        arrived.append(lax.ppermute(pieces[i], axes, pairs))
    return arrived


def exchange(value, axes):
    return lax.all_to_all(value, axes, 0, 0, tiled=True)


def shards(
    tokens,
    cotangent,
    router_logits,
    routes,
    gate_weight,
    up_weight,
    down_weight,
    dir_gate,
    dir_up,
    dir_down,
):
    tok, width = tokens.shape
    rows = EXPERTS * CAP
    units = gate_weight.shape[1]
    quarter = width // X
    routes_t, logits_t = routes.T, router_logits.T
    down_mat = down_weight[0]
    gate_dir, up_dir, down_dir = dir_gate[0], dir_up[0], dir_down[0]
    dma_sems = pltpu.SemaphoreType.DMA

    def pair(value):
        own, other = spread([value] * 2, "c")
        return in_hbm(own), other

    piece = (VMEM, pltpu.HBM((2 * CAP, width), BF16))
    leaves = (VMEM, sds((2 * CAP, width), BF16))
    send_near = call(
        send_near_body,
        [HBM, HBM],
        [(HBM, pltpu.HBM((2 * CAP, width), BF16))]
        + [(VMEM, sds((2 * CAP, width), BF16))] * (len(NEAR) - 1),
        [
            pltpu.VMEM((2 * CAP, width), BF16),
            pltpu.VMEM((2, tok), I32),
            pltpu.VMEM((tok, width), BF16),
            dma_sems((2,)),
        ],
        mflops=200,
    )(in_hbm(routes_t), in_hbm(tokens))
    near_pieces = []
    for i, value in zip(NEAR, send_near):
        if i:
            value = lax.ppermute(value, "y", [(d, d ^ i) for d in range(Y)])
        near_pieces += spread([value] * 2, "c")
    routes_two = pair(routes_t)
    tok_two = pair(tokens)
    send_far = call(send_far_body, [VMEM] * 4, [leaves], mflops=100)(*routes_two, *tok_two)
    far_piece = lax.ppermute(send_far, "y", [(d, d ^ 2) for d in range(Y)])

    send_down = call(
        split_down_body,
        [HBM],
        [(HBM, pltpu.HBM((units, quarter), BF16))]
        + [(VMEM, sds((units, quarter), BF16))] * (X - 1),
        [pltpu.VMEM((units, quarter), BF16), dma_sems((X,))],
        mflops=200,
    )(in_hbm(down_mat))
    down_parts = spread(send_down, "x")
    logits_two = pair(logits_t)
    cot_two = pair(cotangent)
    send_c = call(
        send_cot_body, [VMEM] * 6, [piece] * Y, mflops=400
    )(*routes_two, *logits_two, *cot_two)
    c_pieces = spread(send_c, "y")

    def forward(pieces, near):
        slots = len(pieces) * (CAP if near else 2 * CAP)
        extra = [(HBM, pltpu.HBM((slots, width), BF16))] if near else []
        return call(
            functools.partial(forward_body, near),
            [VMEM] * (len(pieces) + 2),
            [(HBM, pltpu.HBM((slots, units), F32))] * 2
            + [(VMEM, sds((slots, units), BF16))]
            + extra,
            [pltpu.VMEM((slots, units), F32)] * 2
            + [dma_sems((3,))]
            + ([pltpu.VMEM((slots, width), BF16)] if near else []),
            mflops=2 * slots,
        )(*pieces, gate_weight[0], up_weight[0])

    def down(chips, hidden_parts, filled=None):
        extra = [] if filled is None else [in_hbm(filled)]
        return call(
            functools.partial(down_body, chips),
            [VMEM] * (2 * X) + [HBM] * len(extra),
            [(HBM, pltpu.HBM((Z, EXPERTS, HALF, 128), BF16))],
            [
                pltpu.VMEM((2 * len(chips), Z, HALF, 128), BF16),
                dma_sems((2 * len(chips),)),
            ],
            mflops=88 * len(chips),
            input_output_aliases={2 * X: 0} if extra else {},
        )(*hidden_parts, *down_parts, *extra)

    pre_near, value_near, hidden_near, near_rows = forward(near_pieces, True)
    near_parts = spread([hidden_near] * X, "x")
    pre_far, value_far, hidden_far = forward([far_piece], False)
    far_parts = spread([hidden_far] * X, "x")
    filled = down(NEAR, near_parts)
    partial_out = down(FAR, far_parts, filled)

    back = exchange(partial_out.reshape(Z * EXPERTS, HALF, 128), BACK_AXES)
    x_rows = (near_rows, far_piece)
    ordered_c = [c_pieces[i] for i in NEAR + FAR]
    factor = (VMEM, pltpu.HBM((rows, units), F32))
    half_factor = (VMEM, pltpu.HBM((rows, units), BF16))
    *factors, hidden_tang = call(
        tangent_body, [VMEM] * 8, [factor] * 4 + [half_factor], mflops=704
    )(
        *[
            in_hbm(v)
            for v in (*x_rows, pre_near, pre_far, value_near, value_far, gate_dir, up_dir)
        ]
    )
    share = call(
        combine_body, [VMEM] * 3, [(VMEM, pltpu.HBM((Z, 64, tok), BF16))], mflops=100
    )(routes_t, logits_t, back)
    over_z = exchange(share, "z")
    blocks = spread([over_z] * X, "x")
    mixed = call(turn_body, [VMEM] * X, [(VMEM, sds((tok, width), BF16))], mflops=100)(*blocks)

    resid_gate, resid_up = call(
        residual_body, [VMEM] * (2 + Y + 4), [half_factor] * 2, mflops=704
    )(*[in_hbm(v) for v in (down_mat, down_dir, *ordered_c, *factors)])
    hold = pltpu.VMEM((1, units, width), F32)
    out = (HBM, pltpu.HBM((1, units, width), F32))
    hvp = call(
        outer_body, [VMEM] * (5 + Y), [out] * 3, [hold] * 3 + [dma_sems((12,))], mflops=1056
    )(*[in_hbm(v) for v in (resid_gate, resid_up, hidden_tang, *x_rows, *ordered_c)])
    return (mixed, *hvp)


def solution(mesh):
    grid = Mesh(mesh.devices.reshape(X, Z, Y, 2), ("x", "z", "y", "c"))
    by_expert = P(EXPERT_AXES, None)
    by_both = P(EXPERT_AXES, DP_AXES, None)

    def step(*args):
        return shards(*args)

    step = jax.shard_map(
        step,
        mesh=grid,
        in_specs=(by_expert,) * 4 + (by_both,) * 6,
        out_specs=(by_expert,) + (by_both,) * 3,
        check_vma=False,
    )
    return step
```

time: 103 us -> 109 us (1.058)
  blocking collectives: 13 us -> 0 us
  starting transfers between devices: 33.1 us -> 41.6 us
  waiting for transfers between devices: 26.1 us -> 34.1 us
    all_to_all x1 -> x0, blocking collectives: 13 us -> none  [exchange(): return lax.all_to_all(value, axes, 0, 0, tiled=True)]
    ppermute x0 -> x3, waiting for transfers between devices: none -> 10.1 us  [the longest x2 10.1 us: shards(): value = lax.ppermute(value, 'y', [(d, d ^ i) for d in range(Y)])]
    all_to_all x2, waiting for transfers between devices: 16.6 us -> 7.89 us  [exchange(): return lax.all_to_all(value, axes, 0, 0, tiled=True)]
    ppermute x15 -> x22, waiting for transfers between devices: 9.48 us -> 16.1 us  [spread(): arrived.append(lax.ppermute(pieces[i], axes, pairs))]
    ppermute x0 -> x3, starting transfers between devices: none -> 5.62 us  [the longest x2 3.84 us: shards(): value = lax.ppermute(value, 'y', [(d, d ^ i) for d in range(Y)])]
    all_to_all x2, starting transfers between devices: 14.4 us -> 15.9 us  [exchange(): return lax.all_to_all(value, axes, 0, 0, tiled=True)]
    ppermute x15 -> x22, starting transfers between devices: 18.8 us -> 20.1 us  [spread(): arrived.append(lax.ppermute(pieces[i], axes, pairs))]
    pallas_call x10 -> x13, Pallas kernels: 28.6 us -> 29.6 us  [the longest x1 4.87 us: shards(): call(outer_body, [VMEM] * (5 + Y), [out] * 3, [hold] * 3 + [dma_sems((12,...]
  transfers between devices with their start and end apart: 17 -> 27, of which waited for: 5 -> 12; matrix products, arithmetic and copies ran while one was open for 0% -> 0% of each run, Pallas kernels for 21% -> 26%
where the time goes in v3:
time: 109 us; the launch traced here: 107 us
  starting transfers between devices  41.6 us (38%)
  waiting for transfers between devices  34.1 us (31%)
  Pallas kernels  29.6 us (27%)
    ppermute x22, starting transfers between devices, spread(): arrived.append(lax.ppermute(pieces[i], axes, pairs))  20.1 us
    ppermute x22, waiting for transfers between devices, spread(): arrived.append(lax.ppermute(pieces[i], axes, pairs))  16.1 us
    all_to_all x2, starting transfers between devices, exchange(): return lax.all_to_all(value, axes, 0, 0, tiled=True)  15.9 us
    ppermute x2, waiting for transfers between devices, shards(): value = lax.ppermute(value, 'y', [(d, d ^ i) for d in range(Y)])  10.1 us
    all_to_all x2, waiting for transfers between devices, exchange(): return lax.all_to_all(value, axes, 0, 0, tiled=True)  7.89 us
    pallas_call x1, Pallas kernels, shards(): call(outer_body, [VMEM] * (5 + Y), [out] * 3, [hold] * 3 + [dma_sems((12,...  4.87 us
    pallas_call x1, Pallas kernels, shards(): call(tangent_body, [VMEM] * 8, [factor] * 4 + [half_factor], mflops=704)  4.53 us
    pallas_call x1, Pallas kernels, shards(): call(residual_body, [VMEM] * (2 + Y + 4), [half_factor] * 2, mflops=704)  4.14 us
  transfers between devices with their start and end apart: 27, of which 12 were waited for; matrix products, arithmetic and copies ran while one was open for 0% of the time, Pallas kernels for 26%

profile of v3, /device:TPU:32, one launch (start us, length us, event | category | flops | bytes accessed | tf_op | source)
XLA Modules:
  0.0 107.2 jit_solution(4285234236446000479)
XLA Ops:
  0.7 0.1 collective-permute-start.1
  0.8 2.2 %shard_map.132 = (bf16[96,2048]{1,0:T(8,128)(2,1)}, bf16[96,2048]{1,0:T(8,128)(2,1)S(1)}, bf16[96,2048]{1,0:T(8,128)(2,1)S(1)}) custom-call(s32[2,128]{1,0:T(2,128)} %bitcast.13, bf16[128,2048]{1,0:T(8,128)(2,1)} %tok_hbm.1), custom_call_target="tpu_custom_call" | custom-call | flops 200000000 | bytes 4000000 | tf_op jit(solution)/shard_map/pallas_call | solution.py:351
  3.0 0.0 copy-start.4
  3.0 1.7 %collective-permute-start.10 = (bf16[96,2048]{1,0:T(8,128)(2,1)S(1)}, bf16[96,2048]{1,0:T(8,128)(2,1)S(1)}, u32[]{:S(2)}, u32[]{:S(2)}) collective-permute-start(bf16[96,2048]{1,0:T(8,128)(2,1)S(1)} %get-tuple-element.38), channel_id=1, source_target_pairs={{0,2},{2,0},{4,6},{6,4},{1,3},{3,1},{5,7},{7,5},{8,10},{10,8},{12,... | collective-permute-start | bytes 1179656 | tf_op jit(solution)/shard_map/ppermute | solution.py:367
  4.6 2.2 %collective-permute-start.12 = (bf16[96,2048]{1,0:T(8,128)(2,1)S(1)}, bf16[96,2048]{1,0:T(8,128)(2,1)S(1)}, u32[]{:S(2)}, u32[]{:S(2)}) collective-permute-start(bf16[96,2048]{1,0:T(8,128)(2,1)S(1)} %get-tuple-element.39), channel_id=1, source_target_pairs={{0,6},{2,4},{4,2},{6,0},{1,7},{3,5},{5,3},{7,1},{8,14},{10,12},{12... | collective-permute-start | bytes 1179656 | tf_op jit(solution)/shard_map/ppermute | solution.py:367
  6.8 0.0 collective-permute-start.9
  6.8 7.6 %collective-permute-done.10.refs_2_ = bf16[96,2048]{1,0:T(8,128)(2,1)S(1)} collective-permute-done((bf16[96,2048]{1,0:T(8,128)(2,1)S(1)}, bf16[96,2048]{1,0:T(8,128)(2,1)S(1)}, u32[]{:S(2)}, u32[]{:S(2)}) %collective-permute-start.10) | collective-permute-done | bytes 393248 | tf_op jit(solution)/shard_map/ppermute | solution.py:367
  14.5 0.0 collective-permute-start.11
  14.5 2.5 %collective-permute-done.12.refs_4_ = bf16[96,2048]{1,0:T(8,128)(2,1)S(1)} collective-permute-done((bf16[96,2048]{1,0:T(8,128)(2,1)S(1)}, bf16[96,2048]{1,0:T(8,128)(2,1)S(1)}, u32[]{:S(2)}, u32[]{:S(2)}) %collective-permute-start.12) | collective-permute-done | bytes 393248 | tf_op jit(solution)/shard_map/ppermute | solution.py:367
  17.0 0.5 collective-permute-start
  17.5 1.2 %collective-permute-done.refs_1_ = s32[2,128]{1,0:T(2,128)S(1)} collective-permute-done((s32[2,128]{1,0:T(2,128)}, s32[2,128]{1,0:T(2,128)S(1)}, u32[]{:S(2)}, u32[]{:S(2)}) %collective-permute-start) | collective-permute-done | bytes 1056 | tf_op jit(solution)/shard_map/ppermute | solution.py:316
  18.7 1.6 %shard_map.129 = bf16[96,2048]{1,0:T(8,128)(2,1)S(1)} custom-call(s32[2,128]{1,0:T(2,128)} %bitcast.15, s32[2,128]{1,0:T(2,128)S(1)} %collective-permute-done.refs_1_, bf16[128,2048]{1,0:T(8,128)(2,1)} %tok_hbm.1, bf16[128,2048]{1,0:T(8,128)(2,1)S(1)} %collective-permute-done.1.refs_3_), custom_call_target="tpu_custom_call" | custom-call | flops 100000000 | bytes 4000000 | tf_op jit(solution)/shard_map/pallas_call | solution.py:371
  20.3 1.8 %collective-permute-start.2 = (bf16[96,2048]{1,0:T(8,128)(2,1)S(1)}, bf16[96,2048]{1,0:T(8,128)(2,1)S(1)}, u32[]{:S(2)}, u32[]{:S(2)}) collective-permute-start(bf16[96,2048]{1,0:T(8,128)(2,1)S(1)} %shard_map.129), channel_id=1, source_target_pairs={{0,4},{2,6},{4,0},{6,2},{1,5},{3,7},{5,1},{7,3},{8,12},{10,14},{12... | collective-permute-start | bytes 1179656 | tf_op jit(solution)/shard_map/ppermute | solution.py:372
  22.1 1.7 %shard_map.131 = (bf16[224,512]{1,0:T(8,128)(2,1)}, bf16[224,512]{1,0:T(8,128)(2,1)S(1)}, bf16[224,512]{1,0:T(8,128)(2,1)S(1)}, bf16[224,512]{1,0:T(8,128)(2,1)S(1)}) custom-call(bf16[224,2048]{1,0:T(8,128)(2,1)} %bitcast.21), custom_call_target="tpu_custom_call" | custom-call | flops 200000000 | bytes 4000000 | tf_op jit(solution)/shard_map/pallas_call | solution.py:374
  23.7 1.6 %collective-permute-start.6 = (bf16[224,512]{1,0:T(8,128)(2,1)S(1)}, bf16[224,512]{1,0:T(8,128)(2,1)S(1)}, u32[]{:S(2)}, u32[]{:S(2)}) collective-permute-start(bf16[224,512]{1,0:T(8,128)(2,1)S(1)} %get-tuple-element.34), channel_id=1, source_target_pairs={{0,64},{64,0},{128,192},{192,128},{1,65},{65,1},{129,193},{193,129... | collective-permute-start | bytes 688136 | tf_op jit(solution)/shard_map/ppermute | solution.py:316
  25.3 0.0 collective-permute-done.9.refs_1_
  25.3 2.7 %collective-permute-start.7 = (bf16[224,512]{1,0:T(8,128)(2,1)S(1)}, bf16[224,512]{1,0:T(8,128)(2,1)S(1)}, u32[]{:S(2)}, u32[]{:S(2)}) collective-permute-start(bf16[224,512]{1,0:T(8,128)(2,1)S(1)} %get-tuple-element.35), channel_id=1, source_target_pairs={{0,128},{64,192},{128,0},{192,64},{1,129},{65,193},{129,1},{193,65... | collective-permute-start | bytes 688136 | tf_op jit(solution)/shard_map/ppermute | solution.py:316
  28.1 0.5 collective-permute-start.8
  28.5 0.0 collective-permute-done.13.refs_5_
  28.6 1.9 %shard_map.133 = (f32[288,224]{1,0:T(8,128)}, f32[288,224]{1,0:T(8,128)}, bf16[288,224]{1,0:T(8,128)(2,1)S(1)}, bf16[288,2048]{1,0:T(8,128)(2,1)}) custom-call(bf16[96,2048]{1,0:T(8,128)(2,1)S(1)} %copy-done.4, bf16[96,2048]{1,0:T(8,128)(2,1)S(1)} %collective-permute-done.9.refs_1_, bf16[96,2048]{1,0:T(8,128)(2,1)S(1)} %collective-permute-done.10.refs_2_, ...), custom_call_target="tpu_custom_call" | custom-call | flops 576000000 | bytes 4000000 | tf_op jit(solution)/shard_map/pallas_call | solution.py:393
  30.5 0.0 copy-start.3
  30.5 0.4 collective-permute-start.14
  30.9 1.4 %collective-permute-done.6.refs_5_ = bf16[224,512]{1,0:T(8,128)(2,1)S(1)} collective-permute-done((bf16[224,512]{1,0:T(8,128)(2,1)S(1)}, bf16[224,512]{1,0:T(8,128)(2,1)S(1)}, u32[]{:S(2)}, u32[]{:S(2)}) %collective-permute-start.6) | collective-permute-done | bytes 229408 | tf_op jit(solution)/shard_map/ppermute | solution.py:316
  32.3 3.0 %collective-permute-start.15 = (bf16[288,224]{1,0:T(8,128)(2,1)S(1)}, bf16[288,224]{1,0:T(8,128)(2,1)S(1)}, u32[]{:S(2)}, u32[]{:S(2)}) collective-permute-start(bf16[288,224]{1,0:T(8,128)(2,1)S(1)} %get-tuple-element.40.refs_0_), channel_id=1, source_target_pairs={{0,128},{64,192},{128,0},{192,64},{1,129},{65,193},{129,1},{193,65... | collective-permute-start | bytes 387080 | tf_op jit(solution)/shard_map/ppermute | solution.py:316
  35.3 1.1 %collective-permute-start.16 = (bf16[288,224]{1,0:T(8,128)(2,1)S(1)}, bf16[288,224]{1,0:T(8,128)(2,1)S(1)}, u32[]{:S(2)}, u32[]{:S(2)}) collective-permute-start(bf16[288,224]{1,0:T(8,128)(2,1)S(1)} %get-tuple-element.40.refs_0_), channel_id=1, source_target_pairs={{0,192},{64,128},{128,64},{192,0},{1,193},{65,129},{129,65},{193,1... | collective-permute-start | bytes 387080 | tf_op jit(solution)/shard_map/ppermute | solution.py:316
  36.5 1.4 %shard_map.130 = (f32[96,224]{1,0:T(8,128)}, f32[96,224]{1,0:T(8,128)}, bf16[96,224]{1,0:T(8,128)(2,1)S(1)}) custom-call(bf16[96,2048]{1,0:T(8,128)(2,1)S(1)} %collective-permute-done.2.refs_0_.refs_1_, bf16[224,2048]{1,0:T(8,128)(2,1)S(1)} %bitcast.10, bf16[224,2048]{1,0:T(8,128)(2,1)S(1)} %bitcast.12), custom_call_target="tpu_custom_call" | custom-call | flops 192000000 | bytes 4000000 | tf_op jit(solution)/shard_map/pallas_call | solution.py:393
  37.9 1.6 %collective-permute-done.7.refs_6_ = bf16[224,512]{1,0:T(8,128)(2,1)S(1)} collective-permute-done((bf16[224,512]{1,0:T(8,128)(2,1)S(1)}, bf16[224,512]{1,0:T(8,128)(2,1)S(1)}, u32[]{:S(2)}, u32[]{:S(2)}) %collective-permute-start.7) | collective-permute-done | bytes 229408 | tf_op jit(solution)/shard_map/ppermute | solution.py:316
  39.5 0.2 collective-permute-start.3
  39.7 6.4 %collective-permute-done.8.refs_7_ = bf16[224,512]{1,0:T(8,128)(2,1)S(1)} collective-permute-done((bf16[224,512]{1,0:T(8,128)(2,1)S(1)}, bf16[224,512]{1,0:T(8,128)(2,1)S(1)}, u32[]{:S(2)}, u32[]{:S(2)}) %collective-permute-start.8) | collective-permute-done | bytes 229408 | tf_op jit(solution)/shard_map/ppermute | solution.py:316
  46.1 0.5 collective-permute-start.5
  46.6 0.0 collective-permute-done.15.refs_2_
  46.6 1.8 %collective-permute-done.16.refs_3_ = bf16[288,224]{1,0:T(8,128)(2,1)S(1)} collective-permute-done((bf16[288,224]{1,0:T(8,128)(2,1)S(1)}, bf16[288,224]{1,0:T(8,128)(2,1)S(1)}, u32[]{:S(2)}, u32[]{:S(2)}) %collective-permute-start.16) | collective-permute-done | bytes 129056 | tf_op jit(solution)/shard_map/ppermute | solution.py:316
  48.4 1.2 %shard_map.134.refs_8_ = bf16[8,8,24,128]{3,2,1,0:T(8,128)(2,1)} custom-call(bf16[288,224]{1,0:T(8,128)(2,1)S(1)} %get-tuple-element.40.refs_0_, bf16[288,224]{1,0:T(8,128)(2,1)S(1)} %collective-permute-done.14.refs_1_, bf16[288,224]{1,0:T(8,128)(2,1)S(1)} %collective-permute-done.15.refs_2_, bf16[288,224]{1,0:T(8,128)(2,1)S(1)} %collective-permute-done.16.refs_3_, ...), custom_call_target="tpu_custom_call" | custom-call | flops 264000000 | bytes 4000000 | tf_op jit(solution)/shard_map/pallas_call | solution.py:407
  49.6 0.0 copy-start.5
  49.7 0.0 copy-start.7
  49.7 0.0 collective-permute-done.3.refs_1_
  49.7 2.1 %collective-permute-done.4.refs_2_ = bf16[96,224]{1,0:T(8,128)(2,1)S(1)} collective-permute-done((bf16[96,224]{1,0:T(8,128)(2,1)S(1)}, bf16[96,224]{1,0:T(8,128)(2,1)S(1)}, u32[]{:S(2)}, u32[]{:S(2)}) %collective-permute-start.4) | collective-permute-done | bytes 43040 | tf_op jit(solution)/shard_map/ppermute | solution.py:316
  51.8 0.1 collective-permute-done.5.refs_3_
  51.9 1.0 shard_map.135
  53.0 10.6 %all-to-all-start = ((bf16[64,24,128]{2,1,0:T(8,128)(2,1)}), bf16[64,24,128]{2,1,0:T(8,128)(2,1)S(1)}, u32[]{:S(2)}, u32[]{:S(2)}) async-start(bf16[64,24,128]{2,1,0:T(8,128)(2,1)} %bitcast.23), calls=%async_computation | async-start | bytes 786432 | tf_op jit(solution)/shard_map/all_to_all | solution.py:321
  63.6 0.2 collective-permute-start.21
  63.8 0.4 collective-permute-start.20
  64.2 1.4 %collective-permute-done.20.refs_3_ = f32[2,128]{1,0:T(2,128)S(1)} collective-permute-done((f32[2,128]{1,0:T(2,128)S(1)}, f32[2,128]{1,0:T(2,128)S(1)}, u32[]{:S(2)}, u32[]{:S(2)}) %collective-permute-start.20) | collective-permute-done | bytes 1056 | tf_op jit(solution)/shard_map/ppermute | solution.py:316
  65.6 0.0 collective-permute-done.21.refs_5_
  65.6 3.0 %shard_map.138 = (bf16[96,2048]{1,0:T(8,128)(2,1)}, bf16[96,2048]{1,0:T(8,128)(2,1)}, bf16[96,2048]{1,0:T(8,128)(2,1)}, bf16[96,2048]{1,0:T(8,128)(2,1)}) custom-call(s32[2,128]{1,0:T(2,128)} %bitcast.16, s32[2,128]{1,0:T(2,128)S(1)} %collective-permute-done.refs_1_, f32[2,128]{1,0:T(2,128)} %bitcast.18, f32[2,128]{1,0:T(2,128)S(1)} %collective-permute-done.20.refs_3_, ...), custom_call_target="tpu_custom_call" | custom-call | flops 400000000 | bytes 4000000 | tf_op jit(solution)/shard_map/pallas_call | solution.py:385
  68.6 1.5 %collective-permute-start.22 = (bf16[96,2048]{1,0:T(8,128)(2,1)}, bf16[96,2048]{1,0:T(8,128)(2,1)S(1)}, u32[]{:S(2)}, u32[]{:S(2)}) collective-permute-start(bf16[96,2048]{1,0:T(8,128)(2,1)} %get-tuple-element.42), channel_id=1, source_target_pairs={{0,2},{2,0},{4,6},{6,4},{1,3},{3,1},{5,7},{7,5},{8,10},{10,8},{12,... | collective-permute-start | bytes 1179656 | tf_op jit(solution)/shard_map/ppermute | solution.py:316
  70.1 2.1 %collective-permute-start.23 = (bf16[96,2048]{1,0:T(8,128)(2,1)}, bf16[96,2048]{1,0:T(8,128)(2,1)S(1)}, u32[]{:S(2)}, u32[]{:S(2)}) collective-permute-start(bf16[96,2048]{1,0:T(8,128)(2,1)} %get-tuple-element.43), channel_id=1, source_target_pairs={{0,6},{2,4},{4,2},{6,0},{1,7},{3,5},{5,3},{7,1},{8,14},{10,12},{12... | collective-permute-start | bytes 1179656 | tf_op jit(solution)/shard_map/ppermute | solution.py:316
  72.1 0.6 collective-permute-start.24
  72.7 5.0 %all-to-all-done.back_ref = bf16[64,24,128]{2,1,0:T(8,128)(2,1)S(1)} async-done(((bf16[64,24,128]{2,1,0:T(8,128)(2,1)}), bf16[64,24,128]{2,1,0:T(8,128)(2,1)S(1)}, u32[]{:S(2)}, u32[]{:S(2)}) %all-to-all-start) | async-done | bytes 393248 | tf_op jit(solution)/shard_map/all_to_all | solution.py:321
  77.7 1.0 shard_map.136
  78.7 5.3 %all-to-all-start.1 = ((bf16[8,64,128]{2,1,0:T(8,128)(2,1)}), bf16[8,64,128]{2,1,0:T(8,128)(2,1)S(1)}, u32[]{:S(2)}, u32[]{:S(2)}) async-start(bf16[8,64,128]{2,1,0:T(8,128)(2,1)} %shard_map.136), calls=%async_computation.1 | async-start | bytes 262144 | tf_op jit(solution)/shard_map/all_to_all | solution.py:321
  84.1 4.5 %shard_map.139 = (f32[384,224]{1,0:T(8,128)}, f32[384,224]{1,0:T(8,128)}, f32[384,224]{1,0:T(8,128)}, f32[384,224]{1,0:T(8,128)}, bf16[384,224]{1,0:T(8,128)(2,1)}) custom-call(bf16[288,2048]{1,0:T(8,128)(2,1)} %get-tuple-element.45.refs_0_, bf16[96,2048]{1,0:T(8,128)(2,1)} %copy-done.2, f32[288,224]{1,0:T(8,128)} %get-tuple-element.46.refs_2_, ...), custom_call_target="tpu_custom_call" | custom-call | flops 704000000 | bytes 4000000 | tf_op jit(solution)/shard_map/pallas_call | solution.py:431
  88.6 2.9 %all-to-all-done.1.refs_0_ = bf16[8,64,128]{2,1,0:T(8,128)(2,1)S(1)} async-done(((bf16[8,64,128]{2,1,0:T(8,128)(2,1)}), bf16[8,64,128]{2,1,0:T(8,128)(2,1)S(1)}, u32[]{:S(2)}, u32[]{:S(2)}) %all-to-all-start.1) | async-done | bytes 131104 | tf_op jit(solution)/shard_map/all_to_all | solution.py:321
  91.5 0.0 collective-permute-start.17
  91.5 1.9 %collective-permute-start.18 = (bf16[8,64,128]{2,1,0:T(8,128)(2,1)S(1)}, bf16[8,64,128]{2,1,0:T(8,128)(2,1)S(1)}, u32[]{:S(2)}, u32[]{:S(2)}) collective-permute-start(bf16[8,64,128]{2,1,0:T(8,128)(2,1)S(1)} %all-to-all-done.1.refs_0_), channel_id=1, source_target_pairs={{0,128},{64,192},{128,0},{192,64},{1,129},{65,193},{129,1},{193,65... | collective-permute-start | bytes 393224 | tf_op jit(solution)/shard_map/ppermute | solution.py:316
  93.5 2.8 %collective-permute-start.19 = (bf16[8,64,128]{2,1,0:T(8,128)(2,1)S(1)}, bf16[8,64,128]{2,1,0:T(8,128)(2,1)S(1)}, u32[]{:S(2)}, u32[]{:S(2)}) collective-permute-start(bf16[8,64,128]{2,1,0:T(8,128)(2,1)S(1)} %all-to-all-done.1.refs_0_), channel_id=1, source_target_pairs={{0,192},{64,128},{128,64},{192,0},{1,193},{65,129},{129,65},{193,1... | collective-permute-start | bytes 393224 | tf_op jit(solution)/shard_map/ppermute | solution.py:316
  96.2 0.0 collective-permute-done.24.refs_3_.refs_5_
  96.2 0.7 copy-done.9
  97.0 0.1 copy-done.10
  97.1 4.1 %shard_map.140 = (bf16[384,224]{1,0:T(8,128)(2,1)}, bf16[384,224]{1,0:T(8,128)(2,1)}) custom-call(bf16[224,2048]{1,0:T(8,128)(2,1)} %bitcast.22, bf16[224,2048]{1,0:T(8,128)(2,1)} %bitcast.24, bf16[96,2048]{1,0:T(8,128)(2,1)} %get-tuple-element.41.refs_0_.refs_2_, bf16[96,2048]{1,0:T(8,128)(2,1)} %copy-done.8, bf16[96,2048]{1,0:T(8,128)(2,1)} %copy-done.9, ...), custom_call_target="tpu_custom_call" | custom-call | flops 704000000 | bytes 4000000 | tf_op jit(solution)/shard_map/pallas_call | solution.py:446
  101.2 4.9 %shard_map.141 = (f32[1,224,2048]{2,1,0:T(8,128)}, f32[1,224,2048]{2,1,0:T(8,128)}, f32[1,224,2048]{2,1,0:T(8,128)}) custom-call(bf16[384,224]{1,0:T(8,128)(2,1)} %get-tuple-element.54.gate_units_ref, bf16[384,224]{1,0:T(8,128)(2,1)} %get-tuple-element.55.up_units_ref, bf16[384,224]{1,0:T(8,128)(2,1)} %get-tuple-element.56.down_units_ref, ...), custom_call_target="tpu_custom_call" | custom-call | flops 1056000000 | bytes 4000000 | tf_op jit(solution)/shard_map/pallas_call | solution.py:451
  106.1 0.0 collective-permute-done.18.refs_2_
  106.1 0.0 collective-permute-done.19.refs_3_
  106.2 1.0 shard_map.137
  (27 shorter events, 0.1 us)
Async XLA Ops:
  0.6 27.9 %copy-start = (bf16[1,224,2048]{2,1,0:T(8,128)(2,1)S(1)}, bf16[1,224,2048]{2,1,0:T(8,128)(2,1)}, u32[]{:S(2)}) copy-start(bf16[1,224,2048]{2,1,0:T(8,128)(2,1)} %param.14) | copy-start | bytes 2752516
  0.6 27.9 %copy-start.1 = (bf16[1,224,2048]{2,1,0:T(8,128)(2,1)S(1)}, bf16[1,224,2048]{2,1,0:T(8,128)(2,1)}, u32[]{:S(2)}) copy-start(bf16[1,224,2048]{2,1,0:T(8,128)(2,1)} %param.15) | copy-start | bytes 2752516
  0.7 18.0 %collective-permute-start.1 = (bf16[128,2048]{1,0:T(8,128)(2,1)}, bf16[128,2048]{1,0:T(8,128)(2,1)S(1)}, u32[]{:S(2)}, u32[]{:S(2)}) collective-permute-start(bf16[128,2048]{1,0:T(8,128)(2,1)} %tok_hbm.1), channel_id=1, source_target_pairs={{0,1},{1,0},{2,3},{3,2},{4,5},{5,4},{6,7},{7,6},{8,9},{9,8},{10,11... | collective-permute-start | bytes 1572872 | tf_op jit(solution)/shard_map/ppermute | solution.py:316
  3.0 25.6 %copy-start.4 = (bf16[96,2048]{1,0:T(8,128)(2,1)S(1)}, bf16[96,2048]{1,0:T(8,128)(2,1)}, u32[]{:S(2)}) copy-start(bf16[96,2048]{1,0:T(8,128)(2,1)} %get-tuple-element.37.refs_0_) | copy-start | bytes 1179652
  3.0 11.5 %collective-permute-start.10 = (bf16[96,2048]{1,0:T(8,128)(2,1)S(1)}, bf16[96,2048]{1,0:T(8,128)(2,1)S(1)}, u32[]{:S(2)}, u32[]{:S(2)}) collective-permute-start(bf16[96,2048]{1,0:T(8,128)(2,1)S(1)} %get-tuple-element.38), channel_id=1, source_target_pairs={{0,2},{2,0},{4,6},{6,4},{1,3},{3,1},{5,7},{7,5},{8,10},{10,8},{12,... | collective-permute-start | bytes 1179656 | tf_op jit(solution)/shard_map/ppermute | solution.py:367
  4.6 12.3 %collective-permute-start.12 = (bf16[96,2048]{1,0:T(8,128)(2,1)S(1)}, bf16[96,2048]{1,0:T(8,128)(2,1)S(1)}, u32[]{:S(2)}, u32[]{:S(2)}) collective-permute-start(bf16[96,2048]{1,0:T(8,128)(2,1)S(1)} %get-tuple-element.39), channel_id=1, source_target_pairs={{0,6},{2,4},{4,2},{6,0},{1,7},{3,5},{5,3},{7,1},{8,14},{10,12},{12... | collective-permute-start | bytes 1179656 | tf_op jit(solution)/shard_map/ppermute | solution.py:367
  6.8 18.5 %collective-permute-start.9 = (bf16[96,2048]{1,0:T(8,128)(2,1)}, bf16[96,2048]{1,0:T(8,128)(2,1)S(1)}, u32[]{:S(2)}, u32[]{:S(2)}) collective-permute-start(bf16[96,2048]{1,0:T(8,128)(2,1)} %get-tuple-element.37.refs_0_), channel_id=1, source_target_pairs={{0,1},{1,0},{2,3},{3,2},{4,5},{5,4},{6,7},{7,6},{8,9},{9,8},{10,11... | collective-permute-start | bytes 1179656 | tf_op jit(solution)/shard_map/ppermute | solution.py:316
  14.5 13.6 %collective-permute-start.11 = (bf16[96,2048]{1,0:T(8,128)(2,1)S(1)}, bf16[96,2048]{1,0:T(8,128)(2,1)S(1)}, u32[]{:S(2)}, u32[]{:S(2)}) collective-permute-start(bf16[96,2048]{1,0:T(8,128)(2,1)S(1)} %collective-permute-done.10.refs_2_), channel_id=1, source_target_pairs={{0,1},{1,0},{2,3},{3,2},{4,5},{5,4},{6,7},{7,6},{8,9},{9,8},{10,11... | collective-permute-start | bytes 1179656 | tf_op jit(solution)/shard_map/ppermute | solution.py:316
  17.0 11.6 %collective-permute-start.13 = (bf16[96,2048]{1,0:T(8,128)(2,1)S(1)}, bf16[96,2048]{1,0:T(8,128)(2,1)S(1)}, u32[]{:S(2)}, u32[]{:S(2)}) collective-permute-start(bf16[96,2048]{1,0:T(8,128)(2,1)S(1)} %collective-permute-done.12.refs_4_), channel_id=1, source_target_pairs={{0,1},{1,0},{2,3},{3,2},{4,5},{5,4},{6,7},{7,6},{8,9},{9,8},{10,11... | collective-permute-start | bytes 1179656 | tf_op jit(solution)/shard_map/ppermute | solution.py:316
  17.0 1.7 %collective-permute-start = (s32[2,128]{1,0:T(2,128)}, s32[2,128]{1,0:T(2,128)S(1)}, u32[]{:S(2)}, u32[]{:S(2)}) collective-permute-start(s32[2,128]{1,0:T(2,128)} %bitcast.14), channel_id=1, source_target_pairs={{0,1},{1,0},{2,3},{3,2},{4,5},{5,4},{6,7},{7,6},{8,9},{9,8},{10,11... | collective-permute-start | bytes 3080 | tf_op jit(solution)/shard_map/ppermute | solution.py:316
  20.3 15.0 %collective-permute-start.2 = (bf16[96,2048]{1,0:T(8,128)(2,1)S(1)}, bf16[96,2048]{1,0:T(8,128)(2,1)S(1)}, u32[]{:S(2)}, u32[]{:S(2)}) collective-permute-start(bf16[96,2048]{1,0:T(8,128)(2,1)S(1)} %shard_map.129), channel_id=1, source_target_pairs={{0,4},{2,6},{4,0},{6,2},{1,5},{3,7},{5,1},{7,3},{8,12},{10,14},{12... | collective-permute-start | bytes 1179656 | tf_op jit(solution)/shard_map/ppermute | solution.py:372
  23.7 8.6 %collective-permute-start.6 = (bf16[224,512]{1,0:T(8,128)(2,1)S(1)}, bf16[224,512]{1,0:T(8,128)(2,1)S(1)}, u32[]{:S(2)}, u32[]{:S(2)}) collective-permute-start(bf16[224,512]{1,0:T(8,128)(2,1)S(1)} %get-tuple-element.34), channel_id=1, source_target_pairs={{0,64},{64,0},{128,192},{192,128},{1,65},{65,1},{129,193},{193,129... | collective-permute-start | bytes 688136 | tf_op jit(solution)/shard_map/ppermute | solution.py:316
  25.3 14.1 %collective-permute-start.7 = (bf16[224,512]{1,0:T(8,128)(2,1)S(1)}, bf16[224,512]{1,0:T(8,128)(2,1)S(1)}, u32[]{:S(2)}, u32[]{:S(2)}) collective-permute-start(bf16[224,512]{1,0:T(8,128)(2,1)S(1)} %get-tuple-element.35), channel_id=1, source_target_pairs={{0,128},{64,192},{128,0},{192,64},{1,129},{65,193},{129,1},{193,65... | collective-permute-start | bytes 688136 | tf_op jit(solution)/shard_map/ppermute | solution.py:316
  28.1 18.0 %collective-permute-start.8 = (bf16[224,512]{1,0:T(8,128)(2,1)S(1)}, bf16[224,512]{1,0:T(8,128)(2,1)S(1)}, u32[]{:S(2)}, u32[]{:S(2)}) collective-permute-start(bf16[224,512]{1,0:T(8,128)(2,1)S(1)} %get-tuple-element.36), channel_id=1, source_target_pairs={{0,192},{64,128},{128,64},{192,0},{1,193},{65,129},{129,65},{193,1... | collective-permute-start | bytes 688136 | tf_op jit(solution)/shard_map/ppermute | solution.py:316
  30.5 17.9 %copy-start.3 = (bf16[224,512]{1,0:T(8,128)(2,1)S(1)}, bf16[224,512]{1,0:T(8,128)(2,1)}, u32[]{:S(2)}) copy-start(bf16[224,512]{1,0:T(8,128)(2,1)} %get-tuple-element.33.refs_4_) | copy-start | bytes 688132
  30.5 15.6 %collective-permute-start.14 = (bf16[288,224]{1,0:T(8,128)(2,1)S(1)}, bf16[288,224]{1,0:T(8,128)(2,1)S(1)}, u32[]{:S(2)}, u32[]{:S(2)}) collective-permute-start(bf16[288,224]{1,0:T(8,128)(2,1)S(1)} %get-tuple-element.40.refs_0_), channel_id=1, source_target_pairs={{0,64},{64,0},{128,192},{192,128},{1,65},{65,1},{129,193},{193,129... | collective-permute-start | bytes 387080 | tf_op jit(solution)/shard_map/ppermute | solution.py:316
  32.3 14.3 %collective-permute-start.15 = (bf16[288,224]{1,0:T(8,128)(2,1)S(1)}, bf16[288,224]{1,0:T(8,128)(2,1)S(1)}, u32[]{:S(2)}, u32[]{:S(2)}) collective-permute-start(bf16[288,224]{1,0:T(8,128)(2,1)S(1)} %get-tuple-element.40.refs_0_), channel_id=1, source_target_pairs={{0,128},{64,192},{128,0},{192,64},{1,129},{65,193},{129,1},{193,65... | collective-permute-start | bytes 387080 | tf_op jit(solution)/shard_map/ppermute | solution.py:316
  35.3 14.3 %copy-start.2 = (bf16[96,2048]{1,0:T(8,128)(2,1)}, bf16[96,2048]{1,0:T(8,128)(2,1)S(1)}, u32[]{:S(2)}) copy-start(bf16[96,2048]{1,0:T(8,128)(2,1)S(1)} %collective-permute-done.2.refs_0_.refs_1_) | copy-start | bytes 1179652
  35.3 13.0 %collective-permute-start.16 = (bf16[288,224]{1,0:T(8,128)(2,1)S(1)}, bf16[288,224]{1,0:T(8,128)(2,1)S(1)}, u32[]{:S(2)}, u32[]{:S(2)}) collective-permute-start(bf16[288,224]{1,0:T(8,128)(2,1)S(1)} %get-tuple-element.40.refs_0_), channel_id=1, source_target_pairs={{0,192},{64,128},{128,64},{192,0},{1,193},{65,129},{129,65},{193,1... | collective-permute-start | bytes 387080 | tf_op jit(solution)/shard_map/ppermute | solution.py:316
  39.5 10.2 %collective-permute-start.3 = (bf16[96,224]{1,0:T(8,128)(2,1)S(1)}, bf16[96,224]{1,0:T(8,128)(2,1)S(1)}, u32[]{:S(2)}, u32[]{:S(2)}) collective-permute-start(bf16[96,224]{1,0:T(8,128)(2,1)S(1)} %get-tuple-element.32.refs_0_), channel_id=1, source_target_pairs={{0,64},{64,0},{128,192},{192,128},{1,65},{65,1},{129,193},{193,129... | collective-permute-start | bytes 129032 | tf_op jit(solution)/shard_map/ppermute | solution.py:316
  46.1 5.7 %collective-permute-start.4 = (bf16[96,224]{1,0:T(8,128)(2,1)S(1)}, bf16[96,224]{1,0:T(8,128)(2,1)S(1)}, u32[]{:S(2)}, u32[]{:S(2)}) collective-permute-start(bf16[96,224]{1,0:T(8,128)(2,1)S(1)} %get-tuple-element.32.refs_0_), channel_id=1, source_target_pairs={{0,128},{64,192},{128,0},{192,64},{1,129},{65,193},{129,1},{193,65... | collective-permute-start | bytes 129032 | tf_op jit(solution)/shard_map/ppermute | solution.py:316
  46.1 5.8 %collective-permute-start.5 = (bf16[96,224]{1,0:T(8,128)(2,1)S(1)}, bf16[96,224]{1,0:T(8,128)(2,1)S(1)}, u32[]{:S(2)}, u32[]{:S(2)}) collective-permute-start(bf16[96,224]{1,0:T(8,128)(2,1)S(1)} %get-tuple-element.32.refs_0_), channel_id=1, source_target_pairs={{0,192},{64,128},{128,64},{192,0},{1,193},{65,129},{129,65},{193,1... | collective-permute-start | bytes 129032 | tf_op jit(solution)/shard_map/ppermute | solution.py:316
  48.4 15.2 %copy-start.11 = (bf16[128,2048]{1,0:T(8,128)(2,1)S(1)}, bf16[128,2048]{1,0:T(8,128)(2,1)}, u32[]{:S(2)}) copy-start(bf16[128,2048]{1,0:T(8,128)(2,1)} %refs_4_.1) | copy-start | bytes 1572868
  48.4 15.4 %copy-start.6 = (f32[128,2]{0,1:T(2,128)S(1)}, f32[128,2]{0,1:T(2,128)}, u32[]{:S(2)}) copy-start(f32[128,2]{0,1:T(2,128)} %param.12) | copy-start | bytes 3076
  49.6 28.1 %copy-start.5 = (s32[128,2]{0,1:T(2,128)S(1)}, s32[128,2]{0,1:T(2,128)}, u32[]{:S(2)}) copy-start(s32[128,2]{0,1:T(2,128)} %param.13) | copy-start | bytes 3076
  49.7 28.1 %copy-start.7 = (f32[128,2]{0,1:T(2,128)S(1)}, f32[128,2]{0,1:T(2,128)}, u32[]{:S(2)}) copy-start(f32[128,2]{0,1:T(2,128)} %param.12) | copy-start | bytes 3076
  53.0 24.8 %all-to-all-start = ((bf16[64,24,128]{2,1,0:T(8,128)(2,1)}), bf16[64,24,128]{2,1,0:T(8,128)(2,1)S(1)}, u32[]{:S(2)}, u32[]{:S(2)}) async-start(bf16[64,24,128]{2,1,0:T(8,128)(2,1)} %bitcast.23), calls=%async_computation | async-start | bytes 786432 | tf_op jit(solution)/shard_map/all_to_all | solution.py:321
  63.6 2.0 %collective-permute-start.21 = (bf16[128,2048]{1,0:T(8,128)(2,1)S(1)}, bf16[128,2048]{1,0:T(8,128)(2,1)S(1)}, u32[]{:S(2)}, u32[]{:S(2)}) collective-permute-start(bf16[128,2048]{1,0:T(8,128)(2,1)S(1)} %copy-done.11), channel_id=1, source_target_pairs={{0,1},{1,0},{2,3},{3,2},{4,5},{5,4},{6,7},{7,6},{8,9},{9,8},{10,11... | collective-permute-start | bytes 1572872 | tf_op jit(solution)/shard_map/ppermute | solution.py:316
  63.8 1.8 %collective-permute-start.20 = (f32[2,128]{1,0:T(2,128)S(1)}, f32[2,128]{1,0:T(2,128)S(1)}, u32[]{:S(2)}, u32[]{:S(2)}) collective-permute-start(f32[2,128]{1,0:T(2,128)S(1)} %bitcast.19), channel_id=1, source_target_pairs={{0,1},{1,0},{2,3},{3,2},{4,5},{5,4},{6,7},{7,6},{8,9},{9,8},{10,11... | collective-permute-start | bytes 3080 | tf_op jit(solution)/shard_map/ppermute | solution.py:316
  68.6 24.9 %collective-permute-start.22 = (bf16[96,2048]{1,0:T(8,128)(2,1)}, bf16[96,2048]{1,0:T(8,128)(2,1)S(1)}, u32[]{:S(2)}, u32[]{:S(2)}) collective-permute-start(bf16[96,2048]{1,0:T(8,128)(2,1)} %get-tuple-element.42), channel_id=1, source_target_pairs={{0,2},{2,0},{4,6},{6,4},{1,3},{3,1},{5,7},{7,5},{8,10},{10,8},{12,... | collective-permute-start | bytes 1179656 | tf_op jit(solution)/shard_map/ppermute | solution.py:316
  70.1 26.2 %collective-permute-start.23 = (bf16[96,2048]{1,0:T(8,128)(2,1)}, bf16[96,2048]{1,0:T(8,128)(2,1)S(1)}, u32[]{:S(2)}, u32[]{:S(2)}) collective-permute-start(bf16[96,2048]{1,0:T(8,128)(2,1)} %get-tuple-element.43), channel_id=1, source_target_pairs={{0,6},{2,4},{4,2},{6,0},{1,7},{3,5},{5,3},{7,1},{8,14},{10,12},{12... | collective-permute-start | bytes 1179656 | tf_op jit(solution)/shard_map/ppermute | solution.py:316
  72.1 24.1 %collective-permute-start.24 = (bf16[96,2048]{1,0:T(8,128)(2,1)}, bf16[96,2048]{1,0:T(8,128)(2,1)S(1)}, u32[]{:S(2)}, u32[]{:S(2)}) collective-permute-start(bf16[96,2048]{1,0:T(8,128)(2,1)} %get-tuple-element.44), channel_id=1, source_target_pairs={{0,4},{2,6},{4,0},{6,2},{1,5},{3,7},{5,1},{7,3},{8,12},{10,14},{12... | collective-permute-start | bytes 1179656 | tf_op jit(solution)/shard_map/ppermute | solution.py:316
  78.7 12.8 %all-to-all-start.1 = ((bf16[8,64,128]{2,1,0:T(8,128)(2,1)}), bf16[8,64,128]{2,1,0:T(8,128)(2,1)S(1)}, u32[]{:S(2)}, u32[]{:S(2)}) async-start(bf16[8,64,128]{2,1,0:T(8,128)(2,1)} %shard_map.136), calls=%async_computation.1 | async-start | bytes 262144 | tf_op jit(solution)/shard_map/all_to_all | solution.py:321
  91.5 14.6 %collective-permute-start.17 = (bf16[8,64,128]{2,1,0:T(8,128)(2,1)S(1)}, bf16[8,64,128]{2,1,0:T(8,128)(2,1)S(1)}, u32[]{:S(2)}, u32[]{:S(2)}) collective-permute-start(bf16[8,64,128]{2,1,0:T(8,128)(2,1)S(1)} %all-to-all-done.1.refs_0_), channel_id=1, source_target_pairs={{0,64},{64,0},{128,192},{192,128},{1,65},{65,1},{129,193},{193,129... | collective-permute-start | bytes 393224 | tf_op jit(solution)/shard_map/ppermute | solution.py:316
  91.5 14.6 %collective-permute-start.18 = (bf16[8,64,128]{2,1,0:T(8,128)(2,1)S(1)}, bf16[8,64,128]{2,1,0:T(8,128)(2,1)S(1)}, u32[]{:S(2)}, u32[]{:S(2)}) collective-permute-start(bf16[8,64,128]{2,1,0:T(8,128)(2,1)S(1)} %all-to-all-done.1.refs_0_), channel_id=1, source_target_pairs={{0,128},{64,192},{128,0},{192,64},{1,129},{65,193},{129,1},{193,65... | collective-permute-start | bytes 393224 | tf_op jit(solution)/shard_map/ppermute | solution.py:316
  93.4 2.8 %copy-start.8 = (bf16[96,2048]{1,0:T(8,128)(2,1)}, bf16[96,2048]{1,0:T(8,128)(2,1)S(1)}, u32[]{:S(2)}) copy-start(bf16[96,2048]{1,0:T(8,128)(2,1)S(1)} %collective-permute-done.22.refs_1_.refs_3_) | copy-start | bytes 1179652
  93.5 12.7 %collective-permute-start.19 = (bf16[8,64,128]{2,1,0:T(8,128)(2,1)S(1)}, bf16[8,64,128]{2,1,0:T(8,128)(2,1)S(1)}, u32[]{:S(2)}, u32[]{:S(2)}) collective-permute-start(bf16[8,64,128]{2,1,0:T(8,128)(2,1)S(1)} %all-to-all-done.1.refs_0_), channel_id=1, source_target_pairs={{0,192},{64,128},{128,64},{192,0},{1,193},{65,129},{129,65},{193,1... | collective-permute-start | bytes 393224 | tf_op jit(solution)/shard_map/ppermute | solution.py:316
  96.2 0.7 copy-start.9
  96.2 0.9 copy-start.10

commit v4 on v3

--- a/solution.py
+++ b/solution.py
@@ -242,19 +242,14 @@
 
     mixed = prob_first * pick(first, pos_first) + prob_second * pick(second, pos_second)
     mixed = mixed.astype(BF16)
-    for z in range(Z):
-        out_ref[z] = mixed
-
-
-def turn_body(*refs):
-    out_ref = refs[-1]
-    me = lax.axis_index("x")
-    for i, ref in enumerate(refs[:-1]):
-        rows = ref.shape[0] * ref.shape[1]
-        block = ref[...].reshape(rows, ref.shape[2])
-        for m in range(rows // 128):
-            start = pl.multiple_of((me ^ i) * rows + 128 * m, 128)
-            out_ref[:, pl.ds(start, 128)] = block[128 * m : 128 * m + 128].T
+    for peer in range(X * Z):
+        out_ref[peer] = mixed
+
+
+def turn_body(in_ref, out_ref):
+    for m in range(out_ref.shape[1] // 128):
+        block = in_ref[2 * m : 2 * m + 2].reshape(128, out_ref.shape[0])
+        out_ref[:, 128 * m : 128 * m + 128] = block.T
 
 
 def tangent_body(*refs):
@@ -277,34 +272,42 @@
     hidden_tang_ref[...] = (silu_tang * value + silu * tang_up).astype(BF16)
 
 
-def residual_body(down_ref, down_dir_ref, *refs):
-    by_tq_gate_ref, by_q_gate_ref, by_tq_up_ref, by_q_up_ref = refs[Y : Y + 4]
-    resid_gate_ref, resid_up_ref = refs[Y + 4 :]
-    rows = rows_of(refs[:Y])
-    back_grad = nt_dot(rows, down_ref[...])
-    back_tang = nt_dot(rows, down_dir_ref[...])
-    resid_gate = back_tang * by_tq_gate_ref[...] + back_grad * by_q_gate_ref[...]
-    resid_up = back_tang * by_tq_up_ref[...] + back_grad * by_q_up_ref[...]
-    resid_gate_ref[...] = resid_gate.astype(BF16)
-    resid_up_ref[...] = resid_up.astype(BF16)
-
-
-def outer_body(gate_units_ref, up_units_ref, down_units_ref, *refs):
-    x_refs, c_refs = refs[:2], refs[2 : 2 + Y]
-    outs, holds, sems = refs[-7:-4], refs[-4:-1], refs[-1]
-    step = x_refs[0].shape[1] // 4
+def curvature_body(*refs):
+    c_refs, held_hbms, outs = refs[:Y], refs[Y : Y + 9], refs[Y + 9 : Y + 12]
+    holds, held_refs, sems = refs[Y + 12 : Y + 15], refs[Y + 15 : Y + 24], refs[Y + 24]
+    gets = [dma(a, b, sems.at[12 + i]) for i, (a, b) in enumerate(zip(held_hbms, held_refs))]
     puts = []
-    units = [ref[...].T for ref in (gate_units_ref, up_units_ref, down_units_ref)]
-    for g in range(4):
-        cols = slice(g * step, (g + 1) * step)
-        x_rows = jnp.concatenate([ref[:, cols] for ref in x_refs], axis=0)
-        c_rows = jnp.concatenate([ref[:, cols] for ref in c_refs], axis=0)
-        for k, rows in enumerate((x_rows, x_rows, c_rows)):
-            holds[k][0, :, cols] = jnp.dot(units[k], rows, preferred_element_type=F32)
+
+    def held(*places):
+        for place in places:
+            gets[place].wait()
+        values = [held_refs[place][...] for place in places]
+        return values[0] if len(values) == 1 else values
+
+    def outer(k, units, row_refs):
+        units = units.T
+        step = row_refs[0].shape[1] // 4
+        for g in range(4):
+            cols = slice(g * step, (g + 1) * step)
+            rows = jnp.concatenate([ref[:, cols] for ref in row_refs], axis=0)
+            holds[k][0, :, cols] = jnp.dot(units, rows, preferred_element_type=F32)
             where = pl.ds(g * step, step)
             puts.append(
-                dma(holds[k].at[:, :, where], outs[k].at[:, :, where], sems.at[3 * g + k])
+                dma(holds[k].at[:, :, where], outs[k].at[:, :, where], sems.at[4 * k + g])
             )
+
+    outer(2, held(0), c_refs)
+    rows = rows_of(c_refs)
+    back_grad = nt_dot(rows, held(1))
+    back_tang = nt_dot(rows, held(2))
+    by_tq_gate, by_q_gate = held(3, 4)
+    resid_gate = back_tang * by_tq_gate + back_grad * by_q_gate
+    gets[7].wait()
+    gets[8].wait()
+    outer(0, resid_gate.astype(BF16), held_refs[7:9])
+    by_tq_up, by_q_up = held(5, 6)
+    resid_up = back_tang * by_tq_up + back_grad * by_q_up
+    outer(1, resid_up.astype(BF16), held_refs[7:9])
     for put in puts:
         put.wait()
 
@@ -437,20 +440,21 @@
         ]
     )
     share = call(
-        combine_body, [VMEM] * 3, [(VMEM, pltpu.HBM((Z, 64, tok), BF16))], mflops=100
+        combine_body, [VMEM] * 3, [(VMEM, pltpu.HBM((X * Z, 64, tok), BF16))], mflops=100
     )(routes_t, logits_t, back)
-    over_z = exchange(share, "z")
-    blocks = spread([over_z] * X, "x")
-    mixed = call(turn_body, [VMEM] * X, [(VMEM, sds((tok, width), BF16))], mflops=100)(*blocks)
-
-    resid_gate, resid_up = call(
-        residual_body, [VMEM] * (2 + Y + 4), [half_factor] * 2, mflops=704
-    )(*[in_hbm(v) for v in (down_mat, down_dir, *ordered_c, *factors)])
+    copies = exchange(share, DP_AXES)
+    mixed = call(turn_body, [VMEM], [(VMEM, sds((tok, width), BF16))], mflops=100)(copies)
+
     hold = pltpu.VMEM((1, units, width), F32)
     out = (HBM, pltpu.HBM((1, units, width), F32))
+    held = (hidden_tang, down_mat, down_dir, *factors, *x_rows)
     hvp = call(
-        outer_body, [VMEM] * (5 + Y), [out] * 3, [hold] * 3 + [dma_sems((12,))], mflops=1056
-    )(*[in_hbm(v) for v in (resid_gate, resid_up, hidden_tang, *x_rows, *ordered_c)])
+        curvature_body,
+        [VMEM] * Y + [HBM] * len(held),
+        [out] * 3,
+        [hold] * 3 + [pltpu.VMEM(v.shape, v.dtype) for v in held] + [dma_sems((12 + len(held),))],
+        mflops=1760,
+    )(*ordered_c, *[in_hbm(v) for v in held])
     return (mixed, *hvp)
 
 

time: 109 us -> 119 us (1.092); the launches traced: 107 us -> 118 us
  waiting for transfers between devices: 34.1 us -> 52.6 us
  starting transfers between devices: 41.6 us -> 38 us
  Pallas kernels: 29.6 us -> 27 us
    ppermute x22 -> x19, waiting for transfers between devices: 16.1 us -> 28.5 us  [spread(): arrived.append(lax.ppermute(pieces[i], axes, pairs))]
    all_to_all x2, waiting for transfers between devices: 7.89 us -> 13.9 us  [exchange(): return lax.all_to_all(value, axes, 0, 0, tiled=True)]
    ppermute x22 -> x19, starting transfers between devices: 20.1 us -> 15 us  [spread(): arrived.append(lax.ppermute(pieces[i], axes, pairs))]
    pallas_call x4 -> x3, Pallas kernels: 11 us -> 8.35 us  [the longest x1 6.16 us: shards(): call(curvature_body, [VMEM] * Y + [HBM] * len(held), [out] * 3, [hold] *...]
    all_to_all x2, starting transfers between devices: 15.9 us -> 17.3 us  [exchange(): return lax.all_to_all(value, axes, 0, 0, tiled=True)]
  transfers between devices with their start and end apart: 27 -> 24, of which waited for: 12 -> 13; matrix products, arithmetic and copies ran while one was open for 0% -> 0% of each run, Pallas kernels for 26% -> 21%
where the time goes in v4:
time: 119 us; the launch traced here: 118 us
  waiting for transfers between devices  52.6 us (44%)
  starting transfers between devices  38 us (32%)
  Pallas kernels  27 us (23%)
    ppermute x19, waiting for transfers between devices, spread(): arrived.append(lax.ppermute(pieces[i], axes, pairs))  28.5 us
    all_to_all x2, starting transfers between devices, exchange(): return lax.all_to_all(value, axes, 0, 0, tiled=True)  17.3 us
    ppermute x19, starting transfers between devices, spread(): arrived.append(lax.ppermute(pieces[i], axes, pairs))  15 us
    all_to_all x2, waiting for transfers between devices, exchange(): return lax.all_to_all(value, axes, 0, 0, tiled=True)  13.9 us
    ppermute x2, waiting for transfers between devices, shards(): value = lax.ppermute(value, 'y', [(d, d ^ i) for d in range(Y)])  10.1 us
    pallas_call x1, Pallas kernels, shards(): call(curvature_body, [VMEM] * Y + [HBM] * len(held), [out] * 3, [hold] *...  6.16 us
    pallas_call x1, Pallas kernels, shards(): call(tangent_body, [VMEM] * 8, [factor] * 4 + [half_factor], mflops=704)  4.57 us
    ppermute x2, starting transfers between devices, shards(): value = lax.ppermute(value, 'y', [(d, d ^ i) for d in range(Y)])  3.84 us
  transfers between devices with their start and end apart: 24, of which 13 were waited for; matrix products, arithmetic and copies ran while one was open for 0% of the time, Pallas kernels for 21%

profile of v4, /device:TPU:32, one launch (start us, length us, event | category | flops | bytes accessed | tf_op | source)
XLA Modules:
  0.0 118.4 jit_solution(18430953297565652087)
XLA Ops:
  0.7 0.1 collective-permute-start.1
  0.8 2.2 %shard_map.132 = (bf16[96,2048]{1,0:T(8,128)(2,1)}, bf16[96,2048]{1,0:T(8,128)(2,1)S(1)}, bf16[96,2048]{1,0:T(8,128)(2,1)S(1)}) custom-call(s32[2,128]{1,0:T(2,128)} %bitcast.13, bf16[128,2048]{1,0:T(8,128)(2,1)} %tok_hbm.1), custom_call_target="tpu_custom_call" | custom-call | flops 200000000 | bytes 4000000 | tf_op jit(solution)/shard_map/pallas_call | solution.py:354
  3.0 0.0 copy-start.4
  3.0 1.7 %collective-permute-start.10 = (bf16[96,2048]{1,0:T(8,128)(2,1)S(1)}, bf16[96,2048]{1,0:T(8,128)(2,1)S(1)}, u32[]{:S(2)}, u32[]{:S(2)}) collective-permute-start(bf16[96,2048]{1,0:T(8,128)(2,1)S(1)} %get-tuple-element.36), channel_id=1, source_target_pairs={{0,2},{2,0},{4,6},{6,4},{1,3},{3,1},{5,7},{7,5},{8,10},{10,8},{12,... | collective-permute-start | bytes 1179656 | tf_op jit(solution)/shard_map/ppermute | solution.py:370
  4.6 2.2 %collective-permute-start.12 = (bf16[96,2048]{1,0:T(8,128)(2,1)S(1)}, bf16[96,2048]{1,0:T(8,128)(2,1)S(1)}, u32[]{:S(2)}, u32[]{:S(2)}) collective-permute-start(bf16[96,2048]{1,0:T(8,128)(2,1)S(1)} %get-tuple-element.37), channel_id=1, source_target_pairs={{0,6},{2,4},{4,2},{6,0},{1,7},{3,5},{5,3},{7,1},{8,14},{10,12},{12... | collective-permute-start | bytes 1179656 | tf_op jit(solution)/shard_map/ppermute | solution.py:370
  6.8 0.0 collective-permute-start.9
  6.8 7.6 %collective-permute-done.10.refs_2_ = bf16[96,2048]{1,0:T(8,128)(2,1)S(1)} collective-permute-done((bf16[96,2048]{1,0:T(8,128)(2,1)S(1)}, bf16[96,2048]{1,0:T(8,128)(2,1)S(1)}, u32[]{:S(2)}, u32[]{:S(2)}) %collective-permute-start.10) | collective-permute-done | bytes 393248 | tf_op jit(solution)/shard_map/ppermute | solution.py:370
  14.5 0.0 collective-permute-start.11
  14.5 2.5 %collective-permute-done.12.refs_4_ = bf16[96,2048]{1,0:T(8,128)(2,1)S(1)} collective-permute-done((bf16[96,2048]{1,0:T(8,128)(2,1)S(1)}, bf16[96,2048]{1,0:T(8,128)(2,1)S(1)}, u32[]{:S(2)}, u32[]{:S(2)}) %collective-permute-start.12) | collective-permute-done | bytes 393248 | tf_op jit(solution)/shard_map/ppermute | solution.py:370
  17.0 0.0 collective-permute-start.13
  17.0 0.5 collective-permute-start
  17.5 1.2 %collective-permute-done.refs_1_ = s32[2,128]{1,0:T(2,128)S(1)} collective-permute-done((s32[2,128]{1,0:T(2,128)}, s32[2,128]{1,0:T(2,128)S(1)}, u32[]{:S(2)}, u32[]{:S(2)}) %collective-permute-start) | collective-permute-done | bytes 1056 | tf_op jit(solution)/shard_map/ppermute | solution.py:319
  18.7 0.0 collective-permute-done.1.refs_3_
  18.7 1.6 %shard_map.129 = bf16[96,2048]{1,0:T(8,128)(2,1)S(1)} custom-call(s32[2,128]{1,0:T(2,128)} %bitcast.15, s32[2,128]{1,0:T(2,128)S(1)} %collective-permute-done.refs_1_, bf16[128,2048]{1,0:T(8,128)(2,1)} %tok_hbm.1, bf16[128,2048]{1,0:T(8,128)(2,1)S(1)} %collective-permute-done.1.refs_3_), custom_call_target="tpu_custom_call" | custom-call | flops 100000000 | bytes 4000000 | tf_op jit(solution)/shard_map/pallas_call | solution.py:374
  20.3 1.8 %collective-permute-start.2 = (bf16[96,2048]{1,0:T(8,128)(2,1)S(1)}, bf16[96,2048]{1,0:T(8,128)(2,1)S(1)}, u32[]{:S(2)}, u32[]{:S(2)}) collective-permute-start(bf16[96,2048]{1,0:T(8,128)(2,1)S(1)} %shard_map.129), channel_id=1, source_target_pairs={{0,4},{2,6},{4,0},{6,2},{1,5},{3,7},{5,1},{7,3},{8,12},{10,14},{12... | collective-permute-start | bytes 1179656 | tf_op jit(solution)/shard_map/ppermute | solution.py:375
  22.1 1.7 %shard_map.131 = (bf16[224,512]{1,0:T(8,128)(2,1)}, bf16[224,512]{1,0:T(8,128)(2,1)S(1)}, bf16[224,512]{1,0:T(8,128)(2,1)S(1)}, bf16[224,512]{1,0:T(8,128)(2,1)S(1)}) custom-call(bf16[224,2048]{1,0:T(8,128)(2,1)} %bitcast.21), custom_call_target="tpu_custom_call" | custom-call | flops 200000000 | bytes 4000000 | tf_op jit(solution)/shard_map/pallas_call | solution.py:377
  23.7 1.6 %collective-permute-start.6 = (bf16[224,512]{1,0:T(8,128)(2,1)S(1)}, bf16[224,512]{1,0:T(8,128)(2,1)S(1)}, u32[]{:S(2)}, u32[]{:S(2)}) collective-permute-start(bf16[224,512]{1,0:T(8,128)(2,1)S(1)} %get-tuple-element.32), channel_id=1, source_target_pairs={{0,64},{64,0},{128,192},{192,128},{1,65},{65,1},{129,193},{193,129... | collective-permute-start | bytes 688136 | tf_op jit(solution)/shard_map/ppermute | solution.py:319
  25.3 0.0 collective-permute-done.9.refs_1_
  25.3 2.7 %collective-permute-start.7 = (bf16[224,512]{1,0:T(8,128)(2,1)S(1)}, bf16[224,512]{1,0:T(8,128)(2,1)S(1)}, u32[]{:S(2)}, u32[]{:S(2)}) collective-permute-start(bf16[224,512]{1,0:T(8,128)(2,1)S(1)} %get-tuple-element.33), channel_id=1, source_target_pairs={{0,128},{64,192},{128,0},{192,64},{1,129},{65,193},{129,1},{193,65... | collective-permute-start | bytes 688136 | tf_op jit(solution)/shard_map/ppermute | solution.py:319
  28.1 0.0 collective-permute-done.11.refs_3_
  28.1 0.5 collective-permute-start.8
  28.5 0.0 collective-permute-done.13.refs_5_
  28.5 0.0 copy-done.1
  28.6 1.9 %shard_map.133 = (f32[288,224]{1,0:T(8,128)}, f32[288,224]{1,0:T(8,128)}, bf16[288,224]{1,0:T(8,128)(2,1)S(1)}, bf16[288,2048]{1,0:T(8,128)(2,1)}) custom-call(bf16[96,2048]{1,0:T(8,128)(2,1)S(1)} %copy-done.4, bf16[96,2048]{1,0:T(8,128)(2,1)S(1)} %collective-permute-done.9.refs_1_, bf16[96,2048]{1,0:T(8,128)(2,1)S(1)} %collective-permute-done.10.refs_2_, ...), custom_call_target="tpu_custom_call" | custom-call | flops 576000000 | bytes 4000000 | tf_op jit(solution)/shard_map/pallas_call | solution.py:396
  30.5 0.0 copy-start.3
  30.5 0.4 collective-permute-start.14
  30.9 1.4 %collective-permute-done.6.refs_5_ = bf16[224,512]{1,0:T(8,128)(2,1)S(1)} collective-permute-done((bf16[224,512]{1,0:T(8,128)(2,1)S(1)}, bf16[224,512]{1,0:T(8,128)(2,1)S(1)}, u32[]{:S(2)}, u32[]{:S(2)}) %collective-permute-start.6) | collective-permute-done | bytes 229408 | tf_op jit(solution)/shard_map/ppermute | solution.py:319
  32.3 3.0 %collective-permute-start.15 = (bf16[288,224]{1,0:T(8,128)(2,1)S(1)}, bf16[288,224]{1,0:T(8,128)(2,1)S(1)}, u32[]{:S(2)}, u32[]{:S(2)}) collective-permute-start(bf16[288,224]{1,0:T(8,128)(2,1)S(1)} %get-tuple-element.38.refs_0_), channel_id=1, source_target_pairs={{0,128},{64,192},{128,0},{192,64},{1,129},{65,193},{129,1},{193,65... | collective-permute-start | bytes 387080 | tf_op jit(solution)/shard_map/ppermute | solution.py:319
  35.3 0.0 collective-permute-done.2.refs_0_.refs_1_.refs_12_
  35.3 1.1 collective-permute-start.16
  36.5 1.4 %shard_map.130 = (f32[96,224]{1,0:T(8,128)}, f32[96,224]{1,0:T(8,128)}, bf16[96,224]{1,0:T(8,128)(2,1)S(1)}) custom-call(bf16[96,2048]{1,0:T(8,128)(2,1)S(1)} %collective-permute-done.2.refs_0_.refs_1_.refs_12_, bf16[224,2048]{1,0:T(8,128)(2,1)S(1)} %bitcast.10, bf16[224,2048]{1,0:T(8,128)(2,1)S(1)} %bitcast.12), custom_call_target="tpu_custom_call" | custom-call | flops 192000000 | bytes 4000000 | tf_op jit(solution)/shard_map/pallas_call | solution.py:396
  37.9 1.6 %collective-permute-done.7.refs_6_ = bf16[224,512]{1,0:T(8,128)(2,1)S(1)} collective-permute-done((bf16[224,512]{1,0:T(8,128)(2,1)S(1)}, bf16[224,512]{1,0:T(8,128)(2,1)S(1)}, u32[]{:S(2)}, u32[]{:S(2)}) %collective-permute-start.7) | collective-permute-done | bytes 229408 | tf_op jit(solution)/shard_map/ppermute | solution.py:319
  39.5 0.2 collective-permute-start.3
  39.7 6.4 %collective-permute-done.8.refs_7_ = bf16[224,512]{1,0:T(8,128)(2,1)S(1)} collective-permute-done((bf16[224,512]{1,0:T(8,128)(2,1)S(1)}, bf16[224,512]{1,0:T(8,128)(2,1)S(1)}, u32[]{:S(2)}, u32[]{:S(2)}) %collective-permute-start.8) | collective-permute-done | bytes 229408 | tf_op jit(solution)/shard_map/ppermute | solution.py:319
  46.1 0.0 collective-permute-start.4
  46.1 0.0 collective-permute-done.14.refs_1_
  46.1 0.5 collective-permute-start.5
  46.6 0.0 collective-permute-done.15.refs_2_
  46.6 1.8 %collective-permute-done.16.refs_3_ = bf16[288,224]{1,0:T(8,128)(2,1)S(1)} collective-permute-done((bf16[288,224]{1,0:T(8,128)(2,1)S(1)}, bf16[288,224]{1,0:T(8,128)(2,1)S(1)}, u32[]{:S(2)}, u32[]{:S(2)}) %collective-permute-start.16) | collective-permute-done | bytes 129056 | tf_op jit(solution)/shard_map/ppermute | solution.py:319
  48.4 0.0 copy-done.3
  48.4 1.2 %shard_map.134.refs_8_ = bf16[8,8,24,128]{3,2,1,0:T(8,128)(2,1)} custom-call(bf16[288,224]{1,0:T(8,128)(2,1)S(1)} %get-tuple-element.38.refs_0_, bf16[288,224]{1,0:T(8,128)(2,1)S(1)} %collective-permute-done.14.refs_1_, bf16[288,224]{1,0:T(8,128)(2,1)S(1)} %collective-permute-done.15.refs_2_, bf16[288,224]{1,0:T(8,128)(2,1)S(1)} %collective-permute-done.16.refs_3_, ...), custom_call_target="tpu_custom_call" | custom-call | flops 264000000 | bytes 4000000 | tf_op jit(solution)/shard_map/pallas_call | solution.py:410
  49.7 0.0 collective-permute-done.3.refs_1_
  49.7 2.1 %collective-permute-done.4.refs_2_ = bf16[96,224]{1,0:T(8,128)(2,1)S(1)} collective-permute-done((bf16[96,224]{1,0:T(8,128)(2,1)S(1)}, bf16[96,224]{1,0:T(8,128)(2,1)S(1)}, u32[]{:S(2)}, u32[]{:S(2)}) %collective-permute-start.4) | collective-permute-done | bytes 43040 | tf_op jit(solution)/shard_map/ppermute | solution.py:319
  51.8 0.1 collective-permute-done.5.refs_3_
  51.9 1.0 shard_map.135
  52.9 10.6 %all-to-all-start = ((bf16[64,24,128]{2,1,0:T(8,128)(2,1)}), bf16[64,24,128]{2,1,0:T(8,128)(2,1)S(1)}, u32[]{:S(2)}, u32[]{:S(2)}) async-start(bf16[64,24,128]{2,1,0:T(8,128)(2,1)} %bitcast.23), calls=%async_computation | async-start | bytes 786432 | tf_op jit(solution)/shard_map/all_to_all | solution.py:324
  63.6 0.2 collective-permute-start.18
  63.8 13.9 %all-to-all-done.back_ref = bf16[64,24,128]{2,1,0:T(8,128)(2,1)S(1)} async-done(((bf16[64,24,128]{2,1,0:T(8,128)(2,1)}), bf16[64,24,128]{2,1,0:T(8,128)(2,1)S(1)}, u32[]{:S(2)}, u32[]{:S(2)}) %all-to-all-start) | async-done | bytes 393248 | tf_op jit(solution)/shard_map/all_to_all | solution.py:324
  77.7 1.2 %shard_map.136 = bf16[32,64,128]{2,1,0:T(8,128)(2,1)} custom-call(s32[2,128]{1,0:T(2,128)S(1)} %bitcast.17, f32[2,128]{1,0:T(2,128)S(1)} %bitcast.19, bf16[64,24,128]{2,1,0:T(8,128)(2,1)S(1)} %all-to-all-done.back_ref), custom_call_target="tpu_custom_call" | custom-call | flops 100000000 | bytes 4000000 | tf_op jit(solution)/shard_map/pallas_call | solution.py:442
  78.9 6.7 %all-to-all-start.1 = ((bf16[32,64,128]{2,1,0:T(8,128)(2,1)}), bf16[32,64,128]{2,1,0:T(8,128)(2,1)S(1)}, u32[]{:S(2)}, u32[]{:S(2)}) async-start(bf16[32,64,128]{2,1,0:T(8,128)(2,1)} %shard_map.136), calls=%async_computation.1 | async-start | bytes 1048576 | tf_op jit(solution)/shard_map/all_to_all | solution.py:324
  85.6 0.1 collective-permute-start.17
  85.7 1.1 collective-permute-done.17.refs_3_
  86.9 0.0 collective-permute-done.18.refs_5_
  86.9 3.0 %shard_map.138 = (bf16[96,2048]{1,0:T(8,128)(2,1)}, bf16[96,2048]{1,0:T(8,128)(2,1)}, bf16[96,2048]{1,0:T(8,128)(2,1)}, bf16[96,2048]{1,0:T(8,128)(2,1)}) custom-call(s32[2,128]{1,0:T(2,128)} %bitcast.16, s32[2,128]{1,0:T(2,128)S(1)} %collective-permute-done.refs_1_, f32[2,128]{1,0:T(2,128)} %bitcast.18, f32[2,128]{1,0:T(2,128)S(1)} %collective-permute-done.17.refs_3_, ...), custom_call_target="tpu_custom_call" | custom-call | flops 400000000 | bytes 4000000 | tf_op jit(solution)/shard_map/pallas_call | solution.py:388
  89.9 0.6 collective-permute-start.19
  90.5 1.0 collective-permute-start.20
  91.5 2.5 %collective-permute-start.21 = (bf16[96,2048]{1,0:T(8,128)(2,1)}, bf16[96,2048]{1,0:T(8,128)(2,1)S(1)}, u32[]{:S(2)}, u32[]{:S(2)}) collective-permute-start(bf16[96,2048]{1,0:T(8,128)(2,1)} %get-tuple-element.42), channel_id=1, source_target_pairs={{0,4},{2,6},{4,0},{6,2},{1,5},{3,7},{5,1},{7,3},{8,12},{10,14},{12... | collective-permute-start | bytes 1179656 | tf_op jit(solution)/shard_map/ppermute | solution.py:319
  94.0 4.6 %shard_map.139 = (f32[384,224]{1,0:T(8,128)}, f32[384,224]{1,0:T(8,128)}, f32[384,224]{1,0:T(8,128)}, f32[384,224]{1,0:T(8,128)}, bf16[384,224]{1,0:T(8,128)(2,1)}) custom-call(bf16[288,2048]{1,0:T(8,128)(2,1)} %get-tuple-element.43.refs_0_.refs_11_, bf16[96,2048]{1,0:T(8,128)(2,1)} %copy-done.2, f32[288,224]{1,0:T(8,128)} %get-tuple-element.44.refs_2_, ...), custom_call_target="tpu_custom_call" | custom-call | flops 704000000 | bytes 4000000 | tf_op jit(solution)/shard_map/pallas_call | solution.py:434
  98.6 3.5 %collective-permute-done.19.refs_1_ = bf16[96,2048]{1,0:T(8,128)(2,1)S(1)} collective-permute-done((bf16[96,2048]{1,0:T(8,128)(2,1)}, bf16[96,2048]{1,0:T(8,128)(2,1)S(1)}, u32[]{:S(2)}, u32[]{:S(2)}) %collective-permute-start.19) | collective-permute-done | bytes 393248 | tf_op jit(solution)/shard_map/ppermute | solution.py:319
  102.1 9.1 %collective-permute-done.20.refs_2_ = bf16[96,2048]{1,0:T(8,128)(2,1)S(1)} collective-permute-done((bf16[96,2048]{1,0:T(8,128)(2,1)}, bf16[96,2048]{1,0:T(8,128)(2,1)S(1)}, u32[]{:S(2)}, u32[]{:S(2)}) %collective-permute-start.20) | collective-permute-done | bytes 393248 | tf_op jit(solution)/shard_map/ppermute | solution.py:319
  111.2 0.0 collective-permute-done.21.refs_3_
  111.2 6.2 %shard_map.140 = (f32[1,224,2048]{2,1,0:T(8,128)}, f32[1,224,2048]{2,1,0:T(8,128)}, f32[1,224,2048]{2,1,0:T(8,128)}) custom-call(bf16[96,2048]{1,0:T(8,128)(2,1)S(1)} %copy-done.5, bf16[96,2048]{1,0:T(8,128)(2,1)S(1)} %collective-permute-done.19.refs_1_, bf16[96,2048]{1,0:T(8,128)(2,1)S(1)} %collective-permute-done.20.refs_2_, ...), custom_call_target="tpu_custom_call" | custom-call | flops 1760000000 | bytes 4000000 | tf_op jit(solution)/shard_map/pallas_call | solution.py:451
  117.4 0.0 all-to-all-done.1.in_ref
  117.4 1.0 shard_map.137
  (14 shorter events, 0.0 us)
Async XLA Ops:
  0.6 27.9 %copy-start = (bf16[1,224,2048]{2,1,0:T(8,128)(2,1)S(1)}, bf16[1,224,2048]{2,1,0:T(8,128)(2,1)}, u32[]{:S(2)}) copy-start(bf16[1,224,2048]{2,1,0:T(8,128)(2,1)} %param.14) | copy-start | bytes 2752516
  0.6 27.9 %copy-start.1 = (bf16[1,224,2048]{2,1,0:T(8,128)(2,1)S(1)}, bf16[1,224,2048]{2,1,0:T(8,128)(2,1)}, u32[]{:S(2)}) copy-start(bf16[1,224,2048]{2,1,0:T(8,128)(2,1)} %param.15) | copy-start | bytes 2752516
  0.7 18.0 %collective-permute-start.1 = (bf16[128,2048]{1,0:T(8,128)(2,1)}, bf16[128,2048]{1,0:T(8,128)(2,1)S(1)}, u32[]{:S(2)}, u32[]{:S(2)}) collective-permute-start(bf16[128,2048]{1,0:T(8,128)(2,1)} %tok_hbm.1), channel_id=1, source_target_pairs={{0,1},{1,0},{2,3},{3,2},{4,5},{5,4},{6,7},{7,6},{8,9},{9,8},{10,11... | collective-permute-start | bytes 1572872 | tf_op jit(solution)/shard_map/ppermute | solution.py:319
  3.0 25.6 %copy-start.4 = (bf16[96,2048]{1,0:T(8,128)(2,1)S(1)}, bf16[96,2048]{1,0:T(8,128)(2,1)}, u32[]{:S(2)}) copy-start(bf16[96,2048]{1,0:T(8,128)(2,1)} %get-tuple-element.35.refs_0_) | copy-start | bytes 1179652
  3.0 11.5 %collective-permute-start.10 = (bf16[96,2048]{1,0:T(8,128)(2,1)S(1)}, bf16[96,2048]{1,0:T(8,128)(2,1)S(1)}, u32[]{:S(2)}, u32[]{:S(2)}) collective-permute-start(bf16[96,2048]{1,0:T(8,128)(2,1)S(1)} %get-tuple-element.36), channel_id=1, source_target_pairs={{0,2},{2,0},{4,6},{6,4},{1,3},{3,1},{5,7},{7,5},{8,10},{10,8},{12,... | collective-permute-start | bytes 1179656 | tf_op jit(solution)/shard_map/ppermute | solution.py:370
  4.6 12.3 %collective-permute-start.12 = (bf16[96,2048]{1,0:T(8,128)(2,1)S(1)}, bf16[96,2048]{1,0:T(8,128)(2,1)S(1)}, u32[]{:S(2)}, u32[]{:S(2)}) collective-permute-start(bf16[96,2048]{1,0:T(8,128)(2,1)S(1)} %get-tuple-element.37), channel_id=1, source_target_pairs={{0,6},{2,4},{4,2},{6,0},{1,7},{3,5},{5,3},{7,1},{8,14},{10,12},{12... | collective-permute-start | bytes 1179656 | tf_op jit(solution)/shard_map/ppermute | solution.py:370
  6.8 18.5 %collective-permute-start.9 = (bf16[96,2048]{1,0:T(8,128)(2,1)}, bf16[96,2048]{1,0:T(8,128)(2,1)S(1)}, u32[]{:S(2)}, u32[]{:S(2)}) collective-permute-start(bf16[96,2048]{1,0:T(8,128)(2,1)} %get-tuple-element.35.refs_0_), channel_id=1, source_target_pairs={{0,1},{1,0},{2,3},{3,2},{4,5},{5,4},{6,7},{7,6},{8,9},{9,8},{10,11... | collective-permute-start | bytes 1179656 | tf_op jit(solution)/shard_map/ppermute | solution.py:319
  14.5 13.6 %collective-permute-start.11 = (bf16[96,2048]{1,0:T(8,128)(2,1)S(1)}, bf16[96,2048]{1,0:T(8,128)(2,1)S(1)}, u32[]{:S(2)}, u32[]{:S(2)}) collective-permute-start(bf16[96,2048]{1,0:T(8,128)(2,1)S(1)} %collective-permute-done.10.refs_2_), channel_id=1, source_target_pairs={{0,1},{1,0},{2,3},{3,2},{4,5},{5,4},{6,7},{7,6},{8,9},{9,8},{10,11... | collective-permute-start | bytes 1179656 | tf_op jit(solution)/shard_map/ppermute | solution.py:319
  17.0 11.6 %collective-permute-start.13 = (bf16[96,2048]{1,0:T(8,128)(2,1)S(1)}, bf16[96,2048]{1,0:T(8,128)(2,1)S(1)}, u32[]{:S(2)}, u32[]{:S(2)}) collective-permute-start(bf16[96,2048]{1,0:T(8,128)(2,1)S(1)} %collective-permute-done.12.refs_4_), channel_id=1, source_target_pairs={{0,1},{1,0},{2,3},{3,2},{4,5},{5,4},{6,7},{7,6},{8,9},{9,8},{10,11... | collective-permute-start | bytes 1179656 | tf_op jit(solution)/shard_map/ppermute | solution.py:319
  17.0 1.7 %collective-permute-start = (s32[2,128]{1,0:T(2,128)}, s32[2,128]{1,0:T(2,128)S(1)}, u32[]{:S(2)}, u32[]{:S(2)}) collective-permute-start(s32[2,128]{1,0:T(2,128)} %bitcast.14), channel_id=1, source_target_pairs={{0,1},{1,0},{2,3},{3,2},{4,5},{5,4},{6,7},{7,6},{8,9},{9,8},{10,11... | collective-permute-start | bytes 3080 | tf_op jit(solution)/shard_map/ppermute | solution.py:319
  20.3 15.0 %collective-permute-start.2 = (bf16[96,2048]{1,0:T(8,128)(2,1)S(1)}, bf16[96,2048]{1,0:T(8,128)(2,1)S(1)}, u32[]{:S(2)}, u32[]{:S(2)}) collective-permute-start(bf16[96,2048]{1,0:T(8,128)(2,1)S(1)} %shard_map.129), channel_id=1, source_target_pairs={{0,4},{2,6},{4,0},{6,2},{1,5},{3,7},{5,1},{7,3},{8,12},{10,14},{12... | collective-permute-start | bytes 1179656 | tf_op jit(solution)/shard_map/ppermute | solution.py:375
  23.7 8.6 %collective-permute-start.6 = (bf16[224,512]{1,0:T(8,128)(2,1)S(1)}, bf16[224,512]{1,0:T(8,128)(2,1)S(1)}, u32[]{:S(2)}, u32[]{:S(2)}) collective-permute-start(bf16[224,512]{1,0:T(8,128)(2,1)S(1)} %get-tuple-element.32), channel_id=1, source_target_pairs={{0,64},{64,0},{128,192},{192,128},{1,65},{65,1},{129,193},{193,129... | collective-permute-start | bytes 688136 | tf_op jit(solution)/shard_map/ppermute | solution.py:319
  25.3 14.1 %collective-permute-start.7 = (bf16[224,512]{1,0:T(8,128)(2,1)S(1)}, bf16[224,512]{1,0:T(8,128)(2,1)S(1)}, u32[]{:S(2)}, u32[]{:S(2)}) collective-permute-start(bf16[224,512]{1,0:T(8,128)(2,1)S(1)} %get-tuple-element.33), channel_id=1, source_target_pairs={{0,128},{64,192},{128,0},{192,64},{1,129},{65,193},{129,1},{193,65... | collective-permute-start | bytes 688136 | tf_op jit(solution)/shard_map/ppermute | solution.py:319
  28.1 18.0 %collective-permute-start.8 = (bf16[224,512]{1,0:T(8,128)(2,1)S(1)}, bf16[224,512]{1,0:T(8,128)(2,1)S(1)}, u32[]{:S(2)}, u32[]{:S(2)}) collective-permute-start(bf16[224,512]{1,0:T(8,128)(2,1)S(1)} %get-tuple-element.34), channel_id=1, source_target_pairs={{0,192},{64,128},{128,64},{192,0},{1,193},{65,129},{129,65},{193,1... | collective-permute-start | bytes 688136 | tf_op jit(solution)/shard_map/ppermute | solution.py:319
  30.5 17.9 %copy-start.3 = (bf16[224,512]{1,0:T(8,128)(2,1)S(1)}, bf16[224,512]{1,0:T(8,128)(2,1)}, u32[]{:S(2)}) copy-start(bf16[224,512]{1,0:T(8,128)(2,1)} %get-tuple-element.31.refs_4_) | copy-start | bytes 688132
  30.5 15.6 %collective-permute-start.14 = (bf16[288,224]{1,0:T(8,128)(2,1)S(1)}, bf16[288,224]{1,0:T(8,128)(2,1)S(1)}, u32[]{:S(2)}, u32[]{:S(2)}) collective-permute-start(bf16[288,224]{1,0:T(8,128)(2,1)S(1)} %get-tuple-element.38.refs_0_), channel_id=1, source_target_pairs={{0,64},{64,0},{128,192},{192,128},{1,65},{65,1},{129,193},{193,129... | collective-permute-start | bytes 387080 | tf_op jit(solution)/shard_map/ppermute | solution.py:319
  32.3 14.3 %collective-permute-start.15 = (bf16[288,224]{1,0:T(8,128)(2,1)S(1)}, bf16[288,224]{1,0:T(8,128)(2,1)S(1)}, u32[]{:S(2)}, u32[]{:S(2)}) collective-permute-start(bf16[288,224]{1,0:T(8,128)(2,1)S(1)} %get-tuple-element.38.refs_0_), channel_id=1, source_target_pairs={{0,128},{64,192},{128,0},{192,64},{1,129},{65,193},{129,1},{193,65... | collective-permute-start | bytes 387080 | tf_op jit(solution)/shard_map/ppermute | solution.py:319
  35.3 14.3 %copy-start.2 = (bf16[96,2048]{1,0:T(8,128)(2,1)}, bf16[96,2048]{1,0:T(8,128)(2,1)S(1)}, u32[]{:S(2)}) copy-start(bf16[96,2048]{1,0:T(8,128)(2,1)S(1)} %collective-permute-done.2.refs_0_.refs_1_.refs_12_) | copy-start | bytes 1179652
  35.3 13.0 %collective-permute-start.16 = (bf16[288,224]{1,0:T(8,128)(2,1)S(1)}, bf16[288,224]{1,0:T(8,128)(2,1)S(1)}, u32[]{:S(2)}, u32[]{:S(2)}) collective-permute-start(bf16[288,224]{1,0:T(8,128)(2,1)S(1)} %get-tuple-element.38.refs_0_), channel_id=1, source_target_pairs={{0,192},{64,128},{128,64},{192,0},{1,193},{65,129},{129,65},{193,1... | collective-permute-start | bytes 387080 | tf_op jit(solution)/shard_map/ppermute | solution.py:319
  39.5 10.2 %collective-permute-start.3 = (bf16[96,224]{1,0:T(8,128)(2,1)S(1)}, bf16[96,224]{1,0:T(8,128)(2,1)S(1)}, u32[]{:S(2)}, u32[]{:S(2)}) collective-permute-start(bf16[96,224]{1,0:T(8,128)(2,1)S(1)} %get-tuple-element.30.refs_0_), channel_id=1, source_target_pairs={{0,64},{64,0},{128,192},{192,128},{1,65},{65,1},{129,193},{193,129... | collective-permute-start | bytes 129032 | tf_op jit(solution)/shard_map/ppermute | solution.py:319
  46.1 5.7 %collective-permute-start.4 = (bf16[96,224]{1,0:T(8,128)(2,1)S(1)}, bf16[96,224]{1,0:T(8,128)(2,1)S(1)}, u32[]{:S(2)}, u32[]{:S(2)}) collective-permute-start(bf16[96,224]{1,0:T(8,128)(2,1)S(1)} %get-tuple-element.30.refs_0_), channel_id=1, source_target_pairs={{0,128},{64,192},{128,0},{192,64},{1,129},{65,193},{129,1},{193,65... | collective-permute-start | bytes 129032 | tf_op jit(solution)/shard_map/ppermute | solution.py:319
  46.1 5.8 %collective-permute-start.5 = (bf16[96,224]{1,0:T(8,128)(2,1)S(1)}, bf16[96,224]{1,0:T(8,128)(2,1)S(1)}, u32[]{:S(2)}, u32[]{:S(2)}) collective-permute-start(bf16[96,224]{1,0:T(8,128)(2,1)S(1)} %get-tuple-element.30.refs_0_), channel_id=1, source_target_pairs={{0,192},{64,128},{128,64},{192,0},{1,193},{65,129},{129,65},{193,1... | collective-permute-start | bytes 129032 | tf_op jit(solution)/shard_map/ppermute | solution.py:319
  48.4 15.2 %copy-start.8 = (bf16[128,2048]{1,0:T(8,128)(2,1)S(1)}, bf16[128,2048]{1,0:T(8,128)(2,1)}, u32[]{:S(2)}) copy-start(bf16[128,2048]{1,0:T(8,128)(2,1)} %refs_4_.1) | copy-start | bytes 1572868
  48.4 29.3 %copy-start.6 = (s32[128,2]{0,1:T(2,128)S(1)}, s32[128,2]{0,1:T(2,128)}, u32[]{:S(2)}) copy-start(s32[128,2]{0,1:T(2,128)} %param.13) | copy-start | bytes 3076
  48.4 29.3 %copy-start.7 = (f32[128,2]{0,1:T(2,128)S(1)}, f32[128,2]{0,1:T(2,128)}, u32[]{:S(2)}) copy-start(f32[128,2]{0,1:T(2,128)} %param.12) | copy-start | bytes 3076
  52.9 24.8 %all-to-all-start = ((bf16[64,24,128]{2,1,0:T(8,128)(2,1)}), bf16[64,24,128]{2,1,0:T(8,128)(2,1)S(1)}, u32[]{:S(2)}, u32[]{:S(2)}) async-start(bf16[64,24,128]{2,1,0:T(8,128)(2,1)} %bitcast.23), calls=%async_computation | async-start | bytes 786432 | tf_op jit(solution)/shard_map/all_to_all | solution.py:324
  63.6 23.3 %collective-permute-start.18 = (bf16[128,2048]{1,0:T(8,128)(2,1)S(1)}, bf16[128,2048]{1,0:T(8,128)(2,1)S(1)}, u32[]{:S(2)}, u32[]{:S(2)}) collective-permute-start(bf16[128,2048]{1,0:T(8,128)(2,1)S(1)} %copy-done.8), channel_id=1, source_target_pairs={{0,1},{1,0},{2,3},{3,2},{4,5},{5,4},{6,7},{7,6},{8,9},{9,8},{10,11... | collective-permute-start | bytes 1572872 | tf_op jit(solution)/shard_map/ppermute | solution.py:319
  78.9 38.5 %all-to-all-start.1 = ((bf16[32,64,128]{2,1,0:T(8,128)(2,1)}), bf16[32,64,128]{2,1,0:T(8,128)(2,1)S(1)}, u32[]{:S(2)}, u32[]{:S(2)}) async-start(bf16[32,64,128]{2,1,0:T(8,128)(2,1)} %shard_map.136), calls=%async_computation.1 | async-start | bytes 1048576 | tf_op jit(solution)/shard_map/all_to_all | solution.py:324
  85.6 1.2 %collective-permute-start.17 = (f32[2,128]{1,0:T(2,128)S(1)}, f32[2,128]{1,0:T(2,128)S(1)}, u32[]{:S(2)}, u32[]{:S(2)}) collective-permute-start(f32[2,128]{1,0:T(2,128)S(1)} %bitcast.20), channel_id=1, source_target_pairs={{0,1},{1,0},{2,3},{3,2},{4,5},{5,4},{6,7},{7,6},{8,9},{9,8},{10,11... | collective-permute-start | bytes 3080 | tf_op jit(solution)/shard_map/ppermute | solution.py:319
  89.9 12.2 %collective-permute-start.19 = (bf16[96,2048]{1,0:T(8,128)(2,1)}, bf16[96,2048]{1,0:T(8,128)(2,1)S(1)}, u32[]{:S(2)}, u32[]{:S(2)}) collective-permute-start(bf16[96,2048]{1,0:T(8,128)(2,1)} %get-tuple-element.40), channel_id=1, source_target_pairs={{0,2},{2,0},{4,6},{6,4},{1,3},{3,1},{5,7},{7,5},{8,10},{10,8},{12,... | collective-permute-start | bytes 1179656 | tf_op jit(solution)/shard_map/ppermute | solution.py:319
  90.5 20.8 %collective-permute-start.20 = (bf16[96,2048]{1,0:T(8,128)(2,1)}, bf16[96,2048]{1,0:T(8,128)(2,1)S(1)}, u32[]{:S(2)}, u32[]{:S(2)}) collective-permute-start(bf16[96,2048]{1,0:T(8,128)(2,1)} %get-tuple-element.41), channel_id=1, source_target_pairs={{0,6},{2,4},{4,2},{6,0},{1,7},{3,5},{5,3},{7,1},{8,14},{10,12},{12... | collective-permute-start | bytes 1179656 | tf_op jit(solution)/shard_map/ppermute | solution.py:319
  91.5 19.8 %collective-permute-start.21 = (bf16[96,2048]{1,0:T(8,128)(2,1)}, bf16[96,2048]{1,0:T(8,128)(2,1)S(1)}, u32[]{:S(2)}, u32[]{:S(2)}) collective-permute-start(bf16[96,2048]{1,0:T(8,128)(2,1)} %get-tuple-element.42), channel_id=1, source_target_pairs={{0,4},{2,6},{4,0},{6,2},{1,5},{3,7},{5,1},{7,3},{8,12},{10,14},{12... | collective-permute-start | bytes 1179656 | tf_op jit(solution)/shard_map/ppermute | solution.py:319
  94.0 17.2 %copy-start.5 = (bf16[96,2048]{1,0:T(8,128)(2,1)S(1)}, bf16[96,2048]{1,0:T(8,128)(2,1)}, u32[]{:S(2)}) copy-start(bf16[96,2048]{1,0:T(8,128)(2,1)} %get-tuple-element.39.refs_0_) | copy-start | bytes 1179652

commit v5 on v4

--- a/solution.py
+++ b/solution.py
@@ -78,10 +78,6 @@
     return lax.dot_general(rows, matrix, (((1,), (1,)), ((), ())), preferred_element_type=F32)
 
 
-def tn_dot(rows, matrix):
-    return lax.dot_general(rows, matrix, (((0,), (0,)), ((), ())), preferred_element_type=F32)
-
-
 def hits(routes, count, row_of):
     first, second, pos_first, pos_second = slots_of(routes)
     rows = iota((count, routes.shape[1]), 0)
@@ -138,19 +134,21 @@
         out_ref[j * CAP : (j + 1) * CAP] = picked
 
 
-def send_cot_body(*refs):
-    routes_refs, logits_refs, cot_refs = refs[0:2], refs[2:4], refs[4:6]
-    out_refs = refs[6:]
+def send_cot_body(j, routes_ref, logits_ref, cot_ref, *refs):
+    out_hbms, out_ref, sems = refs[-Y - 2 : -2], refs[-2], refs[-1]
     y, c = lax.axis_index("y"), lax.axis_index("c")
 
     def row_of(expert, pos):
         return jnp.where((expert & 1) == c, ((expert >> 1) ^ y) * CAP + pos, -1)
 
-    for j in range(2):
-        probs = gate_probs(logits_refs[j][...])
-        picked = pick_rows(routes_refs[j][...], cot_refs[j][...], Y * CAP, row_of, probs)
-        for i, out_ref in enumerate(out_refs):
-            out_ref[j * CAP : (j + 1) * CAP] = picked[i * CAP : (i + 1) * CAP]
+    probs = gate_probs(logits_ref[...])
+    out_ref[...] = pick_rows(routes_ref[...], cot_ref[...], Y * CAP, row_of, probs)
+    puts = [
+        dma(out_ref.at[pl.ds(i * CAP, CAP)], out_hbm.at[pl.ds(j * CAP, CAP)], sems.at[i])
+        for i, out_hbm in enumerate(out_hbms)
+    ]
+    for put in puts:
+        put.wait()
 
 
 def split_down_body(down_hbm, own_hbm, *refs):
@@ -224,32 +222,49 @@
         put.wait()
 
 
-def combine_body(routes_ref, logits_ref, back_ref, out_ref):
+def places_body(routes_ref, logits_ref, *out_refs):
+    hit_refs, prob_ref = out_refs[:4], out_refs[4]
     first, second, pos_first, pos_second = slots_of(routes_ref[...])
     prob_first, prob_second = gate_probs(logits_ref[...])
-    tok = routes_ref.shape[1]
+    rows = iota((EXPERTS * HALF, routes_ref.shape[1]), 0)
+    for k, (expert, pos) in enumerate(((first, pos_first), (second, pos_second))):
+        base = expert * HALF + pos
+        upper = (rows == base) & (pos < HALF)
+        lower = (rows == base - HALF) & (pos >= HALF)
+        hit_refs[2 * k][...] = jnp.where(upper, 1.0, 0.0).astype(BF16)
+        hit_refs[2 * k + 1][...] = jnp.where(lower, 1.0, 0.0).astype(BF16)
+    prob_ref[0:1] = prob_first
+    prob_ref[1:2] = prob_second
+
+
+def combine_body(back_ref, *refs):
+    hit_refs, prob_ref, out_hbm, mixed_ref, sem = refs[:4], refs[4], refs[5], refs[6], refs[7]
     total = back_ref[0:EXPERTS].astype(F32)
     for z in range(1, Z):
         total = total + back_ref[z * EXPERTS : (z + 1) * EXPERTS].astype(F32)
-    held = total.astype(BF16).reshape(EXPERTS * HALF, 128)
-    rows = iota((EXPERTS * HALF, tok), 0)
-
-    def pick(expert, pos):
-        base = expert * HALF + pos
-        in_upper = jnp.where((rows == base) & (pos < HALF), 1.0, 0.0).astype(BF16)
-        in_lower = jnp.where((rows == base - HALF) & (pos >= HALF), 1.0, 0.0).astype(BF16)
-        return tn_dot(held, in_upper)[0:64] + tn_dot(held, in_lower)[64:128]
-
-    mixed = prob_first * pick(first, pos_first) + prob_second * pick(second, pos_second)
-    mixed = mixed.astype(BF16)
+    held = total.astype(BF16).reshape(EXPERTS * HALF, 128).T
+
+    def pick(k):
+        upper = jnp.dot(held[0:64], hit_refs[2 * k][...], preferred_element_type=F32)
+        lower = jnp.dot(held[64:128], hit_refs[2 * k + 1][...], preferred_element_type=F32)
+        return upper + lower
+
+    mixed = prob_ref[0:1] * pick(0) + prob_ref[1:2] * pick(1)
     for peer in range(X * Z):
-        out_ref[peer] = mixed
-
-
-def turn_body(in_ref, out_ref):
+        mixed_ref[peer] = mixed.astype(BF16)
+    dma(mixed_ref, out_hbm, sem.at[0]).wait()
+
+
+def turn_body(in_ref, out_hbm, out_ref, sems):
+    puts = []
     for m in range(out_ref.shape[1] // 128):
         block = in_ref[2 * m : 2 * m + 2].reshape(128, out_ref.shape[0])
         out_ref[:, 128 * m : 128 * m + 128] = block.T
+        if m % 4 == 3:
+            where = pl.ds(512 * (m // 4), 512)
+            puts.append(dma(out_ref.at[:, where], out_hbm.at[:, where], sems.at[m // 4]))
+    for put in puts:
+        put.wait()
 
 
 def tangent_body(*refs):
@@ -385,9 +400,18 @@
     down_parts = spread(send_down, "x")
     logits_two = pair(logits_t)
     cot_two = pair(cotangent)
-    send_c = call(
-        send_cot_body, [VMEM] * 6, [piece] * Y, mflops=400
-    )(*routes_two, *logits_two, *cot_two)
+
+    def send_cot(j, filled):
+        return call(
+            functools.partial(send_cot_body, j),
+            [VMEM] * 3 + [HBM] * len(filled),
+            [(HBM, pltpu.HBM((2 * CAP, width), BF16))] * Y,
+            [pltpu.VMEM((Y * CAP, width), BF16), dma_sems((Y,))],
+            mflops=200,
+            input_output_aliases={3 + i: i for i in range(len(filled))},
+        )(routes_two[j], logits_two[j], cot_two[j], *[in_hbm(value) for value in filled])
+
+    send_c = send_cot(1, send_cot(0, []))
     c_pieces = spread(send_c, "y")
 
     def forward(pieces, near):
@@ -439,11 +463,28 @@
             for v in (*x_rows, pre_near, pre_far, value_near, value_far, gate_dir, up_dir)
         ]
     )
+    half_rows = EXPERTS * HALF
+    places = call(
+        places_body,
+        [VMEM] * 2,
+        [(VMEM, sds((half_rows, tok), BF16))] * 4 + [(VMEM, sds((2, tok), F32))],
+        mflops=100,
+    )(routes_t, logits_t)
     share = call(
-        combine_body, [VMEM] * 3, [(VMEM, pltpu.HBM((X * Z, 64, tok), BF16))], mflops=100
-    )(routes_t, logits_t, back)
+        combine_body,
+        [VMEM] * 6,
+        [(HBM, pltpu.HBM((X * Z, 64, tok), BF16))],
+        [pltpu.VMEM((X * Z, 64, tok), BF16), dma_sems((1,))],
+        mflops=100,
+    )(back, *places)
     copies = exchange(share, DP_AXES)
-    mixed = call(turn_body, [VMEM], [(VMEM, sds((tok, width), BF16))], mflops=100)(copies)
+    mixed = call(
+        turn_body,
+        [VMEM],
+        [(HBM, pltpu.HBM((tok, width), BF16))],
+        [pltpu.VMEM((tok, width), BF16), dma_sems((4,))],
+        mflops=100,
+    )(copies)
 
     hold = pltpu.VMEM((1, units, width), F32)
     out = (HBM, pltpu.HBM((1, units, width), F32))

time: 119 us -> 119 us (level)
    pallas_call x3 -> x5, Pallas kernels: 5.22 us -> 6.09 us  [the longest x2 3.87 us: send_cot(): call(functools.partial(send_cot_body, j), [VMEM] * 3 + [HBM] * len(filled...]
  transfers between devices with their start and end apart: 24 -> 24, of which waited for: 13 -> 12; matrix products, arithmetic and copies ran while one was open for 0% -> 0% of each run, Pallas kernels for 21% -> 22%
where the time goes in v5:
time: 119 us
  waiting for transfers between devices  51.5 us (43%)
  starting transfers between devices  38.1 us (32%)
  Pallas kernels  27.9 us (23%)
    ppermute x19, waiting for transfers between devices, spread(): arrived.append(lax.ppermute(pieces[i], axes, pairs))  27.7 us
    all_to_all x2, starting transfers between devices, exchange(): return lax.all_to_all(value, axes, 0, 0, tiled=True)  17.3 us
    ppermute x19, starting transfers between devices, spread(): arrived.append(lax.ppermute(pieces[i], axes, pairs))  15.1 us
    all_to_all x2, waiting for transfers between devices, exchange(): return lax.all_to_all(value, axes, 0, 0, tiled=True)  13.7 us
    ppermute x2, waiting for transfers between devices, shards(): value = lax.ppermute(value, 'y', [(d, d ^ i) for d in range(Y)])  10.1 us
    pallas_call x1, Pallas kernels, shards(): call(curvature_body, [VMEM] * Y + [HBM] * len(held), [out] * 3, [hold] *...  6.16 us
    pallas_call x1, Pallas kernels, shards(): call(tangent_body, [VMEM] * 8, [factor] * 4 + [half_factor], mflops=704)  4.6 us
    pallas_call x2, Pallas kernels, send_cot(): call(functools.partial(send_cot_body, j), [VMEM] * 3 + [HBM] * len(filled...  3.87 us
  transfers between devices with their start and end apart: 24, of which 12 were waited for; matrix products, arithmetic and copies ran while one was open for 0% of the time, Pallas kernels for 22%

profile of v5, /device:TPU:32, one launch (start us, length us, event | category | flops | bytes accessed | tf_op | source)
XLA Modules:
  0.0 118.6 jit_solution(9953505897629002651)
XLA Ops:
  0.7 0.1 collective-permute-start.1
  0.8 2.2 %shard_map.132 = (bf16[96,2048]{1,0:T(8,128)(2,1)}, bf16[96,2048]{1,0:T(8,128)(2,1)S(1)}, bf16[96,2048]{1,0:T(8,128)(2,1)S(1)}) custom-call(s32[2,128]{1,0:T(2,128)} %bitcast.13, bf16[128,2048]{1,0:T(8,128)(2,1)} %tok_hbm.1), custom_call_target="tpu_custom_call" | custom-call | flops 200000000 | bytes 4000000 | tf_op jit(solution)/shard_map/pallas_call | solution.py:369
  3.0 0.0 copy-start.5
  3.0 1.7 %collective-permute-start.10 = (bf16[96,2048]{1,0:T(8,128)(2,1)S(1)}, bf16[96,2048]{1,0:T(8,128)(2,1)S(1)}, u32[]{:S(2)}, u32[]{:S(2)}) collective-permute-start(bf16[96,2048]{1,0:T(8,128)(2,1)S(1)} %get-tuple-element.45), channel_id=1, source_target_pairs={{0,2},{2,0},{4,6},{6,4},{1,3},{3,1},{5,7},{7,5},{8,10},{10,8},{12,... | collective-permute-start | bytes 1179656 | tf_op jit(solution)/shard_map/ppermute | solution.py:385
  4.6 2.2 %collective-permute-start.12 = (bf16[96,2048]{1,0:T(8,128)(2,1)S(1)}, bf16[96,2048]{1,0:T(8,128)(2,1)S(1)}, u32[]{:S(2)}, u32[]{:S(2)}) collective-permute-start(bf16[96,2048]{1,0:T(8,128)(2,1)S(1)} %get-tuple-element.46), channel_id=1, source_target_pairs={{0,6},{2,4},{4,2},{6,0},{1,7},{3,5},{5,3},{7,1},{8,14},{10,12},{12... | collective-permute-start | bytes 1179656 | tf_op jit(solution)/shard_map/ppermute | solution.py:385
  6.8 0.0 collective-permute-start.9
  6.8 7.6 %collective-permute-done.10.refs_2_ = bf16[96,2048]{1,0:T(8,128)(2,1)S(1)} collective-permute-done((bf16[96,2048]{1,0:T(8,128)(2,1)S(1)}, bf16[96,2048]{1,0:T(8,128)(2,1)S(1)}, u32[]{:S(2)}, u32[]{:S(2)}) %collective-permute-start.10) | collective-permute-done | bytes 393248 | tf_op jit(solution)/shard_map/ppermute | solution.py:385
  14.5 0.0 collective-permute-start.11
  14.5 2.5 %collective-permute-done.12.refs_4_ = bf16[96,2048]{1,0:T(8,128)(2,1)S(1)} collective-permute-done((bf16[96,2048]{1,0:T(8,128)(2,1)S(1)}, bf16[96,2048]{1,0:T(8,128)(2,1)S(1)}, u32[]{:S(2)}, u32[]{:S(2)}) %collective-permute-start.12) | collective-permute-done | bytes 393248 | tf_op jit(solution)/shard_map/ppermute | solution.py:385
  17.0 0.0 collective-permute-start.13
  17.0 0.5 collective-permute-start
  17.5 1.2 %collective-permute-done.refs_1_.routes_ref = s32[2,128]{1,0:T(2,128)S(1)} collective-permute-done((s32[2,128]{1,0:T(2,128)}, s32[2,128]{1,0:T(2,128)S(1)}, u32[]{:S(2)}, u32[]{:S(2)}) %collective-permute-start) | collective-permute-done | bytes 1056 | tf_op jit(solution)/shard_map/ppermute | solution.py:334
  18.7 0.0 collective-permute-done.1.refs_3_
  18.7 1.6 %shard_map.129 = bf16[96,2048]{1,0:T(8,128)(2,1)S(1)} custom-call(s32[2,128]{1,0:T(2,128)} %bitcast.15, s32[2,128]{1,0:T(2,128)S(1)} %collective-permute-done.refs_1_.routes_ref, bf16[128,2048]{1,0:T(8,128)(2,1)} %tok_hbm.1, bf16[128,2048]{1,0:T(8,128)(2,1)S(1)} %collective-permute-done.1.refs_3_), custom_call_target="tpu_custom_call" | custom-call | flops 100000000 | bytes 4000000 | tf_op jit(solution)/shard_map/pallas_call | solution.py:389
  20.3 1.8 %collective-permute-start.2 = (bf16[96,2048]{1,0:T(8,128)(2,1)S(1)}, bf16[96,2048]{1,0:T(8,128)(2,1)S(1)}, u32[]{:S(2)}, u32[]{:S(2)}) collective-permute-start(bf16[96,2048]{1,0:T(8,128)(2,1)S(1)} %shard_map.129), channel_id=1, source_target_pairs={{0,4},{2,6},{4,0},{6,2},{1,5},{3,7},{5,1},{7,3},{8,12},{10,14},{12... | collective-permute-start | bytes 1179656 | tf_op jit(solution)/shard_map/ppermute | solution.py:390
  22.1 1.7 %shard_map.131 = (bf16[224,512]{1,0:T(8,128)(2,1)}, bf16[224,512]{1,0:T(8,128)(2,1)S(1)}, bf16[224,512]{1,0:T(8,128)(2,1)S(1)}, bf16[224,512]{1,0:T(8,128)(2,1)S(1)}) custom-call(bf16[224,2048]{1,0:T(8,128)(2,1)} %bitcast.21), custom_call_target="tpu_custom_call" | custom-call | flops 200000000 | bytes 4000000 | tf_op jit(solution)/shard_map/pallas_call | solution.py:392
  23.7 1.6 %collective-permute-start.6 = (bf16[224,512]{1,0:T(8,128)(2,1)S(1)}, bf16[224,512]{1,0:T(8,128)(2,1)S(1)}, u32[]{:S(2)}, u32[]{:S(2)}) collective-permute-start(bf16[224,512]{1,0:T(8,128)(2,1)S(1)} %get-tuple-element.41), channel_id=1, source_target_pairs={{0,64},{64,0},{128,192},{192,128},{1,65},{65,1},{129,193},{193,129... | collective-permute-start | bytes 688136 | tf_op jit(solution)/shard_map/ppermute | solution.py:334
  25.3 0.0 collective-permute-done.9.refs_1_
  25.3 2.7 %collective-permute-start.7 = (bf16[224,512]{1,0:T(8,128)(2,1)S(1)}, bf16[224,512]{1,0:T(8,128)(2,1)S(1)}, u32[]{:S(2)}, u32[]{:S(2)}) collective-permute-start(bf16[224,512]{1,0:T(8,128)(2,1)S(1)} %get-tuple-element.42), channel_id=1, source_target_pairs={{0,128},{64,192},{128,0},{192,64},{1,129},{65,193},{129,1},{193,65... | collective-permute-start | bytes 688136 | tf_op jit(solution)/shard_map/ppermute | solution.py:334
  28.1 0.0 collective-permute-done.11.refs_3_
  28.1 0.5 collective-permute-start.8
  28.5 0.0 collective-permute-done.13.refs_5_
  28.6 1.9 %shard_map.133 = (f32[288,224]{1,0:T(8,128)}, f32[288,224]{1,0:T(8,128)}, bf16[288,224]{1,0:T(8,128)(2,1)S(1)}, bf16[288,2048]{1,0:T(8,128)(2,1)}) custom-call(bf16[96,2048]{1,0:T(8,128)(2,1)S(1)} %copy-done.5, bf16[96,2048]{1,0:T(8,128)(2,1)S(1)} %collective-permute-done.9.refs_1_, bf16[96,2048]{1,0:T(8,128)(2,1)S(1)} %collective-permute-done.10.refs_2_, ...), custom_call_target="tpu_custom_call" | custom-call | flops 576000000 | bytes 4000000 | tf_op jit(solution)/shard_map/pallas_call | solution.py:420
  30.5 0.0 copy-start.4
  30.5 0.4 collective-permute-start.14
  30.9 1.4 %collective-permute-done.6.refs_5_ = bf16[224,512]{1,0:T(8,128)(2,1)S(1)} collective-permute-done((bf16[224,512]{1,0:T(8,128)(2,1)S(1)}, bf16[224,512]{1,0:T(8,128)(2,1)S(1)}, u32[]{:S(2)}, u32[]{:S(2)}) %collective-permute-start.6) | collective-permute-done | bytes 229408 | tf_op jit(solution)/shard_map/ppermute | solution.py:334
  32.3 3.0 %collective-permute-start.15 = (bf16[288,224]{1,0:T(8,128)(2,1)S(1)}, bf16[288,224]{1,0:T(8,128)(2,1)S(1)}, u32[]{:S(2)}, u32[]{:S(2)}) collective-permute-start(bf16[288,224]{1,0:T(8,128)(2,1)S(1)} %get-tuple-element.47.refs_0_), channel_id=1, source_target_pairs={{0,128},{64,192},{128,0},{192,64},{1,129},{65,193},{129,1},{193,65... | collective-permute-start | bytes 387080 | tf_op jit(solution)/shard_map/ppermute | solution.py:334
  35.3 0.0 collective-permute-done.2.refs_0_.refs_1_.refs_12_
  35.3 1.1 collective-permute-start.16
  36.5 1.4 %shard_map.130 = (f32[96,224]{1,0:T(8,128)}, f32[96,224]{1,0:T(8,128)}, bf16[96,224]{1,0:T(8,128)(2,1)S(1)}) custom-call(bf16[96,2048]{1,0:T(8,128)(2,1)S(1)} %collective-permute-done.2.refs_0_.refs_1_.refs_12_, bf16[224,2048]{1,0:T(8,128)(2,1)S(1)} %bitcast.10, bf16[224,2048]{1,0:T(8,128)(2,1)S(1)} %bitcast.12), custom_call_target="tpu_custom_call" | custom-call | flops 192000000 | bytes 4000000 | tf_op jit(solution)/shard_map/pallas_call | solution.py:420
  37.9 1.6 %collective-permute-done.7.refs_6_ = bf16[224,512]{1,0:T(8,128)(2,1)S(1)} collective-permute-done((bf16[224,512]{1,0:T(8,128)(2,1)S(1)}, bf16[224,512]{1,0:T(8,128)(2,1)S(1)}, u32[]{:S(2)}, u32[]{:S(2)}) %collective-permute-start.7) | collective-permute-done | bytes 229408 | tf_op jit(solution)/shard_map/ppermute | solution.py:334
  39.5 0.2 collective-permute-start.3
  39.7 6.4 %collective-permute-done.8.refs_7_ = bf16[224,512]{1,0:T(8,128)(2,1)S(1)} collective-permute-done((bf16[224,512]{1,0:T(8,128)(2,1)S(1)}, bf16[224,512]{1,0:T(8,128)(2,1)S(1)}, u32[]{:S(2)}, u32[]{:S(2)}) %collective-permute-start.8) | collective-permute-done | bytes 229408 | tf_op jit(solution)/shard_map/ppermute | solution.py:334
  46.1 0.0 collective-permute-start.4
  46.1 0.0 collective-permute-done.14.refs_1_
  46.1 0.5 collective-permute-start.5
  46.6 0.0 collective-permute-done.15.refs_2_
  46.6 1.8 %collective-permute-done.16.refs_3_ = bf16[288,224]{1,0:T(8,128)(2,1)S(1)} collective-permute-done((bf16[288,224]{1,0:T(8,128)(2,1)S(1)}, bf16[288,224]{1,0:T(8,128)(2,1)S(1)}, u32[]{:S(2)}, u32[]{:S(2)}) %collective-permute-start.16) | collective-permute-done | bytes 129056 | tf_op jit(solution)/shard_map/ppermute | solution.py:334
  48.4 1.2 %shard_map.134.refs_8_ = bf16[8,8,24,128]{3,2,1,0:T(8,128)(2,1)} custom-call(bf16[288,224]{1,0:T(8,128)(2,1)S(1)} %get-tuple-element.47.refs_0_, bf16[288,224]{1,0:T(8,128)(2,1)S(1)} %collective-permute-done.14.refs_1_, bf16[288,224]{1,0:T(8,128)(2,1)S(1)} %collective-permute-done.15.refs_2_, bf16[288,224]{1,0:T(8,128)(2,1)S(1)} %collective-permute-done.16.refs_3_, ...), custom_call_target="tpu_custom_call" | custom-call | flops 264000000 | bytes 4000000 | tf_op jit(solution)/shard_map/pallas_call | solution.py:434
  49.7 0.0 collective-permute-done.3.refs_1_
  49.7 2.1 %collective-permute-done.4.refs_2_ = bf16[96,224]{1,0:T(8,128)(2,1)S(1)} collective-permute-done((bf16[96,224]{1,0:T(8,128)(2,1)S(1)}, bf16[96,224]{1,0:T(8,128)(2,1)S(1)}, u32[]{:S(2)}, u32[]{:S(2)}) %collective-permute-start.4) | collective-permute-done | bytes 43040 | tf_op jit(solution)/shard_map/ppermute | solution.py:334
  51.8 0.1 collective-permute-done.5.refs_3_
  51.9 1.0 shard_map.135
  52.9 10.6 %all-to-all-start = ((bf16[64,24,128]{2,1,0:T(8,128)(2,1)}), bf16[64,24,128]{2,1,0:T(8,128)(2,1)S(1)}, u32[]{:S(2)}, u32[]{:S(2)}) async-start(bf16[64,24,128]{2,1,0:T(8,128)(2,1)} %bitcast.23), calls=%async_computation | async-start | bytes 786432 | tf_op jit(solution)/shard_map/all_to_all | solution.py:339
  63.6 0.2 collective-permute-start.18
  63.8 0.2 shard_map.136
  64.0 13.7 %all-to-all-done.back_ref = bf16[64,24,128]{2,1,0:T(8,128)(2,1)S(1)} async-done(((bf16[64,24,128]{2,1,0:T(8,128)(2,1)}), bf16[64,24,128]{2,1,0:T(8,128)(2,1)S(1)}, u32[]{:S(2)}, u32[]{:S(2)}) %all-to-all-start) | async-done | bytes 393248 | tf_op jit(solution)/shard_map/all_to_all | solution.py:339
  77.7 1.1 shard_map.137
  78.8 6.7 %all-to-all-start.1 = ((bf16[32,64,128]{2,1,0:T(8,128)(2,1)}), bf16[32,64,128]{2,1,0:T(8,128)(2,1)S(1)}, u32[]{:S(2)}, u32[]{:S(2)}) async-start(bf16[32,64,128]{2,1,0:T(8,128)(2,1)} %shard_map.137), calls=%async_computation.1 | async-start | bytes 1048576 | tf_op jit(solution)/shard_map/all_to_all | solution.py:339
  85.5 0.1 collective-permute-start.17
  85.6 2.5 %shard_map.139 = (bf16[96,2048]{1,0:T(8,128)(2,1)}, bf16[96,2048]{1,0:T(8,128)(2,1)}, bf16[96,2048]{1,0:T(8,128)(2,1)}, bf16[96,2048]{1,0:T(8,128)(2,1)}) custom-call(s32[2,128]{1,0:T(2,128)} %bitcast.16, f32[2,128]{1,0:T(2,128)} %bitcast.18, bf16[128,2048]{1,0:T(8,128)(2,1)} %cot_ref.1), custom_call_target="tpu_custom_call" | custom-call | flops 200000000 | bytes 4000000 | tf_op jit(solution)/shard_map/pallas_call | solution.py:405
  88.1 0.0 collective-permute-done.17.logits_ref
  88.1 0.0 collective-permute-done.18.cot_ref
  88.2 1.4 %shard_map.140 = (bf16[96,2048]{1,0:T(8,128)(2,1)}, bf16[96,2048]{1,0:T(8,128)(2,1)}, bf16[96,2048]{1,0:T(8,128)(2,1)}, bf16[96,2048]{1,0:T(8,128)(2,1)}) custom-call(s32[2,128]{1,0:T(2,128)S(1)} %collective-permute-done.refs_1_.routes_ref, ...), custom_call_target="tpu_custom_call", output_to_operand_aliasing={{0}: (3, {}), {1}: (4, {}), {2}: (5, {}), {3}: (6, {})} | custom-call | flops 200000000 | bytes 4000000 | tf_op jit(solution)/shard_map/pallas_call | solution.py:405
  89.6 0.7 collective-permute-start.19
  90.2 1.0 collective-permute-start.20
  91.2 2.5 %collective-permute-start.21 = (bf16[96,2048]{1,0:T(8,128)(2,1)}, bf16[96,2048]{1,0:T(8,128)(2,1)S(1)}, u32[]{:S(2)}, u32[]{:S(2)}) collective-permute-start(bf16[96,2048]{1,0:T(8,128)(2,1)} %get-tuple-element.60), channel_id=1, source_target_pairs={{0,4},{2,6},{4,0},{6,2},{1,5},{3,7},{5,1},{7,3},{8,12},{10,14},{12... | collective-permute-start | bytes 1179656 | tf_op jit(solution)/shard_map/ppermute | solution.py:334
  93.7 4.6 %shard_map.141 = (f32[384,224]{1,0:T(8,128)}, f32[384,224]{1,0:T(8,128)}, f32[384,224]{1,0:T(8,128)}, f32[384,224]{1,0:T(8,128)}, bf16[384,224]{1,0:T(8,128)(2,1)}) custom-call(bf16[288,2048]{1,0:T(8,128)(2,1)} %get-tuple-element.61.refs_0_.refs_11_, bf16[96,2048]{1,0:T(8,128)(2,1)} %copy-done.2, f32[288,224]{1,0:T(8,128)} %get-tuple-element.62.refs_2_, ...), custom_call_target="tpu_custom_call" | custom-call | flops 704000000 | bytes 4000000 | tf_op jit(solution)/shard_map/pallas_call | solution.py:458
  98.3 3.5 %collective-permute-done.19.refs_1_ = bf16[96,2048]{1,0:T(8,128)(2,1)S(1)} collective-permute-done((bf16[96,2048]{1,0:T(8,128)(2,1)}, bf16[96,2048]{1,0:T(8,128)(2,1)S(1)}, u32[]{:S(2)}, u32[]{:S(2)}) %collective-permute-start.19) | collective-permute-done | bytes 393248 | tf_op jit(solution)/shard_map/ppermute | solution.py:334
  101.8 9.5 %collective-permute-done.20.refs_2_ = bf16[96,2048]{1,0:T(8,128)(2,1)S(1)} collective-permute-done((bf16[96,2048]{1,0:T(8,128)(2,1)}, bf16[96,2048]{1,0:T(8,128)(2,1)S(1)}, u32[]{:S(2)}, u32[]{:S(2)}) %collective-permute-start.20) | collective-permute-done | bytes 393248 | tf_op jit(solution)/shard_map/ppermute | solution.py:334
  111.3 0.0 collective-permute-done.21.refs_3_
  111.3 6.2 %shard_map.142 = (f32[1,224,2048]{2,1,0:T(8,128)}, f32[1,224,2048]{2,1,0:T(8,128)}, f32[1,224,2048]{2,1,0:T(8,128)}) custom-call(bf16[96,2048]{1,0:T(8,128)(2,1)S(1)} %copy-done.3, bf16[96,2048]{1,0:T(8,128)(2,1)S(1)} %collective-permute-done.19.refs_1_, bf16[96,2048]{1,0:T(8,128)(2,1)S(1)} %collective-permute-done.20.refs_2_, ...), custom_call_target="tpu_custom_call" | custom-call | flops 1760000000 | bytes 4000000 | tf_op jit(solution)/shard_map/pallas_call | solution.py:492
  117.5 0.0 all-to-all-done.1.in_ref
  117.5 0.9 shard_map.138
  (16 shorter events, 0.0 us)
Async XLA Ops:
  0.6 27.9 %copy-start = (bf16[1,224,2048]{2,1,0:T(8,128)(2,1)S(1)}, bf16[1,224,2048]{2,1,0:T(8,128)(2,1)}, u32[]{:S(2)}) copy-start(bf16[1,224,2048]{2,1,0:T(8,128)(2,1)} %param.14) | copy-start | bytes 2752516
  0.6 27.9 %copy-start.1 = (bf16[1,224,2048]{2,1,0:T(8,128)(2,1)S(1)}, bf16[1,224,2048]{2,1,0:T(8,128)(2,1)}, u32[]{:S(2)}) copy-start(bf16[1,224,2048]{2,1,0:T(8,128)(2,1)} %param.15) | copy-start | bytes 2752516
  0.7 18.0 %collective-permute-start.1 = (bf16[128,2048]{1,0:T(8,128)(2,1)}, bf16[128,2048]{1,0:T(8,128)(2,1)S(1)}, u32[]{:S(2)}, u32[]{:S(2)}) collective-permute-start(bf16[128,2048]{1,0:T(8,128)(2,1)} %tok_hbm.1), channel_id=1, source_target_pairs={{0,1},{1,0},{2,3},{3,2},{4,5},{5,4},{6,7},{7,6},{8,9},{9,8},{10,11... | collective-permute-start | bytes 1572872 | tf_op jit(solution)/shard_map/ppermute | solution.py:334
  3.0 25.6 %copy-start.5 = (bf16[96,2048]{1,0:T(8,128)(2,1)S(1)}, bf16[96,2048]{1,0:T(8,128)(2,1)}, u32[]{:S(2)}) copy-start(bf16[96,2048]{1,0:T(8,128)(2,1)} %get-tuple-element.44.refs_0_) | copy-start | bytes 1179652
  3.0 11.5 %collective-permute-start.10 = (bf16[96,2048]{1,0:T(8,128)(2,1)S(1)}, bf16[96,2048]{1,0:T(8,128)(2,1)S(1)}, u32[]{:S(2)}, u32[]{:S(2)}) collective-permute-start(bf16[96,2048]{1,0:T(8,128)(2,1)S(1)} %get-tuple-element.45), channel_id=1, source_target_pairs={{0,2},{2,0},{4,6},{6,4},{1,3},{3,1},{5,7},{7,5},{8,10},{10,8},{12,... | collective-permute-start | bytes 1179656 | tf_op jit(solution)/shard_map/ppermute | solution.py:385
  4.6 12.3 %collective-permute-start.12 = (bf16[96,2048]{1,0:T(8,128)(2,1)S(1)}, bf16[96,2048]{1,0:T(8,128)(2,1)S(1)}, u32[]{:S(2)}, u32[]{:S(2)}) collective-permute-start(bf16[96,2048]{1,0:T(8,128)(2,1)S(1)} %get-tuple-element.46), channel_id=1, source_target_pairs={{0,6},{2,4},{4,2},{6,0},{1,7},{3,5},{5,3},{7,1},{8,14},{10,12},{12... | collective-permute-start | bytes 1179656 | tf_op jit(solution)/shard_map/ppermute | solution.py:385
  6.8 18.5 %collective-permute-start.9 = (bf16[96,2048]{1,0:T(8,128)(2,1)}, bf16[96,2048]{1,0:T(8,128)(2,1)S(1)}, u32[]{:S(2)}, u32[]{:S(2)}) collective-permute-start(bf16[96,2048]{1,0:T(8,128)(2,1)} %get-tuple-element.44.refs_0_), channel_id=1, source_target_pairs={{0,1},{1,0},{2,3},{3,2},{4,5},{5,4},{6,7},{7,6},{8,9},{9,8},{10,11... | collective-permute-start | bytes 1179656 | tf_op jit(solution)/shard_map/ppermute | solution.py:334
  14.5 13.6 %collective-permute-start.11 = (bf16[96,2048]{1,0:T(8,128)(2,1)S(1)}, bf16[96,2048]{1,0:T(8,128)(2,1)S(1)}, u32[]{:S(2)}, u32[]{:S(2)}) collective-permute-start(bf16[96,2048]{1,0:T(8,128)(2,1)S(1)} %collective-permute-done.10.refs_2_), channel_id=1, source_target_pairs={{0,1},{1,0},{2,3},{3,2},{4,5},{5,4},{6,7},{7,6},{8,9},{9,8},{10,11... | collective-permute-start | bytes 1179656 | tf_op jit(solution)/shard_map/ppermute | solution.py:334
  17.0 11.6 %collective-permute-start.13 = (bf16[96,2048]{1,0:T(8,128)(2,1)S(1)}, bf16[96,2048]{1,0:T(8,128)(2,1)S(1)}, u32[]{:S(2)}, u32[]{:S(2)}) collective-permute-start(bf16[96,2048]{1,0:T(8,128)(2,1)S(1)} %collective-permute-done.12.refs_4_), channel_id=1, source_target_pairs={{0,1},{1,0},{2,3},{3,2},{4,5},{5,4},{6,7},{7,6},{8,9},{9,8},{10,11... | collective-permute-start | bytes 1179656 | tf_op jit(solution)/shard_map/ppermute | solution.py:334
  17.0 1.7 %collective-permute-start = (s32[2,128]{1,0:T(2,128)}, s32[2,128]{1,0:T(2,128)S(1)}, u32[]{:S(2)}, u32[]{:S(2)}) collective-permute-start(s32[2,128]{1,0:T(2,128)} %bitcast.14), channel_id=1, source_target_pairs={{0,1},{1,0},{2,3},{3,2},{4,5},{5,4},{6,7},{7,6},{8,9},{9,8},{10,11... | collective-permute-start | bytes 3080 | tf_op jit(solution)/shard_map/ppermute | solution.py:334
  20.3 15.0 %collective-permute-start.2 = (bf16[96,2048]{1,0:T(8,128)(2,1)S(1)}, bf16[96,2048]{1,0:T(8,128)(2,1)S(1)}, u32[]{:S(2)}, u32[]{:S(2)}) collective-permute-start(bf16[96,2048]{1,0:T(8,128)(2,1)S(1)} %shard_map.129), channel_id=1, source_target_pairs={{0,4},{2,6},{4,0},{6,2},{1,5},{3,7},{5,1},{7,3},{8,12},{10,14},{12... | collective-permute-start | bytes 1179656 | tf_op jit(solution)/shard_map/ppermute | solution.py:390
  23.7 8.6 %collective-permute-start.6 = (bf16[224,512]{1,0:T(8,128)(2,1)S(1)}, bf16[224,512]{1,0:T(8,128)(2,1)S(1)}, u32[]{:S(2)}, u32[]{:S(2)}) collective-permute-start(bf16[224,512]{1,0:T(8,128)(2,1)S(1)} %get-tuple-element.41), channel_id=1, source_target_pairs={{0,64},{64,0},{128,192},{192,128},{1,65},{65,1},{129,193},{193,129... | collective-permute-start | bytes 688136 | tf_op jit(solution)/shard_map/ppermute | solution.py:334
  25.3 14.1 %collective-permute-start.7 = (bf16[224,512]{1,0:T(8,128)(2,1)S(1)}, bf16[224,512]{1,0:T(8,128)(2,1)S(1)}, u32[]{:S(2)}, u32[]{:S(2)}) collective-permute-start(bf16[224,512]{1,0:T(8,128)(2,1)S(1)} %get-tuple-element.42), channel_id=1, source_target_pairs={{0,128},{64,192},{128,0},{192,64},{1,129},{65,193},{129,1},{193,65... | collective-permute-start | bytes 688136 | tf_op jit(solution)/shard_map/ppermute | solution.py:334
  28.1 18.0 %collective-permute-start.8 = (bf16[224,512]{1,0:T(8,128)(2,1)S(1)}, bf16[224,512]{1,0:T(8,128)(2,1)S(1)}, u32[]{:S(2)}, u32[]{:S(2)}) collective-permute-start(bf16[224,512]{1,0:T(8,128)(2,1)S(1)} %get-tuple-element.43), channel_id=1, source_target_pairs={{0,192},{64,128},{128,64},{192,0},{1,193},{65,129},{129,65},{193,1... | collective-permute-start | bytes 688136 | tf_op jit(solution)/shard_map/ppermute | solution.py:334
  30.5 17.9 %copy-start.4 = (bf16[224,512]{1,0:T(8,128)(2,1)S(1)}, bf16[224,512]{1,0:T(8,128)(2,1)}, u32[]{:S(2)}) copy-start(bf16[224,512]{1,0:T(8,128)(2,1)} %get-tuple-element.40.refs_4_) | copy-start | bytes 688132
  30.5 15.6 %collective-permute-start.14 = (bf16[288,224]{1,0:T(8,128)(2,1)S(1)}, bf16[288,224]{1,0:T(8,128)(2,1)S(1)}, u32[]{:S(2)}, u32[]{:S(2)}) collective-permute-start(bf16[288,224]{1,0:T(8,128)(2,1)S(1)} %get-tuple-element.47.refs_0_), channel_id=1, source_target_pairs={{0,64},{64,0},{128,192},{192,128},{1,65},{65,1},{129,193},{193,129... | collective-permute-start | bytes 387080 | tf_op jit(solution)/shard_map/ppermute | solution.py:334
  32.3 14.3 %collective-permute-start.15 = (bf16[288,224]{1,0:T(8,128)(2,1)S(1)}, bf16[288,224]{1,0:T(8,128)(2,1)S(1)}, u32[]{:S(2)}, u32[]{:S(2)}) collective-permute-start(bf16[288,224]{1,0:T(8,128)(2,1)S(1)} %get-tuple-element.47.refs_0_), channel_id=1, source_target_pairs={{0,128},{64,192},{128,0},{192,64},{1,129},{65,193},{129,1},{193,65... | collective-permute-start | bytes 387080 | tf_op jit(solution)/shard_map/ppermute | solution.py:334
  35.3 14.3 %copy-start.2 = (bf16[96,2048]{1,0:T(8,128)(2,1)}, bf16[96,2048]{1,0:T(8,128)(2,1)S(1)}, u32[]{:S(2)}) copy-start(bf16[96,2048]{1,0:T(8,128)(2,1)S(1)} %collective-permute-done.2.refs_0_.refs_1_.refs_12_) | copy-start | bytes 1179652
  35.3 13.0 %collective-permute-start.16 = (bf16[288,224]{1,0:T(8,128)(2,1)S(1)}, bf16[288,224]{1,0:T(8,128)(2,1)S(1)}, u32[]{:S(2)}, u32[]{:S(2)}) collective-permute-start(bf16[288,224]{1,0:T(8,128)(2,1)S(1)} %get-tuple-element.47.refs_0_), channel_id=1, source_target_pairs={{0,192},{64,128},{128,64},{192,0},{1,193},{65,129},{129,65},{193,1... | collective-permute-start | bytes 387080 | tf_op jit(solution)/shard_map/ppermute | solution.py:334
  39.5 10.2 %collective-permute-start.3 = (bf16[96,224]{1,0:T(8,128)(2,1)S(1)}, bf16[96,224]{1,0:T(8,128)(2,1)S(1)}, u32[]{:S(2)}, u32[]{:S(2)}) collective-permute-start(bf16[96,224]{1,0:T(8,128)(2,1)S(1)} %get-tuple-element.39.refs_0_), channel_id=1, source_target_pairs={{0,64},{64,0},{128,192},{192,128},{1,65},{65,1},{129,193},{193,129... | collective-permute-start | bytes 129032 | tf_op jit(solution)/shard_map/ppermute | solution.py:334
  46.1 5.7 %collective-permute-start.4 = (bf16[96,224]{1,0:T(8,128)(2,1)S(1)}, bf16[96,224]{1,0:T(8,128)(2,1)S(1)}, u32[]{:S(2)}, u32[]{:S(2)}) collective-permute-start(bf16[96,224]{1,0:T(8,128)(2,1)S(1)} %get-tuple-element.39.refs_0_), channel_id=1, source_target_pairs={{0,128},{64,192},{128,0},{192,64},{1,129},{65,193},{129,1},{193,65... | collective-permute-start | bytes 129032 | tf_op jit(solution)/shard_map/ppermute | solution.py:334
  46.1 5.8 %collective-permute-start.5 = (bf16[96,224]{1,0:T(8,128)(2,1)S(1)}, bf16[96,224]{1,0:T(8,128)(2,1)S(1)}, u32[]{:S(2)}, u32[]{:S(2)}) collective-permute-start(bf16[96,224]{1,0:T(8,128)(2,1)S(1)} %get-tuple-element.39.refs_0_), channel_id=1, source_target_pairs={{0,192},{64,128},{128,64},{192,0},{1,193},{65,129},{129,65},{193,1... | collective-permute-start | bytes 129032 | tf_op jit(solution)/shard_map/ppermute | solution.py:334
  48.4 15.2 %copy-start.8 = (bf16[128,2048]{1,0:T(8,128)(2,1)S(1)}, bf16[128,2048]{1,0:T(8,128)(2,1)}, u32[]{:S(2)}) copy-start(bf16[128,2048]{1,0:T(8,128)(2,1)} %cot_ref.1) | copy-start | bytes 1572868
  48.4 15.4 %copy-start.6 = (s32[128,2]{0,1:T(2,128)S(1)}, s32[128,2]{0,1:T(2,128)}, u32[]{:S(2)}) copy-start(s32[128,2]{0,1:T(2,128)} %param.13) | copy-start | bytes 3076
  48.4 15.4 %copy-start.7 = (f32[128,2]{0,1:T(2,128)S(1)}, f32[128,2]{0,1:T(2,128)}, u32[]{:S(2)}) copy-start(f32[128,2]{0,1:T(2,128)} %param.12) | copy-start | bytes 3076
  52.9 24.8 %all-to-all-start = ((bf16[64,24,128]{2,1,0:T(8,128)(2,1)}), bf16[64,24,128]{2,1,0:T(8,128)(2,1)S(1)}, u32[]{:S(2)}, u32[]{:S(2)}) async-start(bf16[64,24,128]{2,1,0:T(8,128)(2,1)} %bitcast.23), calls=%async_computation | async-start | bytes 786432 | tf_op jit(solution)/shard_map/all_to_all | solution.py:339
  63.6 24.6 %collective-permute-start.18 = (bf16[128,2048]{1,0:T(8,128)(2,1)S(1)}, bf16[128,2048]{1,0:T(8,128)(2,1)S(1)}, u32[]{:S(2)}, u32[]{:S(2)}) collective-permute-start(bf16[128,2048]{1,0:T(8,128)(2,1)S(1)} %copy-done.8), channel_id=1, source_target_pairs={{0,1},{1,0},{2,3},{3,2},{4,5},{5,4},{6,7},{7,6},{8,9},{9,8},{10,11... | collective-permute-start | bytes 1572872 | tf_op jit(solution)/shard_map/ppermute | solution.py:334
  78.8 38.7 %all-to-all-start.1 = ((bf16[32,64,128]{2,1,0:T(8,128)(2,1)}), bf16[32,64,128]{2,1,0:T(8,128)(2,1)S(1)}, u32[]{:S(2)}, u32[]{:S(2)}) async-start(bf16[32,64,128]{2,1,0:T(8,128)(2,1)} %shard_map.137), calls=%async_computation.1 | async-start | bytes 1048576 | tf_op jit(solution)/shard_map/all_to_all | solution.py:339
  85.5 2.6 %collective-permute-start.17 = (f32[2,128]{1,0:T(2,128)S(1)}, f32[2,128]{1,0:T(2,128)S(1)}, u32[]{:S(2)}, u32[]{:S(2)}) collective-permute-start(f32[2,128]{1,0:T(2,128)S(1)} %bitcast.20), channel_id=1, source_target_pairs={{0,1},{1,0},{2,3},{3,2},{4,5},{5,4},{6,7},{7,6},{8,9},{9,8},{10,11... | collective-permute-start | bytes 3080 | tf_op jit(solution)/shard_map/ppermute | solution.py:334
  89.6 12.3 %collective-permute-start.19 = (bf16[96,2048]{1,0:T(8,128)(2,1)}, bf16[96,2048]{1,0:T(8,128)(2,1)S(1)}, u32[]{:S(2)}, u32[]{:S(2)}) collective-permute-start(bf16[96,2048]{1,0:T(8,128)(2,1)} %get-tuple-element.58), channel_id=1, source_target_pairs={{0,2},{2,0},{4,6},{6,4},{1,3},{3,1},{5,7},{7,5},{8,10},{10,8},{12,... | collective-permute-start | bytes 1179656 | tf_op jit(solution)/shard_map/ppermute | solution.py:334
  90.2 21.1 %collective-permute-start.20 = (bf16[96,2048]{1,0:T(8,128)(2,1)}, bf16[96,2048]{1,0:T(8,128)(2,1)S(1)}, u32[]{:S(2)}, u32[]{:S(2)}) collective-permute-start(bf16[96,2048]{1,0:T(8,128)(2,1)} %get-tuple-element.59), channel_id=1, source_target_pairs={{0,6},{2,4},{4,2},{6,0},{1,7},{3,5},{5,3},{7,1},{8,14},{10,12},{12... | collective-permute-start | bytes 1179656 | tf_op jit(solution)/shard_map/ppermute | solution.py:334
  91.2 20.1 %collective-permute-start.21 = (bf16[96,2048]{1,0:T(8,128)(2,1)}, bf16[96,2048]{1,0:T(8,128)(2,1)S(1)}, u32[]{:S(2)}, u32[]{:S(2)}) collective-permute-start(bf16[96,2048]{1,0:T(8,128)(2,1)} %get-tuple-element.60), channel_id=1, source_target_pairs={{0,4},{2,6},{4,0},{6,2},{1,5},{3,7},{5,1},{7,3},{8,12},{10,14},{12... | collective-permute-start | bytes 1179656 | tf_op jit(solution)/shard_map/ppermute | solution.py:334
  93.7 17.6 %copy-start.3 = (bf16[96,2048]{1,0:T(8,128)(2,1)S(1)}, bf16[96,2048]{1,0:T(8,128)(2,1)}, u32[]{:S(2)}) copy-start(bf16[96,2048]{1,0:T(8,128)(2,1)} %get-tuple-element.57.refs_0_) | copy-start | bytes 1179652

commit v6 on v5

--- a/solution.py
+++ b/solution.py
@@ -69,8 +69,13 @@
     return first, second, pos_first, pos_second
 
 
+def sigmoid(value):
+    small = jnp.exp(-jnp.abs(value))
+    return jnp.where(value >= 0.0, 1.0, small) / (1.0 + small)
+
+
 def gate_probs(logits):
-    first = jax.nn.sigmoid(logits[0:1, :] - logits[1:2, :])
+    first = sigmoid(logits[0:1, :] - logits[1:2, :])
     return first, 1.0 - first
 
 
@@ -190,7 +195,7 @@
     value = nt_dot(rows, up_ref[...])
     value_ref[...] = value
     puts.append(dma(value_ref, value_hbm, sems.at[1]))
-    hidden_ref[...] = (pre * jax.nn.sigmoid(pre) * value).astype(BF16)
+    hidden_ref[...] = (pre * sigmoid(pre) * value).astype(BF16)
     for put in puts:
         put.wait()
 
@@ -275,7 +280,7 @@
     tang_gate = nt_dot(rows, gate_dir_ref[...])
     tang_up = nt_dot(rows, up_dir_ref[...])
     pre, value = rows_of(pre_refs), rows_of(value_refs)
-    sig = jax.nn.sigmoid(pre)
+    sig = sigmoid(pre)
     slope_one = sig * (1.0 + pre * (1.0 - sig))
     slope_two = sig * (1.0 - sig) * (2.0 + pre * (1.0 - 2.0 * sig))
     silu = pre * sig

time: 119 us -> 119 us (level)
  no operation moved by 1% of the time
where the time goes in v6:
time: 119 us
  waiting for transfers between devices  51.4 us (43%)
  starting transfers between devices  38.1 us (32%)
  Pallas kernels  28 us (24%)
    ppermute x19, waiting for transfers between devices, spread(): arrived.append(lax.ppermute(pieces[i], axes, pairs))  27.6 us
    all_to_all x2, starting transfers between devices, exchange(): return lax.all_to_all(value, axes, 0, 0, tiled=True)  17.3 us
    ppermute x19, starting transfers between devices, spread(): arrived.append(lax.ppermute(pieces[i], axes, pairs))  15.1 us
    all_to_all x2, waiting for transfers between devices, exchange(): return lax.all_to_all(value, axes, 0, 0, tiled=True)  13.7 us
    ppermute x2, waiting for transfers between devices, shards(): value = lax.ppermute(value, 'y', [(d, d ^ i) for d in range(Y)])  10.1 us
    pallas_call x1, Pallas kernels, shards(): call(curvature_body, [VMEM] * Y + [HBM] * len(held), [out] * 3, [hold] *...  6.16 us
    pallas_call x1, Pallas kernels, shards(): call(tangent_body, [VMEM] * 8, [factor] * 4 + [half_factor], mflops=704)  4.67 us
    pallas_call x2, Pallas kernels, send_cot(): call(functools.partial(send_cot_body, j), [VMEM] * 3 + [HBM] * len(filled...  3.87 us
  transfers between devices with their start and end apart: 24, of which 12 were waited for; matrix products, arithmetic and copies ran while one was open for 0% of the time, Pallas kernels for 22%

profile of v6, /device:TPU:32, one launch (start us, length us, event | category | flops | bytes accessed | tf_op | source)
XLA Modules:
  0.0 118.6 jit_solution(26601302238600734)
XLA Ops:
  0.7 0.1 collective-permute-start.1
  0.8 2.2 %shard_map.132 = (bf16[96,2048]{1,0:T(8,128)(2,1)}, bf16[96,2048]{1,0:T(8,128)(2,1)S(1)}, bf16[96,2048]{1,0:T(8,128)(2,1)S(1)}) custom-call(s32[2,128]{1,0:T(2,128)} %bitcast.13, bf16[128,2048]{1,0:T(8,128)(2,1)} %tok_hbm.1), custom_call_target="tpu_custom_call" | custom-call | flops 200000000 | bytes 4000000 | tf_op jit(solution)/shard_map/pallas_call | solution.py:374
  3.0 0.0 copy-start.5
  3.0 1.7 %collective-permute-start.10 = (bf16[96,2048]{1,0:T(8,128)(2,1)S(1)}, bf16[96,2048]{1,0:T(8,128)(2,1)S(1)}, u32[]{:S(2)}, u32[]{:S(2)}) collective-permute-start(bf16[96,2048]{1,0:T(8,128)(2,1)S(1)} %get-tuple-element.45), channel_id=1, source_target_pairs={{0,2},{2,0},{4,6},{6,4},{1,3},{3,1},{5,7},{7,5},{8,10},{10,8},{12,... | collective-permute-start | bytes 1179656 | tf_op jit(solution)/shard_map/ppermute | solution.py:390
  4.6 2.2 %collective-permute-start.12 = (bf16[96,2048]{1,0:T(8,128)(2,1)S(1)}, bf16[96,2048]{1,0:T(8,128)(2,1)S(1)}, u32[]{:S(2)}, u32[]{:S(2)}) collective-permute-start(bf16[96,2048]{1,0:T(8,128)(2,1)S(1)} %get-tuple-element.46), channel_id=1, source_target_pairs={{0,6},{2,4},{4,2},{6,0},{1,7},{3,5},{5,3},{7,1},{8,14},{10,12},{12... | collective-permute-start | bytes 1179656 | tf_op jit(solution)/shard_map/ppermute | solution.py:390
  6.8 0.0 collective-permute-start.9
  6.8 7.6 %collective-permute-done.10.refs_2_ = bf16[96,2048]{1,0:T(8,128)(2,1)S(1)} collective-permute-done((bf16[96,2048]{1,0:T(8,128)(2,1)S(1)}, bf16[96,2048]{1,0:T(8,128)(2,1)S(1)}, u32[]{:S(2)}, u32[]{:S(2)}) %collective-permute-start.10) | collective-permute-done | bytes 393248 | tf_op jit(solution)/shard_map/ppermute | solution.py:390
  14.5 0.0 collective-permute-start.11
  14.5 2.5 %collective-permute-done.12.refs_4_ = bf16[96,2048]{1,0:T(8,128)(2,1)S(1)} collective-permute-done((bf16[96,2048]{1,0:T(8,128)(2,1)S(1)}, bf16[96,2048]{1,0:T(8,128)(2,1)S(1)}, u32[]{:S(2)}, u32[]{:S(2)}) %collective-permute-start.12) | collective-permute-done | bytes 393248 | tf_op jit(solution)/shard_map/ppermute | solution.py:390
  17.0 0.0 collective-permute-start.13
  17.0 0.5 collective-permute-start
  17.5 1.2 %collective-permute-done.refs_1_.routes_ref = s32[2,128]{1,0:T(2,128)S(1)} collective-permute-done((s32[2,128]{1,0:T(2,128)}, s32[2,128]{1,0:T(2,128)S(1)}, u32[]{:S(2)}, u32[]{:S(2)}) %collective-permute-start) | collective-permute-done | bytes 1056 | tf_op jit(solution)/shard_map/ppermute | solution.py:339
  18.7 0.0 collective-permute-done.1.refs_3_
  18.7 1.6 %shard_map.129 = bf16[96,2048]{1,0:T(8,128)(2,1)S(1)} custom-call(s32[2,128]{1,0:T(2,128)} %bitcast.15, s32[2,128]{1,0:T(2,128)S(1)} %collective-permute-done.refs_1_.routes_ref, bf16[128,2048]{1,0:T(8,128)(2,1)} %tok_hbm.1, bf16[128,2048]{1,0:T(8,128)(2,1)S(1)} %collective-permute-done.1.refs_3_), custom_call_target="tpu_custom_call" | custom-call | flops 100000000 | bytes 4000000 | tf_op jit(solution)/shard_map/pallas_call | solution.py:394
  20.3 1.8 %collective-permute-start.2 = (bf16[96,2048]{1,0:T(8,128)(2,1)S(1)}, bf16[96,2048]{1,0:T(8,128)(2,1)S(1)}, u32[]{:S(2)}, u32[]{:S(2)}) collective-permute-start(bf16[96,2048]{1,0:T(8,128)(2,1)S(1)} %shard_map.129), channel_id=1, source_target_pairs={{0,4},{2,6},{4,0},{6,2},{1,5},{3,7},{5,1},{7,3},{8,12},{10,14},{12... | collective-permute-start | bytes 1179656 | tf_op jit(solution)/shard_map/ppermute | solution.py:395
  22.1 1.7 %shard_map.131 = (bf16[224,512]{1,0:T(8,128)(2,1)}, bf16[224,512]{1,0:T(8,128)(2,1)S(1)}, bf16[224,512]{1,0:T(8,128)(2,1)S(1)}, bf16[224,512]{1,0:T(8,128)(2,1)S(1)}) custom-call(bf16[224,2048]{1,0:T(8,128)(2,1)} %bitcast.21), custom_call_target="tpu_custom_call" | custom-call | flops 200000000 | bytes 4000000 | tf_op jit(solution)/shard_map/pallas_call | solution.py:397
  23.7 1.6 %collective-permute-start.6 = (bf16[224,512]{1,0:T(8,128)(2,1)S(1)}, bf16[224,512]{1,0:T(8,128)(2,1)S(1)}, u32[]{:S(2)}, u32[]{:S(2)}) collective-permute-start(bf16[224,512]{1,0:T(8,128)(2,1)S(1)} %get-tuple-element.41), channel_id=1, source_target_pairs={{0,64},{64,0},{128,192},{192,128},{1,65},{65,1},{129,193},{193,129... | collective-permute-start | bytes 688136 | tf_op jit(solution)/shard_map/ppermute | solution.py:339
  25.3 0.0 collective-permute-done.9.refs_1_
  25.3 2.7 %collective-permute-start.7 = (bf16[224,512]{1,0:T(8,128)(2,1)S(1)}, bf16[224,512]{1,0:T(8,128)(2,1)S(1)}, u32[]{:S(2)}, u32[]{:S(2)}) collective-permute-start(bf16[224,512]{1,0:T(8,128)(2,1)S(1)} %get-tuple-element.42), channel_id=1, source_target_pairs={{0,128},{64,192},{128,0},{192,64},{1,129},{65,193},{129,1},{193,65... | collective-permute-start | bytes 688136 | tf_op jit(solution)/shard_map/ppermute | solution.py:339
  28.1 0.0 collective-permute-done.11.refs_3_
  28.1 0.5 collective-permute-start.8
  28.5 0.0 collective-permute-done.13.refs_5_
  28.6 1.9 %shard_map.133 = (f32[288,224]{1,0:T(8,128)}, f32[288,224]{1,0:T(8,128)}, bf16[288,224]{1,0:T(8,128)(2,1)S(1)}, bf16[288,2048]{1,0:T(8,128)(2,1)}) custom-call(bf16[96,2048]{1,0:T(8,128)(2,1)S(1)} %copy-done.5, bf16[96,2048]{1,0:T(8,128)(2,1)S(1)} %collective-permute-done.9.refs_1_, bf16[96,2048]{1,0:T(8,128)(2,1)S(1)} %collective-permute-done.10.refs_2_, ...), custom_call_target="tpu_custom_call" | custom-call | flops 576000000 | bytes 4000000 | tf_op jit(solution)/shard_map/pallas_call | solution.py:425
  30.5 0.0 copy-start.4
  30.5 0.4 collective-permute-start.14
  30.9 1.4 %collective-permute-done.6.refs_5_ = bf16[224,512]{1,0:T(8,128)(2,1)S(1)} collective-permute-done((bf16[224,512]{1,0:T(8,128)(2,1)S(1)}, bf16[224,512]{1,0:T(8,128)(2,1)S(1)}, u32[]{:S(2)}, u32[]{:S(2)}) %collective-permute-start.6) | collective-permute-done | bytes 229408 | tf_op jit(solution)/shard_map/ppermute | solution.py:339
  32.3 3.0 %collective-permute-start.15 = (bf16[288,224]{1,0:T(8,128)(2,1)S(1)}, bf16[288,224]{1,0:T(8,128)(2,1)S(1)}, u32[]{:S(2)}, u32[]{:S(2)}) collective-permute-start(bf16[288,224]{1,0:T(8,128)(2,1)S(1)} %get-tuple-element.47.refs_0_), channel_id=1, source_target_pairs={{0,128},{64,192},{128,0},{192,64},{1,129},{65,193},{129,1},{193,65... | collective-permute-start | bytes 387080 | tf_op jit(solution)/shard_map/ppermute | solution.py:339
  35.3 0.0 collective-permute-done.2.refs_0_.refs_1_.refs_12_
  35.3 1.1 collective-permute-start.16
  36.5 1.4 %shard_map.130 = (f32[96,224]{1,0:T(8,128)}, f32[96,224]{1,0:T(8,128)}, bf16[96,224]{1,0:T(8,128)(2,1)S(1)}) custom-call(bf16[96,2048]{1,0:T(8,128)(2,1)S(1)} %collective-permute-done.2.refs_0_.refs_1_.refs_12_, bf16[224,2048]{1,0:T(8,128)(2,1)S(1)} %bitcast.10, bf16[224,2048]{1,0:T(8,128)(2,1)S(1)} %bitcast.12), custom_call_target="tpu_custom_call" | custom-call | flops 192000000 | bytes 4000000 | tf_op jit(solution)/shard_map/pallas_call | solution.py:425
  37.9 1.6 %collective-permute-done.7.refs_6_ = bf16[224,512]{1,0:T(8,128)(2,1)S(1)} collective-permute-done((bf16[224,512]{1,0:T(8,128)(2,1)S(1)}, bf16[224,512]{1,0:T(8,128)(2,1)S(1)}, u32[]{:S(2)}, u32[]{:S(2)}) %collective-permute-start.7) | collective-permute-done | bytes 229408 | tf_op jit(solution)/shard_map/ppermute | solution.py:339
  39.5 0.2 collective-permute-start.3
  39.7 6.4 %collective-permute-done.8.refs_7_ = bf16[224,512]{1,0:T(8,128)(2,1)S(1)} collective-permute-done((bf16[224,512]{1,0:T(8,128)(2,1)S(1)}, bf16[224,512]{1,0:T(8,128)(2,1)S(1)}, u32[]{:S(2)}, u32[]{:S(2)}) %collective-permute-start.8) | collective-permute-done | bytes 229408 | tf_op jit(solution)/shard_map/ppermute | solution.py:339
  46.1 0.0 collective-permute-start.4
  46.1 0.0 collective-permute-done.14.refs_1_
  46.1 0.5 collective-permute-start.5
  46.6 0.0 collective-permute-done.15.refs_2_
  46.6 1.8 %collective-permute-done.16.refs_3_ = bf16[288,224]{1,0:T(8,128)(2,1)S(1)} collective-permute-done((bf16[288,224]{1,0:T(8,128)(2,1)S(1)}, bf16[288,224]{1,0:T(8,128)(2,1)S(1)}, u32[]{:S(2)}, u32[]{:S(2)}) %collective-permute-start.16) | collective-permute-done | bytes 129056 | tf_op jit(solution)/shard_map/ppermute | solution.py:339
  48.4 1.2 %shard_map.134.refs_8_ = bf16[8,8,24,128]{3,2,1,0:T(8,128)(2,1)} custom-call(bf16[288,224]{1,0:T(8,128)(2,1)S(1)} %get-tuple-element.47.refs_0_, bf16[288,224]{1,0:T(8,128)(2,1)S(1)} %collective-permute-done.14.refs_1_, bf16[288,224]{1,0:T(8,128)(2,1)S(1)} %collective-permute-done.15.refs_2_, bf16[288,224]{1,0:T(8,128)(2,1)S(1)} %collective-permute-done.16.refs_3_, ...), custom_call_target="tpu_custom_call" | custom-call | flops 264000000 | bytes 4000000 | tf_op jit(solution)/shard_map/pallas_call | solution.py:439
  49.7 0.0 collective-permute-done.3.refs_1_
  49.7 2.1 %collective-permute-done.4.refs_2_ = bf16[96,224]{1,0:T(8,128)(2,1)S(1)} collective-permute-done((bf16[96,224]{1,0:T(8,128)(2,1)S(1)}, bf16[96,224]{1,0:T(8,128)(2,1)S(1)}, u32[]{:S(2)}, u32[]{:S(2)}) %collective-permute-start.4) | collective-permute-done | bytes 43040 | tf_op jit(solution)/shard_map/ppermute | solution.py:339
  51.8 0.1 collective-permute-done.5.refs_3_
  51.9 1.0 shard_map.135
  52.9 10.6 %all-to-all-start = ((bf16[64,24,128]{2,1,0:T(8,128)(2,1)}), bf16[64,24,128]{2,1,0:T(8,128)(2,1)S(1)}, u32[]{:S(2)}, u32[]{:S(2)}) async-start(bf16[64,24,128]{2,1,0:T(8,128)(2,1)} %bitcast.23), calls=%async_computation | async-start | bytes 786432 | tf_op jit(solution)/shard_map/all_to_all | solution.py:344
  63.6 0.2 collective-permute-start.18
  63.8 0.2 shard_map.136
  64.0 13.7 %all-to-all-done.back_ref = bf16[64,24,128]{2,1,0:T(8,128)(2,1)S(1)} async-done(((bf16[64,24,128]{2,1,0:T(8,128)(2,1)}), bf16[64,24,128]{2,1,0:T(8,128)(2,1)S(1)}, u32[]{:S(2)}, u32[]{:S(2)}) %all-to-all-start) | async-done | bytes 393248 | tf_op jit(solution)/shard_map/all_to_all | solution.py:344
  77.7 1.1 shard_map.137
  78.8 6.7 %all-to-all-start.1 = ((bf16[32,64,128]{2,1,0:T(8,128)(2,1)}), bf16[32,64,128]{2,1,0:T(8,128)(2,1)S(1)}, u32[]{:S(2)}, u32[]{:S(2)}) async-start(bf16[32,64,128]{2,1,0:T(8,128)(2,1)} %shard_map.137), calls=%async_computation.1 | async-start | bytes 1048576 | tf_op jit(solution)/shard_map/all_to_all | solution.py:344
  85.5 0.1 collective-permute-start.17
  85.6 2.5 %shard_map.139 = (bf16[96,2048]{1,0:T(8,128)(2,1)}, bf16[96,2048]{1,0:T(8,128)(2,1)}, bf16[96,2048]{1,0:T(8,128)(2,1)}, bf16[96,2048]{1,0:T(8,128)(2,1)}) custom-call(s32[2,128]{1,0:T(2,128)} %bitcast.16, f32[2,128]{1,0:T(2,128)} %bitcast.18, bf16[128,2048]{1,0:T(8,128)(2,1)} %cot_ref.1), custom_call_target="tpu_custom_call" | custom-call | flops 200000000 | bytes 4000000 | tf_op jit(solution)/shard_map/pallas_call | solution.py:410
  88.1 0.0 collective-permute-done.17.logits_ref
  88.1 0.0 collective-permute-done.18.cot_ref
  88.2 1.4 %shard_map.140 = (bf16[96,2048]{1,0:T(8,128)(2,1)}, bf16[96,2048]{1,0:T(8,128)(2,1)}, bf16[96,2048]{1,0:T(8,128)(2,1)}, bf16[96,2048]{1,0:T(8,128)(2,1)}) custom-call(s32[2,128]{1,0:T(2,128)S(1)} %collective-permute-done.refs_1_.routes_ref, ...), custom_call_target="tpu_custom_call", output_to_operand_aliasing={{0}: (3, {}), {1}: (4, {}), {2}: (5, {}), {3}: (6, {})} | custom-call | flops 200000000 | bytes 4000000 | tf_op jit(solution)/shard_map/pallas_call | solution.py:410
  89.6 0.7 collective-permute-start.19
  90.2 1.0 collective-permute-start.20
  91.2 2.5 %collective-permute-start.21 = (bf16[96,2048]{1,0:T(8,128)(2,1)}, bf16[96,2048]{1,0:T(8,128)(2,1)S(1)}, u32[]{:S(2)}, u32[]{:S(2)}) collective-permute-start(bf16[96,2048]{1,0:T(8,128)(2,1)} %get-tuple-element.60), channel_id=1, source_target_pairs={{0,4},{2,6},{4,0},{6,2},{1,5},{3,7},{5,1},{7,3},{8,12},{10,14},{12... | collective-permute-start | bytes 1179656 | tf_op jit(solution)/shard_map/ppermute | solution.py:339
  93.7 4.7 %shard_map.141 = (f32[384,224]{1,0:T(8,128)}, f32[384,224]{1,0:T(8,128)}, f32[384,224]{1,0:T(8,128)}, f32[384,224]{1,0:T(8,128)}, bf16[384,224]{1,0:T(8,128)(2,1)}) custom-call(bf16[288,2048]{1,0:T(8,128)(2,1)} %get-tuple-element.61.refs_0_.refs_11_, bf16[96,2048]{1,0:T(8,128)(2,1)} %copy-done.2, f32[288,224]{1,0:T(8,128)} %get-tuple-element.62.refs_2_, ...), custom_call_target="tpu_custom_call" | custom-call | flops 704000000 | bytes 4000000 | tf_op jit(solution)/shard_map/pallas_call | solution.py:463
  98.4 3.4 %collective-permute-done.19.refs_1_ = bf16[96,2048]{1,0:T(8,128)(2,1)S(1)} collective-permute-done((bf16[96,2048]{1,0:T(8,128)(2,1)}, bf16[96,2048]{1,0:T(8,128)(2,1)S(1)}, u32[]{:S(2)}, u32[]{:S(2)}) %collective-permute-start.19) | collective-permute-done | bytes 393248 | tf_op jit(solution)/shard_map/ppermute | solution.py:339
  101.8 9.5 %collective-permute-done.20.refs_2_ = bf16[96,2048]{1,0:T(8,128)(2,1)S(1)} collective-permute-done((bf16[96,2048]{1,0:T(8,128)(2,1)}, bf16[96,2048]{1,0:T(8,128)(2,1)S(1)}, u32[]{:S(2)}, u32[]{:S(2)}) %collective-permute-start.20) | collective-permute-done | bytes 393248 | tf_op jit(solution)/shard_map/ppermute | solution.py:339
  111.3 0.0 collective-permute-done.21.refs_3_
  111.3 6.2 %shard_map.142 = (f32[1,224,2048]{2,1,0:T(8,128)}, f32[1,224,2048]{2,1,0:T(8,128)}, f32[1,224,2048]{2,1,0:T(8,128)}) custom-call(bf16[96,2048]{1,0:T(8,128)(2,1)S(1)} %copy-done.3, bf16[96,2048]{1,0:T(8,128)(2,1)S(1)} %collective-permute-done.19.refs_1_, bf16[96,2048]{1,0:T(8,128)(2,1)S(1)} %collective-permute-done.20.refs_2_, ...), custom_call_target="tpu_custom_call" | custom-call | flops 1760000000 | bytes 4000000 | tf_op jit(solution)/shard_map/pallas_call | solution.py:497
  117.5 0.0 all-to-all-done.1.in_ref
  117.5 0.9 shard_map.138
  (16 shorter events, 0.0 us)
Async XLA Ops:
  0.6 27.9 %copy-start = (bf16[1,224,2048]{2,1,0:T(8,128)(2,1)S(1)}, bf16[1,224,2048]{2,1,0:T(8,128)(2,1)}, u32[]{:S(2)}) copy-start(bf16[1,224,2048]{2,1,0:T(8,128)(2,1)} %param.14) | copy-start | bytes 2752516
  0.6 27.9 %copy-start.1 = (bf16[1,224,2048]{2,1,0:T(8,128)(2,1)S(1)}, bf16[1,224,2048]{2,1,0:T(8,128)(2,1)}, u32[]{:S(2)}) copy-start(bf16[1,224,2048]{2,1,0:T(8,128)(2,1)} %param.15) | copy-start | bytes 2752516
  0.7 18.0 %collective-permute-start.1 = (bf16[128,2048]{1,0:T(8,128)(2,1)}, bf16[128,2048]{1,0:T(8,128)(2,1)S(1)}, u32[]{:S(2)}, u32[]{:S(2)}) collective-permute-start(bf16[128,2048]{1,0:T(8,128)(2,1)} %tok_hbm.1), channel_id=1, source_target_pairs={{0,1},{1,0},{2,3},{3,2},{4,5},{5,4},{6,7},{7,6},{8,9},{9,8},{10,11... | collective-permute-start | bytes 1572872 | tf_op jit(solution)/shard_map/ppermute | solution.py:339
  3.0 25.6 %copy-start.5 = (bf16[96,2048]{1,0:T(8,128)(2,1)S(1)}, bf16[96,2048]{1,0:T(8,128)(2,1)}, u32[]{:S(2)}) copy-start(bf16[96,2048]{1,0:T(8,128)(2,1)} %get-tuple-element.44.refs_0_) | copy-start | bytes 1179652
  3.0 11.5 %collective-permute-start.10 = (bf16[96,2048]{1,0:T(8,128)(2,1)S(1)}, bf16[96,2048]{1,0:T(8,128)(2,1)S(1)}, u32[]{:S(2)}, u32[]{:S(2)}) collective-permute-start(bf16[96,2048]{1,0:T(8,128)(2,1)S(1)} %get-tuple-element.45), channel_id=1, source_target_pairs={{0,2},{2,0},{4,6},{6,4},{1,3},{3,1},{5,7},{7,5},{8,10},{10,8},{12,... | collective-permute-start | bytes 1179656 | tf_op jit(solution)/shard_map/ppermute | solution.py:390
  4.6 12.3 %collective-permute-start.12 = (bf16[96,2048]{1,0:T(8,128)(2,1)S(1)}, bf16[96,2048]{1,0:T(8,128)(2,1)S(1)}, u32[]{:S(2)}, u32[]{:S(2)}) collective-permute-start(bf16[96,2048]{1,0:T(8,128)(2,1)S(1)} %get-tuple-element.46), channel_id=1, source_target_pairs={{0,6},{2,4},{4,2},{6,0},{1,7},{3,5},{5,3},{7,1},{8,14},{10,12},{12... | collective-permute-start | bytes 1179656 | tf_op jit(solution)/shard_map/ppermute | solution.py:390
  6.8 18.5 %collective-permute-start.9 = (bf16[96,2048]{1,0:T(8,128)(2,1)}, bf16[96,2048]{1,0:T(8,128)(2,1)S(1)}, u32[]{:S(2)}, u32[]{:S(2)}) collective-permute-start(bf16[96,2048]{1,0:T(8,128)(2,1)} %get-tuple-element.44.refs_0_), channel_id=1, source_target_pairs={{0,1},{1,0},{2,3},{3,2},{4,5},{5,4},{6,7},{7,6},{8,9},{9,8},{10,11... | collective-permute-start | bytes 1179656 | tf_op jit(solution)/shard_map/ppermute | solution.py:339
  14.5 13.6 %collective-permute-start.11 = (bf16[96,2048]{1,0:T(8,128)(2,1)S(1)}, bf16[96,2048]{1,0:T(8,128)(2,1)S(1)}, u32[]{:S(2)}, u32[]{:S(2)}) collective-permute-start(bf16[96,2048]{1,0:T(8,128)(2,1)S(1)} %collective-permute-done.10.refs_2_), channel_id=1, source_target_pairs={{0,1},{1,0},{2,3},{3,2},{4,5},{5,4},{6,7},{7,6},{8,9},{9,8},{10,11... | collective-permute-start | bytes 1179656 | tf_op jit(solution)/shard_map/ppermute | solution.py:339
  17.0 11.6 %collective-permute-start.13 = (bf16[96,2048]{1,0:T(8,128)(2,1)S(1)}, bf16[96,2048]{1,0:T(8,128)(2,1)S(1)}, u32[]{:S(2)}, u32[]{:S(2)}) collective-permute-start(bf16[96,2048]{1,0:T(8,128)(2,1)S(1)} %collective-permute-done.12.refs_4_), channel_id=1, source_target_pairs={{0,1},{1,0},{2,3},{3,2},{4,5},{5,4},{6,7},{7,6},{8,9},{9,8},{10,11... | collective-permute-start | bytes 1179656 | tf_op jit(solution)/shard_map/ppermute | solution.py:339
  17.0 1.7 %collective-permute-start = (s32[2,128]{1,0:T(2,128)}, s32[2,128]{1,0:T(2,128)S(1)}, u32[]{:S(2)}, u32[]{:S(2)}) collective-permute-start(s32[2,128]{1,0:T(2,128)} %bitcast.14), channel_id=1, source_target_pairs={{0,1},{1,0},{2,3},{3,2},{4,5},{5,4},{6,7},{7,6},{8,9},{9,8},{10,11... | collective-permute-start | bytes 3080 | tf_op jit(solution)/shard_map/ppermute | solution.py:339
  20.3 15.0 %collective-permute-start.2 = (bf16[96,2048]{1,0:T(8,128)(2,1)S(1)}, bf16[96,2048]{1,0:T(8,128)(2,1)S(1)}, u32[]{:S(2)}, u32[]{:S(2)}) collective-permute-start(bf16[96,2048]{1,0:T(8,128)(2,1)S(1)} %shard_map.129), channel_id=1, source_target_pairs={{0,4},{2,6},{4,0},{6,2},{1,5},{3,7},{5,1},{7,3},{8,12},{10,14},{12... | collective-permute-start | bytes 1179656 | tf_op jit(solution)/shard_map/ppermute | solution.py:395
  23.7 8.6 %collective-permute-start.6 = (bf16[224,512]{1,0:T(8,128)(2,1)S(1)}, bf16[224,512]{1,0:T(8,128)(2,1)S(1)}, u32[]{:S(2)}, u32[]{:S(2)}) collective-permute-start(bf16[224,512]{1,0:T(8,128)(2,1)S(1)} %get-tuple-element.41), channel_id=1, source_target_pairs={{0,64},{64,0},{128,192},{192,128},{1,65},{65,1},{129,193},{193,129... | collective-permute-start | bytes 688136 | tf_op jit(solution)/shard_map/ppermute | solution.py:339
  25.3 14.1 %collective-permute-start.7 = (bf16[224,512]{1,0:T(8,128)(2,1)S(1)}, bf16[224,512]{1,0:T(8,128)(2,1)S(1)}, u32[]{:S(2)}, u32[]{:S(2)}) collective-permute-start(bf16[224,512]{1,0:T(8,128)(2,1)S(1)} %get-tuple-element.42), channel_id=1, source_target_pairs={{0,128},{64,192},{128,0},{192,64},{1,129},{65,193},{129,1},{193,65... | collective-permute-start | bytes 688136 | tf_op jit(solution)/shard_map/ppermute | solution.py:339
  28.1 18.0 %collective-permute-start.8 = (bf16[224,512]{1,0:T(8,128)(2,1)S(1)}, bf16[224,512]{1,0:T(8,128)(2,1)S(1)}, u32[]{:S(2)}, u32[]{:S(2)}) collective-permute-start(bf16[224,512]{1,0:T(8,128)(2,1)S(1)} %get-tuple-element.43), channel_id=1, source_target_pairs={{0,192},{64,128},{128,64},{192,0},{1,193},{65,129},{129,65},{193,1... | collective-permute-start | bytes 688136 | tf_op jit(solution)/shard_map/ppermute | solution.py:339
  30.5 17.9 %copy-start.4 = (bf16[224,512]{1,0:T(8,128)(2,1)S(1)}, bf16[224,512]{1,0:T(8,128)(2,1)}, u32[]{:S(2)}) copy-start(bf16[224,512]{1,0:T(8,128)(2,1)} %get-tuple-element.40.refs_4_) | copy-start | bytes 688132
  30.5 15.6 %collective-permute-start.14 = (bf16[288,224]{1,0:T(8,128)(2,1)S(1)}, bf16[288,224]{1,0:T(8,128)(2,1)S(1)}, u32[]{:S(2)}, u32[]{:S(2)}) collective-permute-start(bf16[288,224]{1,0:T(8,128)(2,1)S(1)} %get-tuple-element.47.refs_0_), channel_id=1, source_target_pairs={{0,64},{64,0},{128,192},{192,128},{1,65},{65,1},{129,193},{193,129... | collective-permute-start | bytes 387080 | tf_op jit(solution)/shard_map/ppermute | solution.py:339
  32.3 14.3 %collective-permute-start.15 = (bf16[288,224]{1,0:T(8,128)(2,1)S(1)}, bf16[288,224]{1,0:T(8,128)(2,1)S(1)}, u32[]{:S(2)}, u32[]{:S(2)}) collective-permute-start(bf16[288,224]{1,0:T(8,128)(2,1)S(1)} %get-tuple-element.47.refs_0_), channel_id=1, source_target_pairs={{0,128},{64,192},{128,0},{192,64},{1,129},{65,193},{129,1},{193,65... | collective-permute-start | bytes 387080 | tf_op jit(solution)/shard_map/ppermute | solution.py:339
  35.3 14.3 %copy-start.2 = (bf16[96,2048]{1,0:T(8,128)(2,1)}, bf16[96,2048]{1,0:T(8,128)(2,1)S(1)}, u32[]{:S(2)}) copy-start(bf16[96,2048]{1,0:T(8,128)(2,1)S(1)} %collective-permute-done.2.refs_0_.refs_1_.refs_12_) | copy-start | bytes 1179652
  35.3 13.0 %collective-permute-start.16 = (bf16[288,224]{1,0:T(8,128)(2,1)S(1)}, bf16[288,224]{1,0:T(8,128)(2,1)S(1)}, u32[]{:S(2)}, u32[]{:S(2)}) collective-permute-start(bf16[288,224]{1,0:T(8,128)(2,1)S(1)} %get-tuple-element.47.refs_0_), channel_id=1, source_target_pairs={{0,192},{64,128},{128,64},{192,0},{1,193},{65,129},{129,65},{193,1... | collective-permute-start | bytes 387080 | tf_op jit(solution)/shard_map/ppermute | solution.py:339
  39.5 10.2 %collective-permute-start.3 = (bf16[96,224]{1,0:T(8,128)(2,1)S(1)}, bf16[96,224]{1,0:T(8,128)(2,1)S(1)}, u32[]{:S(2)}, u32[]{:S(2)}) collective-permute-start(bf16[96,224]{1,0:T(8,128)(2,1)S(1)} %get-tuple-element.39.refs_0_), channel_id=1, source_target_pairs={{0,64},{64,0},{128,192},{192,128},{1,65},{65,1},{129,193},{193,129... | collective-permute-start | bytes 129032 | tf_op jit(solution)/shard_map/ppermute | solution.py:339
  46.1 5.7 %collective-permute-start.4 = (bf16[96,224]{1,0:T(8,128)(2,1)S(1)}, bf16[96,224]{1,0:T(8,128)(2,1)S(1)}, u32[]{:S(2)}, u32[]{:S(2)}) collective-permute-start(bf16[96,224]{1,0:T(8,128)(2,1)S(1)} %get-tuple-element.39.refs_0_), channel_id=1, source_target_pairs={{0,128},{64,192},{128,0},{192,64},{1,129},{65,193},{129,1},{193,65... | collective-permute-start | bytes 129032 | tf_op jit(solution)/shard_map/ppermute | solution.py:339
  46.1 5.8 %collective-permute-start.5 = (bf16[96,224]{1,0:T(8,128)(2,1)S(1)}, bf16[96,224]{1,0:T(8,128)(2,1)S(1)}, u32[]{:S(2)}, u32[]{:S(2)}) collective-permute-start(bf16[96,224]{1,0:T(8,128)(2,1)S(1)} %get-tuple-element.39.refs_0_), channel_id=1, source_target_pairs={{0,192},{64,128},{128,64},{192,0},{1,193},{65,129},{129,65},{193,1... | collective-permute-start | bytes 129032 | tf_op jit(solution)/shard_map/ppermute | solution.py:339
  48.4 15.2 %copy-start.8 = (bf16[128,2048]{1,0:T(8,128)(2,1)S(1)}, bf16[128,2048]{1,0:T(8,128)(2,1)}, u32[]{:S(2)}) copy-start(bf16[128,2048]{1,0:T(8,128)(2,1)} %cot_ref.1) | copy-start | bytes 1572868
  48.4 15.4 %copy-start.6 = (s32[128,2]{0,1:T(2,128)S(1)}, s32[128,2]{0,1:T(2,128)}, u32[]{:S(2)}) copy-start(s32[128,2]{0,1:T(2,128)} %param.13) | copy-start | bytes 3076
  48.4 15.4 %copy-start.7 = (f32[128,2]{0,1:T(2,128)S(1)}, f32[128,2]{0,1:T(2,128)}, u32[]{:S(2)}) copy-start(f32[128,2]{0,1:T(2,128)} %param.12) | copy-start | bytes 3076
  52.9 24.8 %all-to-all-start = ((bf16[64,24,128]{2,1,0:T(8,128)(2,1)}), bf16[64,24,128]{2,1,0:T(8,128)(2,1)S(1)}, u32[]{:S(2)}, u32[]{:S(2)}) async-start(bf16[64,24,128]{2,1,0:T(8,128)(2,1)} %bitcast.23), calls=%async_computation | async-start | bytes 786432 | tf_op jit(solution)/shard_map/all_to_all | solution.py:344
  63.6 24.6 %collective-permute-start.18 = (bf16[128,2048]{1,0:T(8,128)(2,1)S(1)}, bf16[128,2048]{1,0:T(8,128)(2,1)S(1)}, u32[]{:S(2)}, u32[]{:S(2)}) collective-permute-start(bf16[128,2048]{1,0:T(8,128)(2,1)S(1)} %copy-done.8), channel_id=1, source_target_pairs={{0,1},{1,0},{2,3},{3,2},{4,5},{5,4},{6,7},{7,6},{8,9},{9,8},{10,11... | collective-permute-start | bytes 1572872 | tf_op jit(solution)/shard_map/ppermute | solution.py:339
  78.8 38.7 %all-to-all-start.1 = ((bf16[32,64,128]{2,1,0:T(8,128)(2,1)}), bf16[32,64,128]{2,1,0:T(8,128)(2,1)S(1)}, u32[]{:S(2)}, u32[]{:S(2)}) async-start(bf16[32,64,128]{2,1,0:T(8,128)(2,1)} %shard_map.137), calls=%async_computation.1 | async-start | bytes 1048576 | tf_op jit(solution)/shard_map/all_to_all | solution.py:344
  85.5 2.6 %collective-permute-start.17 = (f32[2,128]{1,0:T(2,128)S(1)}, f32[2,128]{1,0:T(2,128)S(1)}, u32[]{:S(2)}, u32[]{:S(2)}) collective-permute-start(f32[2,128]{1,0:T(2,128)S(1)} %bitcast.20), channel_id=1, source_target_pairs={{0,1},{1,0},{2,3},{3,2},{4,5},{5,4},{6,7},{7,6},{8,9},{9,8},{10,11... | collective-permute-start | bytes 3080 | tf_op jit(solution)/shard_map/ppermute | solution.py:339
  89.6 12.3 %collective-permute-start.19 = (bf16[96,2048]{1,0:T(8,128)(2,1)}, bf16[96,2048]{1,0:T(8,128)(2,1)S(1)}, u32[]{:S(2)}, u32[]{:S(2)}) collective-permute-start(bf16[96,2048]{1,0:T(8,128)(2,1)} %get-tuple-element.58), channel_id=1, source_target_pairs={{0,2},{2,0},{4,6},{6,4},{1,3},{3,1},{5,7},{7,5},{8,10},{10,8},{12,... | collective-permute-start | bytes 1179656 | tf_op jit(solution)/shard_map/ppermute | solution.py:339
  90.2 21.1 %collective-permute-start.20 = (bf16[96,2048]{1,0:T(8,128)(2,1)}, bf16[96,2048]{1,0:T(8,128)(2,1)S(1)}, u32[]{:S(2)}, u32[]{:S(2)}) collective-permute-start(bf16[96,2048]{1,0:T(8,128)(2,1)} %get-tuple-element.59), channel_id=1, source_target_pairs={{0,6},{2,4},{4,2},{6,0},{1,7},{3,5},{5,3},{7,1},{8,14},{10,12},{12... | collective-permute-start | bytes 1179656 | tf_op jit(solution)/shard_map/ppermute | solution.py:339
  91.2 20.1 %collective-permute-start.21 = (bf16[96,2048]{1,0:T(8,128)(2,1)}, bf16[96,2048]{1,0:T(8,128)(2,1)S(1)}, u32[]{:S(2)}, u32[]{:S(2)}) collective-permute-start(bf16[96,2048]{1,0:T(8,128)(2,1)} %get-tuple-element.60), channel_id=1, source_target_pairs={{0,4},{2,6},{4,0},{6,2},{1,5},{3,7},{5,1},{7,3},{8,12},{10,14},{12... | collective-permute-start | bytes 1179656 | tf_op jit(solution)/shard_map/ppermute | solution.py:339
  93.7 17.6 %copy-start.3 = (bf16[96,2048]{1,0:T(8,128)(2,1)S(1)}, bf16[96,2048]{1,0:T(8,128)(2,1)}, u32[]{:S(2)}) copy-start(bf16[96,2048]{1,0:T(8,128)(2,1)} %get-tuple-element.57.refs_0_) | copy-start | bytes 1179652
